TPU v7x, 32 devices: a whole 2x2x4 slice. The times are simulated.
32 devices in a mesh: row: 8 (over z, y), col: 4 (over x, core).
Axes of the slice: x: 2, y: 2, z: 4, core: 2. Of those that a mesh axis runs over, the one named last changes fastest.
Arguments:
- coarse_kernel: bfloat16 [1024, 1024], P('row', 'col'), may hold values from -0.04453125 to 0.04453125, as said below
- correlations: bfloat16 [128, 128, 128], P(('row', 'col')), may hold values from -0.5 to 0.5
- neighbor: int32 [128], P(('row', 'col')), may hold values from 0 to 7
- pair_weight: float32 [128, 128], P('row'), may hold values from 0.13 to 7.4, as said below
- energies: float32 [16384], P(('row', 'col')), may hold values from 0.5 to 2
- start_block: float32 [16384, 64], P(('row', 'col')), may hold values from -120 to 120
Outputs:
- residual: float32 [16384, 64], P(('row', 'col'))
- coefficients: float32 [3, 64, 64], replicated
Inputs may be any that keep to these rules, and one draw needn't show every extreme that they name: coarse_kernel equals its transpose. pair_weight equals its transpose.
All inputs are finite; a program needn't handle non-finite values.
Results may differ from a plain program's by a relative error of at most 0.0085.
Values may be sent and summed in bfloat16 or wider, within the bound.
No kernel may reach another device: no remote copies, remote signals or barrier semaphores. Data moves between devices by JAX's collectives and lax.ppermute only.
A program may use at most 64 MiB of HBM per device.

v0:
```python
import functools

import jax
import jax.numpy as jnp
from jax import lax
from jax.experimental import pallas as pl
from jax.experimental.pallas import tpu as pltpu
from jax.sharding import PartitionSpec as P


highest = lax.Precision.HIGHEST
AXES = ("row", "col")
SHIFT = 1.25
HALVES = False
FLOPS_PER_US = 5e8


def build_tile(row_correlation, row_neighbor, column_correlation, column_neighbor, coarse, weights):
    band_size = row_correlation.shape[1]
    coarse_count = coarse.shape[0] // band_size
    blocks = coarse.reshape(coarse_count, band_size, coarse_count, band_size)[
        :, :, column_neighbor, :
    ]
    mapped = jnp.einsum(
        "cakb,kbe->cake", blocks, column_correlation, preferred_element_type=jnp.float32
    ).astype(jnp.bfloat16)
    chosen = mapped[row_neighbor]
    product = jnp.einsum(
        "kai,kaje->kije", row_correlation, chosen, preferred_element_type=jnp.float32
    )
    scaled = (product * weights[:, None, :, None]).astype(jnp.bfloat16)
    return scaled.reshape(
        row_correlation.shape[0] * band_size, column_correlation.shape[0] * band_size
    )


def apply_down(kernel_tile, vectors):
    partial_value = jnp.dot(
        kernel_tile,
        lax.all_gather(vectors, "row", axis=0, tiled=True),
        preferred_element_type=jnp.float32,
    )
    return lax.psum_scatter(partial_value, "col", scatter_dimension=0, tiled=True)


def general_form(coarse_kernel, correlations, neighbor, pair_weight, energies, start_block):
    row_correlation, row_neighbor = (
        lax.all_gather(correlations, "col", axis=0, tiled=True),
        lax.all_gather(neighbor, "col", axis=0, tiled=True),
    )
    column_correlation, column_neighbor = (
        lax.all_gather(correlations, "row", axis=0, tiled=True),
        lax.all_gather(neighbor, "row", axis=0, tiled=True),
    )
    coarse_strip = lax.all_gather(coarse_kernel, "row", axis=0, tiled=True)
    coarse = lax.all_gather(coarse_strip, "col", axis=1, tiled=True)
    row_count = lax.axis_size("row")
    col_count = lax.axis_size("col")
    fine_rows = pair_weight.shape[0]
    per_device = fine_rows // col_count
    weight_grid = pair_weight.reshape(fine_rows, row_count, col_count, per_device)
    weights = lax.dynamic_index_in_dim(weight_grid, lax.axis_index("col"), 2, keepdims=False)
    weights = weights.reshape(fine_rows, row_count * per_device)
    kernel_tile = build_tile(
        row_correlation, row_neighbor, column_correlation, column_neighbor, coarse, weights
    )
    total_rows = float(start_block.shape[0] * row_count * col_count)
    first_gram = (
        lax.psum(jnp.dot(start_block.T, start_block, precision=highest), ("row", "col"))
        / total_rows
    )
    lower_first = jnp.linalg.cholesky(first_gram)
    basis = jax.scipy.linalg.solve_triangular(lower_first, start_block.T, lower=True).T
    first_term = apply_down(kernel_tile, basis.astype(jnp.bfloat16))
    image = energies[:, None] * basis + first_term
    local_projection = jnp.dot(basis.T, image, precision=highest)
    summed_projection, summed_square = lax.psum(
        (local_projection, jnp.dot(image.T, image, precision=highest)), ("row", "col")
    )
    alpha_first = summed_projection / total_rows
    remainder = image - jnp.dot(basis, alpha_first, precision=highest)
    next_gram = summed_square / total_rows - jnp.dot(alpha_first.T, alpha_first, precision=highest)
    lower_next = jnp.linalg.cholesky(next_gram)
    second = jax.scipy.linalg.solve_triangular(lower_next, remainder.T, lower=True).T
    second_term = apply_down(kernel_tile, second.astype(jnp.bfloat16))
    image_next = (
        energies[:, None] * second + second_term - jnp.dot(basis, lower_next, precision=highest)
    )
    alpha_next = (
        lax.psum(jnp.dot(second.T, image_next, precision=highest), ("row", "col")) / total_rows
    )
    residual = image_next - jnp.dot(second, alpha_next, precision=highest)
    return (residual, jnp.stack([alpha_first, lower_next, alpha_next]))


def permute(value, dims, step):
    nz, ny, nx, nc = dims
    pairs = []
    for z in range(nz):
        for y in range(ny):
            for x in range(nx):
                for c in range(nc):
                    source = ((z * ny + y) * nx + x) * nc + c
                    target = (
                        (((z + step[0]) % nz) * ny + (y + step[1]) % ny) * nx + (x + step[2]) % nx
                    ) * nc + (c + step[3]) % nc
                    pairs.append((source, target))
    return lax.ppermute(value, AXES, pairs)


def line_order(nz):
    return [0] + sorted(range(1, nz), key=lambda s: min(s, nz - s))


def gather_everywhere(block, dims, groups, halves=False):
    nz, ny, nx, nc = dims
    line = [block]
    for s in line_order(nz)[1:]:
        line.append(permute(block, dims, (s, 0, 0, 0)))
    found = {}
    for lo, hi in groups:
        own = line[lo] if hi == lo + 1 else jnp.concatenate(line[lo:hi])
        found[(0, 0, 0, lo, hi)] = own
        middle = (lo + hi) // 2
        for y, x in sorted(((y, x) for y in range(ny) for x in range(nx)), key=sum):
            if (y, x) == (0, 0):
                continue
            if halves and y and x and lo < middle:
                at = (middle - lo) * block.shape[0]
                found[(y, x, 0, lo, middle)] = permute(
                    found[(0, x, 0, lo, hi)][:at], dims, (0, y, 0, 0)
                )
                found[(y, x, 0, middle, hi)] = permute(
                    found[(y, 0, 0, lo, hi)][at:], dims, (0, 0, x, 0)
                )
            else:
                found[(y, x, 0, lo, hi)] = permute(own, dims, (0, y, x, 0))
    for y, x, _, lo, hi in list(found):
        for c in range(1, nc):
            found[(y, x, c, lo, hi)] = permute(found[(y, x, 0, lo, hi)], dims, (0, 0, 0, c))
    return list(found.values()), list(found)


def exchange(value, dims, axis, bit):
    nz, ny, nx, nc = dims
    pairs = []
    for z in range(nz):
        for y in range(ny):
            for x in range(nx):
                for c in range(nc):
                    to = [z, y, x, c]
                    to[axis] ^= bit
                    pairs.append(
                        tuple(
                            ((p[0] * ny + p[1]) * nx + p[2]) * nc + p[3]
                            for p in ((z, y, x, c), to)
                        )
                    )
    return lax.ppermute(value, AXES, pairs)


def sum_everywhere(value, dims):
    for axis in (3, 2, 0, 1):
        n = dims[axis]
        if n & (n - 1) == 0:
            bit = 1
            while bit < n:
                other = exchange(value, dims, axis, bit)
                value = value + other
                bit *= 2
        else:
            total = value
            for s in range(1, n):
                step = [0, 0, 0, 0]
                step[axis] = s
                total = total + permute(value, dims, tuple(step))
            value = total
    return value


def split(value):
    high = value.astype(jnp.bfloat16)
    low = (value - high.astype(jnp.float32)).astype(jnp.bfloat16)
    return high, low


def times(value, weight, transposed):
    high, low = split(value)
    n = value.shape[0]
    both = lax.dot_general(
        jnp.concatenate([high, low]),
        weight,
        (((1,), (1 if transposed else 0,)), ((), ())),
        preferred_element_type=jnp.float32,
    )
    return both[:n] + both[n:]


def nt(a, b):
    return lax.dot_general(
        a, b, (((1,), (1,)), ((), ())), precision=highest, preferred_element_type=jnp.float32
    )


def nn(a, b):
    return lax.dot_general(
        a, b, (((1,), (0,)), ((), ())), precision=highest, preferred_element_type=jnp.float32
    )


def first_kernel(points, neighbor, turned, correlation, payload):
    band = correlation.shape[1]
    columns = turned.shape[0]
    for p in range(points):
        u = times(turned[:, p * band : (p + 1) * band], correlation[p], True)
        payload[pl.ds(p * columns, columns), :] = u.astype(jnp.bfloat16)
    lane = lax.broadcasted_iota(jnp.int32, (16, band), 1)
    value = jnp.zeros((16, band), jnp.float32)
    for p in range(points):
        value = jnp.where(lane == p, neighbor[p].astype(jnp.float32), value)
    payload[pl.ds(points * columns, 16), :] = value.astype(jnp.bfloat16)


def wrapped(value, n):
    return lax.rem(value + 2 * n, n)


def place(geometry):
    _, ny, _, nc = geometry.dims
    row, col = lax.axis_index("row"), lax.axis_index("col")
    return row // ny, lax.rem(row, ny), col // nc, lax.rem(col, nc)


def line_step(geometry, line):
    step = jnp.int32(geometry.order[0])
    for k in range(1, len(geometry.order)):
        step = jnp.where(line == k, geometry.order[k], step)
    return step


def weigh_kernel(geometry, pieces, block_rows, with_neighbors, continued, *refs):
    dims, points, columns = geometry.dims, geometry.points, geometry.columns
    nz, ny, nx, nc = dims
    n = len(pieces)
    starts = [sum(p[4] - p[3] for p in pieces[:k]) for k in range(n)]
    u_refs, refs = refs[:n], refs[n:]
    weight, refs = refs[0], refs[1:]
    if continued:
        before, refs = refs[:2], refs[2:]
    if with_neighbors:
        acc_0, acc_1, nbs_out, nbv, nbs, sem = refs
        for index, piece in enumerate(pieces):
            for line in range(piece[4] - piece[3]):
                at = line * block_rows + points * columns
                tile = u_refs[index][pl.ds(at, 16), :].astype(jnp.float32)
                nbv[pl.ds(starts[index] + line, 1), :] = tile[0:1].astype(jnp.int32)
        copy = pltpu.make_async_copy(nbv, nbs, sem)
        copy.start()
        nbs_out[...] = nbv[...]
    else:
        nbs, acc_0, acc_1 = refs
    sums = (acc_0, acc_1)
    for k in range(2):
        sums[k][...] = before[k][...] if continued else jnp.zeros_like(sums[k])
    if with_neighbors:
        copy.wait()
    z, y, x, c = place(geometry)
    col = lax.axis_index("col")
    for index, ref in enumerate(u_refs):
        dy, dx, dc, lo, hi = pieces[index]

        def body(line, carry, ref=ref, index=index, dy=dy, dx=dx, dc=dc, lo=lo):
            device = (
                (wrapped(z - line_step(geometry, line + lo), nz) * ny + wrapped(y - dy, ny)) * nx
                + wrapped(x - dx, nx)
            ) * nc + wrapped(c - dc, nc)
            for q in range(points):
                base = pl.multiple_of(line * block_rows + q * columns, 16)
                u = ref[pl.ds(base, columns), :].astype(jnp.float32)
                j = nbs[starts[index] + line, q]
                acc = sums[q % 2]
                for p in range(points):
                    w = weight[col * points + p, device * points + q]
                    acc[j, p] += w * u
            return carry

        lax.fori_loop(0, hi - lo, body, 0)


def choose_blocks(geometry, pieces, coarse_refs, own, chosen):
    nz, ny, nx, nc = geometry.dims
    band, per_row, per_col = geometry.band, geometry.per_row, geometry.per_col
    lines = len(geometry.order)
    z, y, x, c = place(geometry)
    for p in range(geometry.points):
        owner_row = own[p] // per_row
        dz = wrapped(z - owner_row // ny, nz)
        dy = wrapped(y - lax.rem(owner_row, ny), ny)
        line = jnp.int32(0)
        for k in range(lines):
            line = jnp.where(dz == geometry.order[k], k, line)
        inner = lax.rem(own[p], per_row)
        for dx in range(nx):
            for dc in range(nc):
                owner_col = wrapped(x - dx, nx) * nc + wrapped(c - dc, nc)
                for k in range(per_col):
                    cut = slice(k * band, (k + 1) * band)
                    block = None
                    for ref, piece in zip(coarse_refs, pieces):
                        if piece[1:3] != (dx, dc):
                            continue
                        lo, hi = piece[3:]
                        at = jnp.clip(line - lo, 0, hi - lo - 1)
                        base = pl.multiple_of((at * per_row + inner) * band, 16)
                        other = ref[pl.ds(base, band), cut]
                        if block is None:
                            block = other
                        else:
                            hit = (dy == piece[0]) & (line >= lo) & (line < hi)
                            block = jnp.where(hit, other, block)
                    chosen[p, owner_col * per_col + k] = block


def image_of(acc_0, acc_1, chosen, correlation, p):
    total = times(acc_0[0, p] + acc_1[0, p], chosen[p, 0], True)
    for j in range(1, acc_0.shape[0]):
        total += times(acc_0[j, p] + acc_1[j, p], chosen[p, j], True)
    return times(total, correlation[p], False)


def first_image_kernel(geometry, pieces, count, *refs):
    n = len(pieces)
    coarse_refs = refs[:n]
    (acc_0, acc_1, own, correlation, turned, energy, chosen, payload, image, grams) = refs[n:]
    columns, band = geometry.columns, geometry.band
    choose_blocks(geometry, pieces, coarse_refs, own, chosen)
    for p in range(geometry.points):
        cut = slice(p * band, (p + 1) * band)
        value = energy[:, cut] * turned[:, cut] + image_of(acc_0, acc_1, chosen, correlation, p)
        image[:, cut] = value
        payload[pl.ds(p * columns, columns), :] = times(value, correlation[p], True).astype(
            jnp.bfloat16
        )
    pair = jnp.concatenate([turned[...], image[...]])
    grams[...] = nt(pair, pair) * (1.0 / count)


def second_image_kernel(
    geometry, count, acc_0, acc_1, chosen, correlation, first, energy, image, gram
):
    band = geometry.band
    for p in range(geometry.points):
        cut = slice(p * band, (p + 1) * band)
        image[:, cut] = energy[:, cut] * first[:, cut] + image_of(acc_0, acc_1, chosen, correlation, p)
    gram[...] = nt(first[...], image[...]) * (1.0 / count)


def eliminate(work, begin, end):
    rows = lax.broadcasted_iota(jnp.int32, (work.shape[0], 1), 0)
    for k in range(begin, end):
        scale = lax.rsqrt(work[k : k + 1, k : k + 1])
        pivot = work[k : k + 1, :] * scale
        column = jnp.where(rows > k, work[:, k : k + 1] * scale, 0.0)
        work = jnp.where(rows == k, pivot, work - column * pivot)
    return work


def unit(m):
    return (
        lax.broadcasted_iota(jnp.int32, (m, m), 0) == lax.broadcasted_iota(jnp.int32, (m, m), 1)
    ).astype(jnp.float32)


def eliminate_kernel_1(joint, out):
    m = joint.shape[0] // 2
    work = jnp.concatenate([joint[:m, :m], unit(m), joint[:m, m:]], axis=1)
    out[...] = eliminate(work, 0, m // 2)


def eliminate_kernel_2(joint, given, out, schur):
    m = joint.shape[0] // 2
    work = eliminate(given[...], m // 2, m)
    out[...] = work
    z1 = work[:, 2 * m :]
    schur[...] = jnp.concatenate([joint[m:, m:] - nn(z1.T, z1), unit(m)], axis=1)


def eliminate_kernel_3(given, out):
    m = given.shape[0]
    out[...] = eliminate(given[...], 0, m // 2)


def eliminate_kernel_4(joint, one, given, first_two, parts):
    m = given.shape[0]
    work = eliminate(given[...], m // 2, m)
    keep = lax.broadcasted_iota(jnp.int32, (m, m), 0) <= lax.broadcasted_iota(jnp.int32, (m, m), 1)
    upper = jnp.where(keep, work[:, :m], 0.0)
    t_x = work[:, m:]
    inverse_first, z1 = one[:, m : 2 * m], one[:, 2 * m :]
    g01, g11 = joint[:m, m:], joint[m:, m:]
    first_two[0] = nt(z1, inverse_first) + SHIFT * unit(m)
    first_two[1] = nn(inverse_first, upper.T)
    t_s = -nn(t_x, nn(z1.T, inverse_first))
    p_s = nn(t_s, g01) + nn(t_x, g11)
    parts[0] = t_s
    parts[1] = t_x
    parts[2] = nt(p_s, t_s) + nt(nn(t_s, g11), t_x)
    parts[3] = nn(nn(upper, inverse_first.T), inverse_first)


def last_kernel(*refs):
    n = len(refs) - 7
    (first_two, parts, turned, first, second, residual, coefficients) = refs[n:]
    g12 = refs[0][...]
    for k in range(1, n):
        g12 += refs[k][...]
    m = g12.shape[0]
    t_s, t_x = parts[0], parts[1]
    alpha_next = parts[2] + nt(nn(t_x, g12), t_x)
    on_start = -parts[3] - nn(alpha_next, t_s)
    on_first = t_s - nn(alpha_next, t_x)
    coefficients[0] = first_two[0]
    coefficients[1] = first_two[1]
    coefficients[2] = alpha_next + SHIFT * unit(m)
    factors = jnp.concatenate([on_start, on_first, t_x], axis=1)
    residual[...] = nn(factors, jnp.concatenate([turned[...], first[...], second[...]]))


VMEM = pl.BlockSpec(memory_space=pltpu.VMEM)
SMEM = pl.BlockSpec(memory_space=pltpu.SMEM)


class Geometry:
    def __init__(self, **values):
        self.__dict__.update(values)


def shaped(shape, dtype=jnp.float32):
    return jax.ShapeDtypeStruct(shape, dtype)


def call(kernel, inputs, outputs, scratch=(), work=0.0, aliases=None):
    return pl.pallas_call(
        kernel,
        in_specs=[spec for _, spec in inputs],
        out_shape=outputs,
        out_specs=[VMEM] * len(outputs),
        scratch_shapes=list(scratch),
        input_output_aliases=aliases or {},
        cost_estimate=pl.CostEstimate(
            flops=int(work * FLOPS_PER_US), bytes_accessed=0, transcendentals=0
        ),
        compiler_params=pltpu.CompilerParams(vmem_limit_bytes=48 * 2**20),
    )(*[value for value, _ in inputs])


def weigh(geometry, arrays, pieces, block_rows, weight, neighbors, before=None):
    shape = (geometry.coarse_count, geometry.points, geometry.columns, geometry.band)
    inputs = [(a, VMEM) for a in arrays] + [(weight, SMEM)]
    at = len(inputs)
    if before is not None:
        inputs += [(b, VMEM) for b in before]
    outputs = [shaped(shape), shaped(shape)]
    scratch = []
    count = sum(piece[4] - piece[3] for piece in pieces)
    if neighbors is None:
        outputs.append(shaped((count, geometry.band), jnp.int32))
        scratch = [
            pltpu.VMEM((count, geometry.band), jnp.int32),
            pltpu.SMEM((count, geometry.band), jnp.int32),
            pltpu.SemaphoreType.DMA,
        ]
    else:
        inputs.append((neighbors, SMEM))
    found = call(
        functools.partial(
            weigh_kernel, geometry, pieces, block_rows, neighbors is None, before is not None
        ),
        inputs,
        outputs,
        scratch,
        work=1.0 * len(arrays) / 2,
        aliases={at: 0, at + 1: 1} if before is not None else None,
    )
    return found[:2], found[2:]


def on_device(coarse_kernel, correlations, neighbor, pair_weight, energies, start_block):
    rows, cols = lax.axis_size("row"), lax.axis_size("col")
    points, band, _ = correlations.shape
    columns = start_block.shape[1]
    if rows % 2 or cols % 2 or coarse_kernel.shape[0] % band or coarse_kernel.shape[1] % band:
        return general_form(
            coarse_kernel, correlations, neighbor, pair_weight, energies, start_block
        )
    dims = (rows // 2, 2, cols // 2, 2)
    order = line_order(dims[0])
    per_row, per_col = coarse_kernel.shape[0] // band, coarse_kernel.shape[1] // band
    geometry = Geometry(
        dims=dims, order=order, points=points, columns=columns, band=band,
        per_row=per_row, per_col=per_col, coarse_count=per_row * rows,
    )
    count = float(start_block.shape[0] * rows * cols)
    half = points * columns
    turned = start_block.T
    (payload,) = call(
        functools.partial(first_kernel, points),
        [(neighbor, SMEM), (turned, VMEM), (correlations, VMEM)],
        [shaped((half + 16, band), jnp.bfloat16)],
        work=1.0,
    )
    shifted = energies[None, :] - SHIFT

    nz = dims[0]
    apart = [(0, 1), (1, nz)] if nz > 1 else [(0, 1)]
    u, pieces = gather_everywhere(payload, dims, apart)
    coarse, coarse_pieces = gather_everywhere(coarse_kernel, dims, [(0, nz)], HALVES)

    def group_of(piece):
        y, x, _, lo, _ = piece
        return 0 if lo == 0 or (y, x) == (0, 0) else 1 if y == 0 else 2

    groups = [[k for k, p in enumerate(pieces) if group_of(p) == g] for g in range(3)]
    groups = [group for group in groups if group]
    acc, neighbors = None, []
    for group in groups:
        acc, found = weigh(
            geometry, [u[k] for k in group], [pieces[k] for k in group], half + 16,
            pair_weight, None, acc,
        )
        neighbors.append(found[0])
    own = neighbors[0][0, :points]
    coarse_count = geometry.coarse_count
    chosen, payload, first, joint = call(
        functools.partial(first_image_kernel, geometry, coarse_pieces, count),
        [(a, VMEM) for a in coarse]
        + [(acc[0], VMEM), (acc[1], VMEM), (own, SMEM), (correlations, VMEM), (turned, VMEM), (shifted, VMEM)],
        [
            shaped((points, coarse_count, band, band), jnp.bfloat16),
            shaped((half, band), jnp.bfloat16),
            shaped(turned.shape),
            shaped((2 * columns, 2 * columns)),
        ],
        work=3.0,
    )
    u, _ = gather_everywhere(payload, dims, apart)
    joint = sum_everywhere(joint, dims)
    acc = None
    for group, found in zip(groups, neighbors):
        acc, _ = weigh(
            geometry, [u[k] for k in group], [pieces[k] for k in group], half,
            pair_weight, found, acc,
        )
    second, g12 = call(
        functools.partial(second_image_kernel, geometry, count),
        [(acc[0], VMEM), (acc[1], VMEM), (chosen, VMEM), (correlations, VMEM), (first, VMEM), (shifted, VMEM)],
        [shaped(turned.shape), shaped((columns, columns))],
        work=3.0,
    )
    m = columns
    (one,) = call(eliminate_kernel_1, [(joint, VMEM)], [shaped((m, 3 * m))], work=3.0)
    one, schur = call(
        eliminate_kernel_2, [(joint, VMEM), (one, VMEM)],
        [shaped((m, 3 * m)), shaped((m, 2 * m))], work=3.0,
    )
    (two,) = call(eliminate_kernel_3, [(schur, VMEM)], [shaped((m, 2 * m))], work=3.0)
    first_two, parts = call(
        eliminate_kernel_4, [(joint, VMEM), (one, VMEM), (two, VMEM)],
        [shaped((2, m, m)), shaped((4, m, m))], work=3.0,
    )
    g12 = sum_everywhere(g12, dims)
    residual, coefficients = call(
        last_kernel,
        [(g12, VMEM), (first_two, VMEM), (parts, VMEM), (turned, VMEM), (first, VMEM),
         (second, VMEM)],
        [shaped(turned.shape), shaped((3, columns, columns))],
        work=2.0,
    )
    return residual.T, coefficients


def solution(mesh):
    in_specs = (
        P("row", "col"),
        P(("row", "col"), None, None),
        P(("row", "col")),
        P("row", None),
        P(("row", "col")),
        P(("row", "col"), None),
    )
    out_specs = (P(("row", "col"), None), P())
    return jax.shard_map(
        on_device, mesh=mesh, in_specs=in_specs, out_specs=out_specs, check_vma=False
    )
```

profile of v0, /device:TPU:0, one launch (start us, length us, event | category | flops | bytes accessed | tf_op | source)
XLA Modules:
  0.0 119.3 jit_solution(17126136941015765422)
XLA Ops:
  1.3 0.9 copy-done.1
  2.2 0.9 copy-done.3
  3.1 0.7 shard_map.77.refs_0_
  3.8 3.1 %collective-permute-start.10 = (bf16[272,128]{1,0:T(8,128)(2,1)S(1)}, bf16[272,128]{1,0:T(8,128)(2,1)S(1)}, u32[]{:S(2)}, u32[]{:S(2)}) collective-permute-start(bf16[272,128]{1,0:T(8,128)(2,1)S(1)} %shard_map.77.refs_0_), channel_id=1, source_target_pairs={{0,8},{1,9},{2,10},{3,11},{4,12},{5,13},{6,14},{7,15},{8,16},{9,17... | collective-permute-start | bytes 208904 | tf_op jit(solution)/shard_map/ppermute | solution.py:108
  6.9 2.1 %collective-permute-start.11 = (bf16[272,128]{1,0:T(8,128)(2,1)S(1)}, bf16[272,128]{1,0:T(8,128)(2,1)S(1)}, u32[]{:S(2)}, u32[]{:S(2)}) collective-permute-start(bf16[272,128]{1,0:T(8,128)(2,1)S(1)} %shard_map.77.refs_0_), channel_id=1, source_target_pairs={{0,24},{1,25},{2,26},{3,27},{4,28},{5,29},{6,30},{7,31},{8,0},{9,1... | collective-permute-start | bytes 208904 | tf_op jit(solution)/shard_map/ppermute | solution.py:108
  9.0 0.9 collective-permute-start.12
  10.0 1.5 %collective-permute-start.19 = (bf16[272,128]{1,0:T(8,128)(2,1)S(1)}, bf16[272,128]{1,0:T(8,128)(2,1)S(1)}, u32[]{:S(2)}, u32[]{:S(2)}) collective-permute-start(bf16[272,128]{1,0:T(8,128)(2,1)S(1)} %shard_map.77.refs_0_), channel_id=1, source_target_pairs={{0,2},{1,3},{2,0},{3,1},{4,6},{5,7},{6,4},{7,5},{8,10},{9,11},{10,... | collective-permute-start | bytes 208904 | tf_op jit(solution)/shard_map/ppermute | solution.py:108
  11.5 1.6 %collective-permute-start = (bf16[128,256]{1,0:T(8,128)(2,1)S(1)}, bf16[128,256]{1,0:T(8,128)(2,1)S(1)}, u32[]{:S(2)}, u32[]{:S(2)}) collective-permute-start(bf16[128,256]{1,0:T(8,128)(2,1)S(1)} %copy-done.6), channel_id=1, source_target_pairs={{0,8},{1,9},{2,10},{3,11},{4,12},{5,13},{6,14},{7,15},{8,16},{9,17... | collective-permute-start | bytes 196616 | tf_op jit(solution)/shard_map/ppermute | solution.py:108
  13.1 4.5 %collective-permute-done = bf16[128,256]{1,0:T(8,128)(2,1)S(1)} collective-permute-done((bf16[128,256]{1,0:T(8,128)(2,1)S(1)}, bf16[128,256]{1,0:T(8,128)(2,1)S(1)}, u32[]{:S(2)}, u32[]{:S(2)}) %collective-permute-start) | collective-permute-done | bytes 65568 | tf_op jit(solution)/shard_map/ppermute | solution.py:108
  17.5 1.5 %collective-permute-start.20 = (bf16[272,128]{1,0:T(8,128)(2,1)S(1)}, bf16[272,128]{1,0:T(8,128)(2,1)S(1)}, u32[]{:S(2)}, u32[]{:S(2)}) collective-permute-start(bf16[272,128]{1,0:T(8,128)(2,1)S(1)} %shard_map.77.refs_0_), channel_id=1, source_target_pairs={{0,4},{1,5},{2,6},{3,7},{4,0},{5,1},{6,2},{7,3},{8,12},{9,13},{10,... | collective-permute-start | bytes 208904 | tf_op jit(solution)/shard_map/ppermute | solution.py:108
  20.2 1.3 %collective-permute-start.2 = (bf16[128,256]{1,0:T(8,128)(2,1)S(1)}, bf16[128,256]{1,0:T(8,128)(2,1)S(1)}, u32[]{:S(2)}, u32[]{:S(2)}) collective-permute-start(bf16[128,256]{1,0:T(8,128)(2,1)S(1)} %copy-done.6), channel_id=1, source_target_pairs={{0,16},{1,17},{2,18},{3,19},{4,20},{5,21},{6,22},{7,23},{8,24},{9,... | collective-permute-start | bytes 196616 | tf_op jit(solution)/shard_map/ppermute | solution.py:108
  21.5 2.6 %collective-permute-done.1 = bf16[128,256]{1,0:T(8,128)(2,1)S(1)} collective-permute-done((bf16[128,256]{1,0:T(8,128)(2,1)S(1)}, bf16[128,256]{1,0:T(8,128)(2,1)S(1)}, u32[]{:S(2)}, u32[]{:S(2)}) %collective-permute-start.1) | collective-permute-done | bytes 65568 | tf_op jit(solution)/shard_map/ppermute | solution.py:108
  24.0 1.3 %collective-permute-done.2 = bf16[128,256]{1,0:T(8,128)(2,1)S(1)} collective-permute-done((bf16[128,256]{1,0:T(8,128)(2,1)S(1)}, bf16[128,256]{1,0:T(8,128)(2,1)S(1)}, u32[]{:S(2)}, u32[]{:S(2)}) %collective-permute-start.2) | collective-permute-done | bytes 65568 | tf_op jit(solution)/shard_map/ppermute | solution.py:108
  25.4 2.6 %collective-permute-start.17 = (bf16[816,128]{1,0:T(8,128)(2,1)S(1)}, bf16[816,128]{1,0:T(8,128)(2,1)S(1)}, u32[]{:S(2)}, u32[]{:S(2)}) collective-permute-start(bf16[816,128]{1,0:T(8,128)(2,1)S(1)} %constant_dynamic-update-slice_fusion.4.refs_4_), channel_id=1, source_target_pairs={{0,2},{1,3},{2,0},{3,1},{4,6},{5,7},{6,4},{7,5},{8,10},{9,11},{10,... | collective-permute-start | bytes 626696 | tf_op jit(solution)/shard_map/ppermute | solution.py:108
  29.6 1.5 %collective-permute-start.4 = (bf16[512,256]{1,0:T(8,128)(2,1)S(1)}, bf16[512,256]{1,0:T(8,128)(2,1)S(1)}, u32[]{:S(2)}, u32[]{:S(2)}) collective-permute-start(bf16[512,256]{1,0:T(8,128)(2,1)S(1)} %constant_dynamic-update-slice_fusion.refs_0_), channel_id=1, source_target_pairs={{0,4},{1,5},{2,6},{3,7},{4,0},{5,1},{6,2},{7,3},{8,12},{9,13},{10,... | collective-permute-start | bytes 786440 | tf_op jit(solution)/shard_map/ppermute | solution.py:108
  31.1 1.7 %collective-permute-start.5 = (bf16[512,256]{1,0:T(8,128)(2,1)S(1)}, bf16[512,256]{1,0:T(8,128)(2,1)S(1)}, u32[]{:S(2)}, u32[]{:S(2)}) collective-permute-start(bf16[512,256]{1,0:T(8,128)(2,1)S(1)} %constant_dynamic-update-slice_fusion.refs_0_), channel_id=1, source_target_pairs={{0,6},{1,7},{2,4},{3,5},{4,2},{5,3},{6,0},{7,1},{8,14},{9,15},{10,... | collective-permute-start | bytes 786440 | tf_op jit(solution)/shard_map/ppermute | solution.py:108
  32.9 1.5 %collective-permute-start.13 = (bf16[816,128]{1,0:T(8,128)(2,1)S(1)}, bf16[816,128]{1,0:T(8,128)(2,1)S(1)}, u32[]{:S(2)}, u32[]{:S(2)}) collective-permute-start(bf16[816,128]{1,0:T(8,128)(2,1)S(1)} %constant_dynamic-update-slice_fusion.4.refs_4_), channel_id=1, source_target_pairs={{0,4},{1,5},{2,6},{3,7},{4,0},{5,1},{6,2},{7,3},{8,12},{9,13},{10,... | collective-permute-start | bytes 626696 | tf_op jit(solution)/shard_map/ppermute | solution.py:108
  34.4 2.6 %collective-permute-start.14 = (bf16[816,128]{1,0:T(8,128)(2,1)S(1)}, bf16[816,128]{1,0:T(8,128)(2,1)S(1)}, u32[]{:S(2)}, u32[]{:S(2)}) collective-permute-start(bf16[816,128]{1,0:T(8,128)(2,1)S(1)} %constant_dynamic-update-slice_fusion.4.refs_4_), channel_id=1, source_target_pairs={{0,6},{1,7},{2,4},{3,5},{4,2},{5,3},{6,0},{7,1},{8,14},{9,15},{10,... | collective-permute-start | bytes 626696 | tf_op jit(solution)/shard_map/ppermute | solution.py:108
  37.0 15.6 %collective-permute-done.13.refs_0_ = bf16[816,128]{1,0:T(8,128)(2,1)S(1)} collective-permute-done((bf16[816,128]{1,0:T(8,128)(2,1)S(1)}, bf16[816,128]{1,0:T(8,128)(2,1)S(1)}, u32[]{:S(2)}, u32[]{:S(2)}) %collective-permute-start.13) | collective-permute-done | bytes 208928 | tf_op jit(solution)/shard_map/ppermute | solution.py:108
  53.2 2.2 %shard_map.78 = (f32[8,4,64,128]{3,2,1,0:T(8,128)S(1)}, f32[8,4,64,128]{3,2,1,0:T(8,128)S(1)}, s32[14,128]{1,0:T(8,128)S(1)}) custom-call(bf16[272,128]{1,0:T(8,128)(2,1)S(1)} %shard_map.77.refs_0_, bf16[272,128]{1,0:T(8,128)(2,1)S(1)} %collective-permute-done.19.refs_1_, bf16[272,128]{1,0:T(8,128)(2,1)S(1)} %collective-permute-done.20.refs_2_, ...), custom_call_target="tpu_custom_call" | custom-call | flops 2500000000 | tf_op jit(solution)/shard_map/pallas_call | solution.py:443
  56.6 1.7 %shard_map.79 = (f32[8,4,64,128]{3,2,1,0:T(8,128)S(1)}, f32[8,4,64,128]{3,2,1,0:T(8,128)S(1)}, s32[6,128]{1,0:T(8,128)S(1)}) custom-call(bf16[816,128]{1,0:T(8,128)(2,1)S(1)} %collective-permute-done.17.refs_0_, bf16[816,128]{1,0:T(8,128)(2,1)S(1)} %collective-permute-done.18.refs_1_, ...), custom_call_target="tpu_custom_call", output_to_operand_aliasing={{0}: (3, {}), {1}: (4, {})} | custom-call | flops 500000000 | tf_op jit(solution)/shard_map/pallas_call | solution.py:443
  58.3 2.1 %shard_map.80 = (f32[8,4,64,128]{3,2,1,0:T(8,128)S(1)}, f32[8,4,64,128]{3,2,1,0:T(8,128)S(1)}, s32[12,128]{1,0:T(8,128)S(1)}) custom-call(bf16[816,128]{1,0:T(8,128)(2,1)S(1)} %collective-permute-done.13.refs_0_, bf16[816,128]{1,0:T(8,128)(2,1)S(1)} %collective-permute-done.14.refs_1_, ...), custom_call_target="tpu_custom_call", output_to_operand_aliasing={{0}: (5, {}), {1}: (6, {})} | custom-call | flops 1000000000 | tf_op jit(solution)/shard_map/pallas_call | solution.py:443
  60.5 3.4 %shard_map.81 = (bf16[4,8,128,128]{3,2,1,0:T(8,128)(2,1)S(1)}, bf16[256,128]{1,0:T(8,128)(2,1)S(1)}, f32[64,512]{1,0:T(8,128)S(1)}, f32[128,128]{1,0:T(8,128)S(1)}) custom-call(bf16[512,256]{1,0:T(8,128)(2,1)S(1)} %constant_dynamic-update-slice_fusion.refs_0_, bf16[512,256]{1,0:T(8,128)(2,1)S(1)} %collective-permute-done.3.refs_1_, ...), custom_call_target="tpu_custom_call" | custom-call | flops 1500000000 | tf_op jit(solution)/shard_map/pallas_call | solution.py:443
  64.9 3.3 %collective-permute-start.28 = (bf16[256,128]{1,0:T(8,128)(2,1)S(1)}, bf16[256,128]{1,0:T(8,128)(2,1)S(1)}, u32[]{:S(2)}, u32[]{:S(2)}) collective-permute-start(bf16[256,128]{1,0:T(8,128)(2,1)S(1)} %get-tuple-element.36.refs_0_), channel_id=1, source_target_pairs={{0,24},{1,25},{2,26},{3,27},{4,28},{5,29},{6,30},{7,31},{8,0},{9,1... | collective-permute-start | bytes 196616 | tf_op jit(solution)/shard_map/ppermute | solution.py:108
  68.2 1.5 %collective-permute-start.36 = (bf16[256,128]{1,0:T(8,128)(2,1)S(1)}, bf16[256,128]{1,0:T(8,128)(2,1)S(1)}, u32[]{:S(2)}, u32[]{:S(2)}) collective-permute-start(bf16[256,128]{1,0:T(8,128)(2,1)S(1)} %get-tuple-element.36.refs_0_), channel_id=1, source_target_pairs={{0,2},{1,3},{2,0},{3,1},{4,6},{5,7},{6,4},{7,5},{8,10},{9,11},{10,... | collective-permute-start | bytes 196616 | tf_op jit(solution)/shard_map/ppermute | solution.py:108
  69.7 1.5 %collective-permute-start.37 = (bf16[256,128]{1,0:T(8,128)(2,1)S(1)}, bf16[256,128]{1,0:T(8,128)(2,1)S(1)}, u32[]{:S(2)}, u32[]{:S(2)}) collective-permute-start(bf16[256,128]{1,0:T(8,128)(2,1)S(1)} %get-tuple-element.36.refs_0_), channel_id=1, source_target_pairs={{0,4},{1,5},{2,6},{3,7},{4,0},{5,1},{6,2},{7,3},{8,12},{9,13},{10,... | collective-permute-start | bytes 196616 | tf_op jit(solution)/shard_map/ppermute | solution.py:108
  71.2 2.3 %collective-permute-start.38 = (bf16[256,128]{1,0:T(8,128)(2,1)S(1)}, bf16[256,128]{1,0:T(8,128)(2,1)S(1)}, u32[]{:S(2)}, u32[]{:S(2)}) collective-permute-start(bf16[256,128]{1,0:T(8,128)(2,1)S(1)} %get-tuple-element.36.refs_0_), channel_id=1, source_target_pairs={{0,6},{1,7},{2,4},{3,5},{4,2},{5,3},{6,0},{7,1},{8,14},{9,15},{10,... | collective-permute-start | bytes 196616 | tf_op jit(solution)/shard_map/ppermute | solution.py:108
  74.8 3.1 %collective-permute-done.50 = f32[128,128]{1,0:T(8,128)S(1)} collective-permute-done((f32[128,128]{1,0:T(8,128)S(1)}, f32[128,128]{1,0:T(8,128)S(1)}, u32[]{:S(2)}, u32[]{:S(2)}) %collective-permute-start.50) | collective-permute-done | bytes 65568 | tf_op jit(solution)/shard_map/ppermute | solution.py:159
  78.7 1.1 collective-permute-start.30
  79.9 1.7 %collective-permute-start.31 = (bf16[768,128]{1,0:T(8,128)(2,1)S(1)}, bf16[768,128]{1,0:T(8,128)(2,1)S(1)}, u32[]{:S(2)}, u32[]{:S(2)}) collective-permute-start(bf16[768,128]{1,0:T(8,128)(2,1)S(1)} %constant_dynamic-update-slice_fusion.7.refs_4_), channel_id=1, source_target_pairs={{0,6},{1,7},{2,4},{3,5},{4,2},{5,3},{6,0},{7,1},{8,14},{9,15},{10,... | collective-permute-start | bytes 589832 | tf_op jit(solution)/shard_map/ppermute | solution.py:108
  81.6 0.9 collective-permute-done.51
  82.5 1.3 %collective-permute-start.52 = (f32[128,128]{1,0:T(8,128)S(1)}, f32[128,128]{1,0:T(8,128)S(1)}, u32[]{:S(2)}, u32[]{:S(2)}) collective-permute-start(f32[128,128]{1,0:T(8,128)S(1)} %add.39), channel_id=1, source_target_pairs={{0,16},{1,17},{2,18},{3,19},{4,20},{5,21},{6,22},{7,23},{8,24},{9,... | collective-permute-start | bytes 196616 | tf_op jit(solution)/shard_map/ppermute | solution.py:159
  83.8 5.6 %collective-permute-done.52 = f32[128,128]{1,0:T(8,128)S(1)} collective-permute-done((f32[128,128]{1,0:T(8,128)S(1)}, f32[128,128]{1,0:T(8,128)S(1)}, u32[]{:S(2)}, u32[]{:S(2)}) %collective-permute-start.52) | collective-permute-done | bytes 65568 | tf_op jit(solution)/shard_map/ppermute | solution.py:159
  89.4 1.2 %collective-permute-done.42.refs_8_ = bf16[256,128]{1,0:T(8,128)(2,1)S(1)} collective-permute-done((bf16[256,128]{1,0:T(8,128)(2,1)S(1)}, bf16[256,128]{1,0:T(8,128)(2,1)S(1)}, u32[]{:S(2)}, u32[]{:S(2)}) %collective-permute-start.42) | collective-permute-done | bytes 65568 | tf_op jit(solution)/shard_map/ppermute | solution.py:108
  91.8 1.7 %shard_map.82 = (f32[8,4,64,128]{3,2,1,0:T(8,128)S(1)}, f32[8,4,64,128]{3,2,1,0:T(8,128)S(1)}) custom-call(bf16[256,128]{1,0:T(8,128)(2,1)S(1)} %get-tuple-element.36.refs_0_, bf16[256,128]{1,0:T(8,128)(2,1)S(1)} %collective-permute-done.36.refs_1_, bf16[256,128]{1,0:T(8,128)(2,1)S(1)} %collective-permute-done.37.refs_2_, ...), custom_call_target="tpu_custom_call" | custom-call | flops 2500000000 | tf_op jit(solution)/shard_map/pallas_call | solution.py:443
  93.4 1.4 %shard_map.83 = (f32[8,4,64,128]{3,2,1,0:T(8,128)S(1)}, f32[8,4,64,128]{3,2,1,0:T(8,128)S(1)}) custom-call(bf16[768,128]{1,0:T(8,128)(2,1)S(1)} %collective-permute-done.34.refs_0_, bf16[768,128]{1,0:T(8,128)(2,1)S(1)} %collective-permute-done.35.refs_1_, f32[16,128]{1,0:T(8,128)S(1)} %copy-done, ...), custom_call_target="tpu_custom_call", output_to_operand_aliasing={{0}: (3, {}), {1}: (4, {})} | custom-call | flops 500000000 | tf_op jit(solution)/shard_map/pallas_call | solution.py:443
  94.8 1.8 %shard_map.84 = (f32[8,4,64,128]{3,2,1,0:T(8,128)S(1)}, f32[8,4,64,128]{3,2,1,0:T(8,128)S(1)}) custom-call(bf16[768,128]{1,0:T(8,128)(2,1)S(1)} %collective-permute-done.30.refs_0_, bf16[768,128]{1,0:T(8,128)(2,1)S(1)} %collective-permute-done.31.refs_1_, ...), custom_call_target="tpu_custom_call", output_to_operand_aliasing={{0}: (5, {}), {1}: (6, {})} | custom-call | flops 1000000000 | tf_op jit(solution)/shard_map/pallas_call | solution.py:443
  96.7 1.9 %shard_map.85 = (f32[64,512]{1,0:T(8,128)S(1)}, f32[64,64]{1,0:T(8,128)S(1)}) custom-call(f32[8,4,64,128]{3,2,1,0:T(8,128)S(1)} %get-tuple-element.43.acc_0, f32[8,4,64,128]{3,2,1,0:T(8,128)S(1)} %get-tuple-element.44.acc_1, bf16[4,8,128,128]{3,2,1,0:T(8,128)(2,1)S(1)} %get-tuple-element.45.chosen, bf16[4,128,128]{2,1,0:T(8,128)(2,1)S(1)} %copy-done.2, ...), custom_call_target="tpu_custom_call" | custom-call | flops 1500000000 | tf_op jit(solution)/shard_map/pallas_call | solution.py:443
  99.1 0.8 collective-permute-done.44
  100.0 1.0 collective-permute-start.45
  101.0 2.8 %shard_map.86.given = f32[64,192]{1,0:T(8,128)S(1)} custom-call(f32[128,128]{1,0:T(8,128)S(1)} %add.41.joint), custom_call_target="tpu_custom_call" | custom-call | flops 1500000000 | tf_op jit(solution)/shard_map/pallas_call | solution.py:443
  103.9 0.7 collective-permute-start.46
  104.6 3.0 %shard_map.87 = (f32[64,192]{1,0:T(8,128)S(1)}, f32[64,128]{1,0:T(8,128)S(1)}) custom-call(f32[128,128]{1,0:T(8,128)S(1)} %add.41.joint, f32[64,192]{1,0:T(8,128)S(1)} %shard_map.86.given), custom_call_target="tpu_custom_call" | custom-call | flops 1500000000 | tf_op jit(solution)/shard_map/pallas_call | solution.py:443
  107.8 2.9 %collective-permute-start.47 = (f32[64,64]{1,0:T(8,128)S(1)}, f32[64,64]{1,0:T(8,128)S(1)}, u32[]{:S(2)}, u32[]{:S(2)}) collective-permute-start(f32[64,64]{1,0:T(8,128)S(1)} %add.34), channel_id=1, source_target_pairs={{0,16},{1,17},{2,18},{3,19},{4,20},{5,21},{6,22},{7,23},{8,24},{9,... | collective-permute-start | bytes 49160 | tf_op jit(solution)/shard_map/ppermute | solution.py:159
  110.7 2.7 %shard_map.88.given = f32[64,128]{1,0:T(8,128)S(1)} custom-call(f32[64,128]{1,0:T(8,128)S(1)} %get-tuple-element.50.given), custom_call_target="tpu_custom_call" | custom-call | flops 1500000000 | tf_op jit(solution)/shard_map/pallas_call | solution.py:443
  113.4 0.8 collective-permute-start.48
  114.2 3.4 %shard_map.89 = (f32[2,64,64]{2,1,0:T(8,128)S(1)}, f32[4,64,64]{2,1,0:T(8,128)S(1)}) custom-call(f32[128,128]{1,0:T(8,128)S(1)} %add.41.joint, f32[64,192]{1,0:T(8,128)S(1)} %get-tuple-element.49.one, f32[64,128]{1,0:T(8,128)S(1)} %shard_map.88.given), custom_call_target="tpu_custom_call" | custom-call | flops 1500000000 | tf_op jit(solution)/shard_map/pallas_call | solution.py:443
  117.6 1.6 %shard_map.90 = (f32[64,512]{1,0:T(8,128)}, f32[3,64,64]{2,1,0:T(8,128)}) custom-call(f32[64,64]{1,0:T(8,128)S(1)} %add.36.refs_0_, f32[2,64,64]{2,1,0:T(8,128)S(1)} %get-tuple-element.51.refs_1_, f32[4,64,64]{2,1,0:T(8,128)S(1)} %get-tuple-element.52.refs_2_, f32[64,512]{1,0:T(8,128)S(1)} %bitcast.9, f32[64,512]{1,0:T(8,128)S(1)} %get-tuple-element.46.first.refs_4_, ...), custom_call_target="tpu_custom_call" | custom-call | flops 1000000000 | tf_op jit(solution)/shard_map/pallas_call | solution.py:443
  (112 shorter events, 10.1 us)
Async XLA Ops:
  3.8 15.2 %collective-permute-start.10 = (bf16[272,128]{1,0:T(8,128)(2,1)S(1)}, bf16[272,128]{1,0:T(8,128)(2,1)S(1)}, u32[]{:S(2)}, u32[]{:S(2)}) collective-permute-start(bf16[272,128]{1,0:T(8,128)(2,1)S(1)} %shard_map.77.refs_0_), channel_id=1, source_target_pairs={{0,8},{1,9},{2,10},{3,11},{4,12},{5,13},{6,14},{7,15},{8,16},{9,17... | collective-permute-start | bytes 208904 | tf_op jit(solution)/shard_map/ppermute | solution.py:108
  6.9 12.8 %collective-permute-start.11 = (bf16[272,128]{1,0:T(8,128)(2,1)S(1)}, bf16[272,128]{1,0:T(8,128)(2,1)S(1)}, u32[]{:S(2)}, u32[]{:S(2)}) collective-permute-start(bf16[272,128]{1,0:T(8,128)(2,1)S(1)} %shard_map.77.refs_0_), channel_id=1, source_target_pairs={{0,24},{1,25},{2,26},{3,27},{4,28},{5,29},{6,30},{7,31},{8,0},{9,1... | collective-permute-start | bytes 208904 | tf_op jit(solution)/shard_map/ppermute | solution.py:108
  9.0 11.1 %collective-permute-start.12 = (bf16[272,128]{1,0:T(8,128)(2,1)S(1)}, bf16[272,128]{1,0:T(8,128)(2,1)S(1)}, u32[]{:S(2)}, u32[]{:S(2)}) collective-permute-start(bf16[272,128]{1,0:T(8,128)(2,1)S(1)} %shard_map.77.refs_0_), channel_id=1, source_target_pairs={{0,16},{1,17},{2,18},{3,19},{4,20},{5,21},{6,22},{7,23},{8,24},{9,... | collective-permute-start | bytes 208904 | tf_op jit(solution)/shard_map/ppermute | solution.py:108
  10.0 15.4 %collective-permute-start.19 = (bf16[272,128]{1,0:T(8,128)(2,1)S(1)}, bf16[272,128]{1,0:T(8,128)(2,1)S(1)}, u32[]{:S(2)}, u32[]{:S(2)}) collective-permute-start(bf16[272,128]{1,0:T(8,128)(2,1)S(1)} %shard_map.77.refs_0_), channel_id=1, source_target_pairs={{0,2},{1,3},{2,0},{3,1},{4,6},{5,7},{6,4},{7,5},{8,10},{9,11},{10,... | collective-permute-start | bytes 208904 | tf_op jit(solution)/shard_map/ppermute | solution.py:108
  11.5 6.1 %collective-permute-start = (bf16[128,256]{1,0:T(8,128)(2,1)S(1)}, bf16[128,256]{1,0:T(8,128)(2,1)S(1)}, u32[]{:S(2)}, u32[]{:S(2)}) collective-permute-start(bf16[128,256]{1,0:T(8,128)(2,1)S(1)} %copy-done.6), channel_id=1, source_target_pairs={{0,8},{1,9},{2,10},{3,11},{4,12},{5,13},{6,14},{7,15},{8,16},{9,17... | collective-permute-start | bytes 196616 | tf_op jit(solution)/shard_map/ppermute | solution.py:108
  17.5 10.5 %collective-permute-start.20 = (bf16[272,128]{1,0:T(8,128)(2,1)S(1)}, bf16[272,128]{1,0:T(8,128)(2,1)S(1)}, u32[]{:S(2)}, u32[]{:S(2)}) collective-permute-start(bf16[272,128]{1,0:T(8,128)(2,1)S(1)} %shard_map.77.refs_0_), channel_id=1, source_target_pairs={{0,4},{1,5},{2,6},{3,7},{4,0},{5,1},{6,2},{7,3},{8,12},{9,13},{10,... | collective-permute-start | bytes 208904 | tf_op jit(solution)/shard_map/ppermute | solution.py:108
  19.1 9.3 %collective-permute-start.21 = (bf16[272,128]{1,0:T(8,128)(2,1)S(1)}, bf16[272,128]{1,0:T(8,128)(2,1)S(1)}, u32[]{:S(2)}, u32[]{:S(2)}) collective-permute-start(bf16[272,128]{1,0:T(8,128)(2,1)S(1)} %shard_map.77.refs_0_), channel_id=1, source_target_pairs={{0,6},{1,7},{2,4},{3,5},{4,2},{5,3},{6,0},{7,1},{8,14},{9,15},{10,... | collective-permute-start | bytes 208904 | tf_op jit(solution)/shard_map/ppermute | solution.py:108
  19.7 4.3 %collective-permute-start.1 = (bf16[128,256]{1,0:T(8,128)(2,1)S(1)}, bf16[128,256]{1,0:T(8,128)(2,1)S(1)}, u32[]{:S(2)}, u32[]{:S(2)}) collective-permute-start(bf16[128,256]{1,0:T(8,128)(2,1)S(1)} %copy-done.6), channel_id=1, source_target_pairs={{0,24},{1,25},{2,26},{3,27},{4,28},{5,29},{6,30},{7,31},{8,0},{9,1... | collective-permute-start | bytes 196616 | tf_op jit(solution)/shard_map/ppermute | solution.py:108
  20.2 5.2 %collective-permute-start.2 = (bf16[128,256]{1,0:T(8,128)(2,1)S(1)}, bf16[128,256]{1,0:T(8,128)(2,1)S(1)}, u32[]{:S(2)}, u32[]{:S(2)}) collective-permute-start(bf16[128,256]{1,0:T(8,128)(2,1)S(1)} %copy-done.6), channel_id=1, source_target_pairs={{0,16},{1,17},{2,18},{3,19},{4,20},{5,21},{6,22},{7,23},{8,24},{9,... | collective-permute-start | bytes 196616 | tf_op jit(solution)/shard_map/ppermute | solution.py:108
  24.0 4.6 %collective-permute-start.22 = (bf16[272,128]{1,0:T(8,128)(2,1)S(1)}, bf16[272,128]{1,0:T(8,128)(2,1)S(1)}, u32[]{:S(2)}, u32[]{:S(2)}) collective-permute-start(bf16[272,128]{1,0:T(8,128)(2,1)S(1)} %shard_map.77.refs_0_), channel_id=1, source_target_pairs={{0,1},{1,0},{2,3},{3,2},{4,5},{5,4},{6,7},{7,6},{8,9},{9,8},{10,11... | collective-permute-start | bytes 208904 | tf_op jit(solution)/shard_map/ppermute | solution.py:108
  25.4 7.5 %collective-permute-start.26 = (bf16[816,128]{1,0:T(8,128)(2,1)S(1)}, bf16[816,128]{1,0:T(8,128)(2,1)S(1)}, u32[]{:S(2)}, u32[]{:S(2)}) collective-permute-start(bf16[816,128]{1,0:T(8,128)(2,1)S(1)} %constant_dynamic-update-slice_fusion.4.refs_4_), channel_id=1, source_target_pairs={{0,1},{1,0},{2,3},{3,2},{4,5},{5,4},{6,7},{7,6},{8,9},{9,8},{10,11... | collective-permute-start | bytes 626696 | tf_op jit(solution)/shard_map/ppermute | solution.py:108
  25.4 9.0 %collective-permute-start.17 = (bf16[816,128]{1,0:T(8,128)(2,1)S(1)}, bf16[816,128]{1,0:T(8,128)(2,1)S(1)}, u32[]{:S(2)}, u32[]{:S(2)}) collective-permute-start(bf16[816,128]{1,0:T(8,128)(2,1)S(1)} %constant_dynamic-update-slice_fusion.4.refs_4_), channel_id=1, source_target_pairs={{0,2},{1,3},{2,0},{3,1},{4,6},{5,7},{6,4},{7,5},{8,10},{9,11},{10,... | collective-permute-start | bytes 626696 | tf_op jit(solution)/shard_map/ppermute | solution.py:108
  29.4 26.0 %collective-permute-start.3 = (bf16[512,256]{1,0:T(8,128)(2,1)S(1)}, bf16[512,256]{1,0:T(8,128)(2,1)S(1)}, u32[]{:S(2)}, u32[]{:S(2)}) collective-permute-start(bf16[512,256]{1,0:T(8,128)(2,1)S(1)} %constant_dynamic-update-slice_fusion.refs_0_), channel_id=1, source_target_pairs={{0,2},{1,3},{2,0},{3,1},{4,6},{5,7},{6,4},{7,5},{8,10},{9,11},{10,... | collective-permute-start | bytes 786440 | tf_op jit(solution)/shard_map/ppermute | solution.py:108
  29.6 25.9 %collective-permute-start.4 = (bf16[512,256]{1,0:T(8,128)(2,1)S(1)}, bf16[512,256]{1,0:T(8,128)(2,1)S(1)}, u32[]{:S(2)}, u32[]{:S(2)}) collective-permute-start(bf16[512,256]{1,0:T(8,128)(2,1)S(1)} %constant_dynamic-update-slice_fusion.refs_0_), channel_id=1, source_target_pairs={{0,4},{1,5},{2,6},{3,7},{4,0},{5,1},{6,2},{7,3},{8,12},{9,13},{10,... | collective-permute-start | bytes 786440 | tf_op jit(solution)/shard_map/ppermute | solution.py:108
  31.1 24.9 %collective-permute-start.5 = (bf16[512,256]{1,0:T(8,128)(2,1)S(1)}, bf16[512,256]{1,0:T(8,128)(2,1)S(1)}, u32[]{:S(2)}, u32[]{:S(2)}) collective-permute-start(bf16[512,256]{1,0:T(8,128)(2,1)S(1)} %constant_dynamic-update-slice_fusion.refs_0_), channel_id=1, source_target_pairs={{0,6},{1,7},{2,4},{3,5},{4,2},{5,3},{6,0},{7,1},{8,14},{9,15},{10,... | collective-permute-start | bytes 786440 | tf_op jit(solution)/shard_map/ppermute | solution.py:108
  32.9 19.8 %collective-permute-start.13 = (bf16[816,128]{1,0:T(8,128)(2,1)S(1)}, bf16[816,128]{1,0:T(8,128)(2,1)S(1)}, u32[]{:S(2)}, u32[]{:S(2)}) collective-permute-start(bf16[816,128]{1,0:T(8,128)(2,1)S(1)} %constant_dynamic-update-slice_fusion.4.refs_4_), channel_id=1, source_target_pairs={{0,4},{1,5},{2,6},{3,7},{4,0},{5,1},{6,2},{7,3},{8,12},{9,13},{10,... | collective-permute-start | bytes 626696 | tf_op jit(solution)/shard_map/ppermute | solution.py:108
  34.4 18.3 %collective-permute-start.14 = (bf16[816,128]{1,0:T(8,128)(2,1)S(1)}, bf16[816,128]{1,0:T(8,128)(2,1)S(1)}, u32[]{:S(2)}, u32[]{:S(2)}) collective-permute-start(bf16[816,128]{1,0:T(8,128)(2,1)S(1)} %constant_dynamic-update-slice_fusion.4.refs_4_), channel_id=1, source_target_pairs={{0,6},{1,7},{2,4},{3,5},{4,2},{5,3},{6,0},{7,1},{8,14},{9,15},{10,... | collective-permute-start | bytes 626696 | tf_op jit(solution)/shard_map/ppermute | solution.py:108
  52.7 3.4 %collective-permute-start.18 = (bf16[816,128]{1,0:T(8,128)(2,1)S(1)}, bf16[816,128]{1,0:T(8,128)(2,1)S(1)}, u32[]{:S(2)}, u32[]{:S(2)}) collective-permute-start(bf16[816,128]{1,0:T(8,128)(2,1)S(1)} %collective-permute-done.17.refs_0_), channel_id=1, source_target_pairs={{0,1},{1,0},{2,3},{3,2},{4,5},{5,4},{6,7},{7,6},{8,9},{9,8},{10,11... | collective-permute-start | bytes 626696 | tf_op jit(solution)/shard_map/ppermute | solution.py:108
  52.7 3.8 %collective-permute-start.15 = (bf16[816,128]{1,0:T(8,128)(2,1)S(1)}, bf16[816,128]{1,0:T(8,128)(2,1)S(1)}, u32[]{:S(2)}, u32[]{:S(2)}) collective-permute-start(bf16[816,128]{1,0:T(8,128)(2,1)S(1)} %collective-permute-done.13.refs_0_), channel_id=1, source_target_pairs={{0,1},{1,0},{2,3},{3,2},{4,5},{5,4},{6,7},{7,6},{8,9},{9,8},{10,11... | collective-permute-start | bytes 626696 | tf_op jit(solution)/shard_map/ppermute | solution.py:108
  55.4 5.0 %collective-permute-start.6 = (bf16[512,256]{1,0:T(8,128)(2,1)S(1)}, bf16[512,256]{1,0:T(8,128)(2,1)S(1)}, u32[]{:S(2)}, u32[]{:S(2)}) collective-permute-start(bf16[512,256]{1,0:T(8,128)(2,1)S(1)} %constant_dynamic-update-slice_fusion.refs_0_), channel_id=1, source_target_pairs={{0,1},{1,0},{2,3},{3,2},{4,5},{5,4},{6,7},{7,6},{8,9},{9,8},{10,11... | collective-permute-start | bytes 786440 | tf_op jit(solution)/shard_map/ppermute | solution.py:108
  55.5 2.8 %collective-permute-start.16 = (bf16[816,128]{1,0:T(8,128)(2,1)S(1)}, bf16[816,128]{1,0:T(8,128)(2,1)S(1)}, u32[]{:S(2)}, u32[]{:S(2)}) collective-permute-start(bf16[816,128]{1,0:T(8,128)(2,1)S(1)} %collective-permute-done.14.refs_1_), channel_id=1, source_target_pairs={{0,1},{1,0},{2,3},{3,2},{4,5},{5,4},{6,7},{7,6},{8,9},{9,8},{10,11... | collective-permute-start | bytes 626696 | tf_op jit(solution)/shard_map/ppermute | solution.py:108
  56.0 4.4 %collective-permute-start.7 = (bf16[512,256]{1,0:T(8,128)(2,1)S(1)}, bf16[512,256]{1,0:T(8,128)(2,1)S(1)}, u32[]{:S(2)}, u32[]{:S(2)}) collective-permute-start(bf16[512,256]{1,0:T(8,128)(2,1)S(1)} %collective-permute-done.3.refs_1_), channel_id=1, source_target_pairs={{0,1},{1,0},{2,3},{3,2},{4,5},{5,4},{6,7},{7,6},{8,9},{9,8},{10,11... | collective-permute-start | bytes 786440 | tf_op jit(solution)/shard_map/ppermute | solution.py:108
  56.1 4.3 %collective-permute-start.8 = (bf16[512,256]{1,0:T(8,128)(2,1)S(1)}, bf16[512,256]{1,0:T(8,128)(2,1)S(1)}, u32[]{:S(2)}, u32[]{:S(2)}) collective-permute-start(bf16[512,256]{1,0:T(8,128)(2,1)S(1)} %collective-permute-done.4.refs_2_), channel_id=1, source_target_pairs={{0,1},{1,0},{2,3},{3,2},{4,5},{5,4},{6,7},{7,6},{8,9},{9,8},{10,11... | collective-permute-start | bytes 786440 | tf_op jit(solution)/shard_map/ppermute | solution.py:108
  56.5 3.9 %collective-permute-start.9 = (bf16[512,256]{1,0:T(8,128)(2,1)S(1)}, bf16[512,256]{1,0:T(8,128)(2,1)S(1)}, u32[]{:S(2)}, u32[]{:S(2)}) collective-permute-start(bf16[512,256]{1,0:T(8,128)(2,1)S(1)} %collective-permute-done.5.refs_3_), channel_id=1, source_target_pairs={{0,1},{1,0},{2,3},{3,2},{4,5},{5,4},{6,7},{7,6},{8,9},{9,8},{10,11... | collective-permute-start | bytes 786440 | tf_op jit(solution)/shard_map/ppermute | solution.py:108
  63.9 5.8 %collective-permute-start.49 = (f32[128,128]{1,0:T(8,128)S(1)}, f32[128,128]{1,0:T(8,128)S(1)}, u32[]{:S(2)}, u32[]{:S(2)}) collective-permute-start(f32[128,128]{1,0:T(8,128)S(1)} %get-tuple-element.48), channel_id=1, source_target_pairs={{0,1},{1,0},{2,3},{3,2},{4,5},{5,4},{6,7},{7,6},{8,9},{9,8},{10,11... | collective-permute-start | bytes 196616 | tf_op jit(solution)/shard_map/ppermute | solution.py:159
  64.4 6.8 %collective-permute-start.27 = (bf16[256,128]{1,0:T(8,128)(2,1)S(1)}, bf16[256,128]{1,0:T(8,128)(2,1)S(1)}, u32[]{:S(2)}, u32[]{:S(2)}) collective-permute-start(bf16[256,128]{1,0:T(8,128)(2,1)S(1)} %get-tuple-element.36.refs_0_), channel_id=1, source_target_pairs={{0,8},{1,9},{2,10},{3,11},{4,12},{5,13},{6,14},{7,15},{8,16},{9,17... | collective-permute-start | bytes 196616 | tf_op jit(solution)/shard_map/ppermute | solution.py:108
  64.9 8.7 %collective-permute-start.28 = (bf16[256,128]{1,0:T(8,128)(2,1)S(1)}, bf16[256,128]{1,0:T(8,128)(2,1)S(1)}, u32[]{:S(2)}, u32[]{:S(2)}) collective-permute-start(bf16[256,128]{1,0:T(8,128)(2,1)S(1)} %get-tuple-element.36.refs_0_), channel_id=1, source_target_pairs={{0,24},{1,25},{2,26},{3,27},{4,28},{5,29},{6,30},{7,31},{8,0},{9,1... | collective-permute-start | bytes 196616 | tf_op jit(solution)/shard_map/ppermute | solution.py:108
  68.2 9.7 %collective-permute-start.29 = (bf16[256,128]{1,0:T(8,128)(2,1)S(1)}, bf16[256,128]{1,0:T(8,128)(2,1)S(1)}, u32[]{:S(2)}, u32[]{:S(2)}) collective-permute-start(bf16[256,128]{1,0:T(8,128)(2,1)S(1)} %get-tuple-element.36.refs_0_), channel_id=1, source_target_pairs={{0,16},{1,17},{2,18},{3,19},{4,20},{5,21},{6,22},{7,23},{8,24},{9,... | collective-permute-start | bytes 196616 | tf_op jit(solution)/shard_map/ppermute | solution.py:108
  68.2 6.0 %collective-permute-start.36 = (bf16[256,128]{1,0:T(8,128)(2,1)S(1)}, bf16[256,128]{1,0:T(8,128)(2,1)S(1)}, u32[]{:S(2)}, u32[]{:S(2)}) collective-permute-start(bf16[256,128]{1,0:T(8,128)(2,1)S(1)} %get-tuple-element.36.refs_0_), channel_id=1, source_target_pairs={{0,2},{1,3},{2,0},{3,1},{4,6},{5,7},{6,4},{7,5},{8,10},{9,11},{10,... | collective-permute-start | bytes 196616 | tf_op jit(solution)/shard_map/ppermute | solution.py:108
  69.7 5.0 %collective-permute-start.37 = (bf16[256,128]{1,0:T(8,128)(2,1)S(1)}, bf16[256,128]{1,0:T(8,128)(2,1)S(1)}, u32[]{:S(2)}, u32[]{:S(2)}) collective-permute-start(bf16[256,128]{1,0:T(8,128)(2,1)S(1)} %get-tuple-element.36.refs_0_), channel_id=1, source_target_pairs={{0,4},{1,5},{2,6},{3,7},{4,0},{5,1},{6,2},{7,3},{8,12},{9,13},{10,... | collective-permute-start | bytes 196616 | tf_op jit(solution)/shard_map/ppermute | solution.py:108
  71.2 6.8 %collective-permute-start.38 = (bf16[256,128]{1,0:T(8,128)(2,1)S(1)}, bf16[256,128]{1,0:T(8,128)(2,1)S(1)}, u32[]{:S(2)}, u32[]{:S(2)}) collective-permute-start(bf16[256,128]{1,0:T(8,128)(2,1)S(1)} %get-tuple-element.36.refs_0_), channel_id=1, source_target_pairs={{0,6},{1,7},{2,4},{3,5},{4,2},{5,3},{6,0},{7,1},{8,14},{9,15},{10,... | collective-permute-start | bytes 196616 | tf_op jit(solution)/shard_map/ppermute | solution.py:108
  73.6 4.3 %collective-permute-start.50 = (f32[128,128]{1,0:T(8,128)S(1)}, f32[128,128]{1,0:T(8,128)S(1)}, u32[]{:S(2)}, u32[]{:S(2)}) collective-permute-start(f32[128,128]{1,0:T(8,128)S(1)} %add.37), channel_id=1, source_target_pairs={{0,2},{1,3},{2,0},{3,1},{4,6},{5,7},{6,4},{7,5},{8,10},{9,11},{10,... | collective-permute-start | bytes 196616 | tf_op jit(solution)/shard_map/ppermute | solution.py:159
  74.2 4.5 %collective-permute-start.39 = (bf16[256,128]{1,0:T(8,128)(2,1)S(1)}, bf16[256,128]{1,0:T(8,128)(2,1)S(1)}, u32[]{:S(2)}, u32[]{:S(2)}) collective-permute-start(bf16[256,128]{1,0:T(8,128)(2,1)S(1)} %get-tuple-element.36.refs_0_), channel_id=1, source_target_pairs={{0,1},{1,0},{2,3},{3,2},{4,5},{5,4},{6,7},{7,6},{8,9},{9,8},{10,11... | collective-permute-start | bytes 196616 | tf_op jit(solution)/shard_map/ppermute | solution.py:108
  74.6 5.2 %collective-permute-start.40 = (bf16[256,128]{1,0:T(8,128)(2,1)S(1)}, bf16[256,128]{1,0:T(8,128)(2,1)S(1)}, u32[]{:S(2)}, u32[]{:S(2)}) collective-permute-start(bf16[256,128]{1,0:T(8,128)(2,1)S(1)} %collective-permute-done.36.refs_1_), channel_id=1, source_target_pairs={{0,1},{1,0},{2,3},{3,2},{4,5},{5,4},{6,7},{7,6},{8,9},{9,8},{10,11... | collective-permute-start | bytes 196616 | tf_op jit(solution)/shard_map/ppermute | solution.py:108
  77.9 4.6 %collective-permute-start.41 = (bf16[256,128]{1,0:T(8,128)(2,1)S(1)}, bf16[256,128]{1,0:T(8,128)(2,1)S(1)}, u32[]{:S(2)}, u32[]{:S(2)}) collective-permute-start(bf16[256,128]{1,0:T(8,128)(2,1)S(1)} %collective-permute-done.37.refs_2_), channel_id=1, source_target_pairs={{0,1},{1,0},{2,3},{3,2},{4,5},{5,4},{6,7},{7,6},{8,9},{9,8},{10,11... | collective-permute-start | bytes 196616 | tf_op jit(solution)/shard_map/ppermute | solution.py:108
  77.9 4.6 %collective-permute-start.51 = (f32[128,128]{1,0:T(8,128)S(1)}, f32[128,128]{1,0:T(8,128)S(1)}, u32[]{:S(2)}, u32[]{:S(2)}) collective-permute-start(f32[128,128]{1,0:T(8,128)S(1)} %add.38), channel_id=1, source_target_pairs={{0,8},{1,9},{2,10},{3,11},{4,12},{5,13},{6,14},{7,15},{8,0},{9,1},... | collective-permute-start | bytes 196616 | tf_op jit(solution)/shard_map/ppermute | solution.py:159
  78.0 13.1 %collective-permute-start.34 = (bf16[768,128]{1,0:T(8,128)(2,1)S(1)}, bf16[768,128]{1,0:T(8,128)(2,1)S(1)}, u32[]{:S(2)}, u32[]{:S(2)}) collective-permute-start(bf16[768,128]{1,0:T(8,128)(2,1)S(1)} %constant_dynamic-update-slice_fusion.7.refs_4_), channel_id=1, source_target_pairs={{0,2},{1,3},{2,0},{3,1},{4,6},{5,7},{6,4},{7,5},{8,10},{9,11},{10,... | collective-permute-start | bytes 589832 | tf_op jit(solution)/shard_map/ppermute | solution.py:108
  78.7 12.4 %collective-permute-start.30 = (bf16[768,128]{1,0:T(8,128)(2,1)S(1)}, bf16[768,128]{1,0:T(8,128)(2,1)S(1)}, u32[]{:S(2)}, u32[]{:S(2)}) collective-permute-start(bf16[768,128]{1,0:T(8,128)(2,1)S(1)} %constant_dynamic-update-slice_fusion.7.refs_4_), channel_id=1, source_target_pairs={{0,4},{1,5},{2,6},{3,7},{4,0},{5,1},{6,2},{7,3},{8,12},{9,13},{10,... | collective-permute-start | bytes 589832 | tf_op jit(solution)/shard_map/ppermute | solution.py:108
  79.9 11.8 %collective-permute-start.31 = (bf16[768,128]{1,0:T(8,128)(2,1)S(1)}, bf16[768,128]{1,0:T(8,128)(2,1)S(1)}, u32[]{:S(2)}, u32[]{:S(2)}) collective-permute-start(bf16[768,128]{1,0:T(8,128)(2,1)S(1)} %constant_dynamic-update-slice_fusion.7.refs_4_), channel_id=1, source_target_pairs={{0,6},{1,7},{2,4},{3,5},{4,2},{5,3},{6,0},{7,1},{8,14},{9,15},{10,... | collective-permute-start | bytes 589832 | tf_op jit(solution)/shard_map/ppermute | solution.py:108
  82.5 9.3 %collective-permute-start.43 = (bf16[768,128]{1,0:T(8,128)(2,1)S(1)}, bf16[768,128]{1,0:T(8,128)(2,1)S(1)}, u32[]{:S(2)}, u32[]{:S(2)}) collective-permute-start(bf16[768,128]{1,0:T(8,128)(2,1)S(1)} %constant_dynamic-update-slice_fusion.7.refs_4_), channel_id=1, source_target_pairs={{0,1},{1,0},{2,3},{3,2},{4,5},{5,4},{6,7},{7,6},{8,9},{9,8},{10,11... | collective-permute-start | bytes 589832 | tf_op jit(solution)/shard_map/ppermute | solution.py:108
  82.5 6.9 %collective-permute-start.52 = (f32[128,128]{1,0:T(8,128)S(1)}, f32[128,128]{1,0:T(8,128)S(1)}, u32[]{:S(2)}, u32[]{:S(2)}) collective-permute-start(f32[128,128]{1,0:T(8,128)S(1)} %add.39), channel_id=1, source_target_pairs={{0,16},{1,17},{2,18},{3,19},{4,20},{5,21},{6,22},{7,23},{8,24},{9,... | collective-permute-start | bytes 196616 | tf_op jit(solution)/shard_map/ppermute | solution.py:159
  90.7 8.5 %collective-permute-start.53 = (f32[128,128]{1,0:T(8,128)S(1)}, f32[128,128]{1,0:T(8,128)S(1)}, u32[]{:S(2)}, u32[]{:S(2)}) collective-permute-start(f32[128,128]{1,0:T(8,128)S(1)} %add.40), channel_id=1, source_target_pairs={{0,4},{1,5},{2,6},{3,7},{4,0},{5,1},{6,2},{7,3},{8,12},{9,13},{10,... | collective-permute-start | bytes 196616 | tf_op jit(solution)/shard_map/ppermute | solution.py:159
  91.2 3.7 %collective-permute-start.32 = (bf16[768,128]{1,0:T(8,128)(2,1)S(1)}, bf16[768,128]{1,0:T(8,128)(2,1)S(1)}, u32[]{:S(2)}, u32[]{:S(2)}) collective-permute-start(bf16[768,128]{1,0:T(8,128)(2,1)S(1)} %collective-permute-done.30.refs_0_), channel_id=1, source_target_pairs={{0,1},{1,0},{2,3},{3,2},{4,5},{5,4},{6,7},{7,6},{8,9},{9,8},{10,11... | collective-permute-start | bytes 589832 | tf_op jit(solution)/shard_map/ppermute | solution.py:108
  91.7 3.2 %collective-permute-start.33 = (bf16[768,128]{1,0:T(8,128)(2,1)S(1)}, bf16[768,128]{1,0:T(8,128)(2,1)S(1)}, u32[]{:S(2)}, u32[]{:S(2)}) collective-permute-start(bf16[768,128]{1,0:T(8,128)(2,1)S(1)} %collective-permute-done.31.refs_1_), channel_id=1, source_target_pairs={{0,1},{1,0},{2,3},{3,2},{4,5},{5,4},{6,7},{7,6},{8,9},{9,8},{10,11... | collective-permute-start | bytes 589832 | tf_op jit(solution)/shard_map/ppermute | solution.py:108
  100.0 3.9 %collective-permute-start.45 = (f32[64,64]{1,0:T(8,128)S(1)}, f32[64,64]{1,0:T(8,128)S(1)}, u32[]{:S(2)}, u32[]{:S(2)}) collective-permute-start(f32[64,64]{1,0:T(8,128)S(1)} %add.32), channel_id=1, source_target_pairs={{0,2},{1,3},{2,0},{3,1},{4,6},{5,7},{6,4},{7,5},{8,10},{9,11},{10,... | collective-permute-start | bytes 49160 | tf_op jit(solution)/shard_map/ppermute | solution.py:159
  103.9 3.9 %collective-permute-start.46 = (f32[64,64]{1,0:T(8,128)S(1)}, f32[64,64]{1,0:T(8,128)S(1)}, u32[]{:S(2)}, u32[]{:S(2)}) collective-permute-start(f32[64,64]{1,0:T(8,128)S(1)} %add.33), channel_id=1, source_target_pairs={{0,8},{1,9},{2,10},{3,11},{4,12},{5,13},{6,14},{7,15},{8,0},{9,1},... | collective-permute-start | bytes 49160 | tf_op jit(solution)/shard_map/ppermute | solution.py:159
  107.8 5.5 %collective-permute-start.47 = (f32[64,64]{1,0:T(8,128)S(1)}, f32[64,64]{1,0:T(8,128)S(1)}, u32[]{:S(2)}, u32[]{:S(2)}) collective-permute-start(f32[64,64]{1,0:T(8,128)S(1)} %add.34), channel_id=1, source_target_pairs={{0,16},{1,17},{2,18},{3,19},{4,20},{5,21},{6,22},{7,23},{8,24},{9,... | collective-permute-start | bytes 49160 | tf_op jit(solution)/shard_map/ppermute | solution.py:159
  113.4 4.2 %collective-permute-start.48 = (f32[64,64]{1,0:T(8,128)S(1)}, f32[64,64]{1,0:T(8,128)S(1)}, u32[]{:S(2)}, u32[]{:S(2)}) collective-permute-start(f32[64,64]{1,0:T(8,128)S(1)} %add.35), channel_id=1, source_target_pairs={{0,4},{1,5},{2,6},{3,7},{4,0},{5,1},{6,2},{7,3},{8,12},{9,13},{10,... | collective-permute-start | bytes 49160 | tf_op jit(solution)/shard_map/ppermute | solution.py:159
  (14 other events, 59.3 us)
where the time goes:
time: 119 us
  starting transfers between devices  48.2 us (41%)
  waiting for transfers between devices  37 us (31%)
  Pallas kernels  30.4 us (26%)
  local copies, waits for them, and re-layouts  2.57 us (2%)
    ppermute x44, starting transfers between devices, permute(): return lax.ppermute(value, AXES, pairs)  39.3 us
    pallas_call x14, Pallas kernels, call(): pl.pallas_call(kernel, in_specs=[spec for _, spec in inputs], out_shape=o...  30.4 us
    ppermute x44, waiting for transfers between devices, permute(): return lax.ppermute(value, AXES, pairs)  26.3 us
    ppermute x10, waiting for transfers between devices, exchange(): return lax.ppermute(value, AXES, pairs)  10.8 us
    ppermute x10, starting transfers between devices, exchange(): return lax.ppermute(value, AXES, pairs)  8.84 us
    unnamed x23, local copies, waits for them, and re-layouts  2.53 us
  transfers between devices with their start and end apart: 54, of which 13 were waited for; matrix products, arithmetic and copies ran while one was open for 0% of the time, Pallas kernels for 21%

commit v1 on v0

--- a/solution.py
+++ b/solution.py
@@ -214,7 +214,7 @@
     for p in range(points):
         u = times(turned[:, p * band : (p + 1) * band], correlation[p], True)
         payload[pl.ds(p * columns, columns), :] = u.astype(jnp.bfloat16)
-    lane = lax.broadcasted_iota(jnp.int32, (16, band), 1)
+    lane = lax.rem(lax.broadcasted_iota(jnp.int32, (16, band), 1), points)
     value = jnp.zeros((16, band), jnp.float32)
     for p in range(points):
         value = jnp.where(lane == p, neighbor[p].astype(jnp.float32), value)
@@ -239,7 +239,7 @@
 
 
 def weigh_kernel(geometry, pieces, block_rows, with_neighbors, continued, *refs):
-    dims, points, columns = geometry.dims, geometry.points, geometry.columns
+    dims, points, columns, band = geometry.dims, geometry.points, geometry.columns, geometry.band
     nz, ny, nx, nc = dims
     n = len(pieces)
     starts = [sum(p[4] - p[3] for p in pieces[:k]) for k in range(n)]
@@ -249,11 +249,17 @@
         before, refs = refs[:2], refs[2:]
     if with_neighbors:
         acc_0, acc_1, nbs_out, nbv, nbs, sem = refs
+        per = band // points
+        lane = lax.broadcasted_iota(jnp.int32, (16, band), 1) // points
+        rows = [jnp.zeros((16, band), jnp.float32) for _ in range(nbv.shape[0])]
         for index, piece in enumerate(pieces):
             for line in range(piece[4] - piece[3]):
                 at = line * block_rows + points * columns
                 tile = u_refs[index][pl.ds(at, 16), :].astype(jnp.float32)
-                nbv[pl.ds(starts[index] + line, 1), :] = tile[0:1].astype(jnp.int32)
+                k = starts[index] + line
+                rows[k // per] = jnp.where(lane == k % per, tile, rows[k // per])
+        for k, row in enumerate(rows):
+            nbv[pl.ds(k, 1), :] = row[0:1].astype(jnp.int32)
         copy = pltpu.make_async_copy(nbv, nbs, sem)
         copy.start()
         nbs_out[...] = nbv[...]
@@ -265,7 +271,7 @@
     if with_neighbors:
         copy.wait()
     z, y, x, c = place(geometry)
-    col = lax.axis_index("col")
+    per = band // points
     for index, ref in enumerate(u_refs):
         dy, dx, dc, lo, hi = pieces[index]
 
@@ -277,10 +283,11 @@
             for q in range(points):
                 base = pl.multiple_of(line * block_rows + q * columns, 16)
                 u = ref[pl.ds(base, columns), :].astype(jnp.float32)
-                j = nbs[starts[index] + line, q]
+                k = starts[index] + line
+                j = nbs[k // per, lax.rem(k, per) * points + q]
                 acc = sums[q % 2]
                 for p in range(points):
-                    w = weight[col * points + p, device * points + q]
+                    w = weight[p, device * points + q]
                     acc[j, p] += w * u
             return carry
 
@@ -328,10 +335,10 @@
     return times(total, correlation[p], False)
 
 
-def first_image_kernel(geometry, pieces, count, *refs):
+def first_image_kernel(geometry, pieces, *refs):
     n = len(pieces)
     coarse_refs = refs[:n]
-    (acc_0, acc_1, own, correlation, turned, energy, chosen, payload, image, grams) = refs[n:]
+    (acc_0, acc_1, own, correlation, turned, energy, chosen, payload, image) = refs[n:]
     columns, band = geometry.columns, geometry.band
     choose_blocks(geometry, pieces, coarse_refs, own, chosen)
     for p in range(geometry.points):
@@ -341,6 +348,9 @@
         payload[pl.ds(p * columns, columns), :] = times(value, correlation[p], True).astype(
             jnp.bfloat16
         )
+
+
+def gram_kernel(count, turned, image, grams):
     pair = jnp.concatenate([turned[...], image[...]])
     grams[...] = nt(pair, pair) * (1.0 / count)
 
@@ -462,7 +472,8 @@
         inputs += [(b, VMEM) for b in before]
     outputs = [shaped(shape), shaped(shape)]
     scratch = []
-    count = sum(piece[4] - piece[3] for piece in pieces)
+    blocks = sum(piece[4] - piece[3] for piece in pieces)
+    count = pl.cdiv(blocks, geometry.band // geometry.points)
     if neighbors is None:
         outputs.append(shaped((count, geometry.band), jnp.int32))
         scratch = [
@@ -489,7 +500,7 @@
     rows, cols = lax.axis_size("row"), lax.axis_size("col")
     points, band, _ = correlations.shape
     columns = start_block.shape[1]
-    if rows % 2 or cols % 2 or coarse_kernel.shape[0] % band or coarse_kernel.shape[1] % band:
+    if rows % 2 or cols % 2 or coarse_kernel.shape[0] % band or coarse_kernel.shape[1] % band or band % points:
         return general_form(
             coarse_kernel, correlations, neighbor, pair_weight, energies, start_block
         )
@@ -503,6 +514,9 @@
     count = float(start_block.shape[0] * rows * cols)
     half = points * columns
     turned = start_block.T
+    own_weight = lax.dynamic_slice_in_dim(
+        pair_weight, lax.axis_index("col") * points, points, axis=0
+    )
     (payload,) = call(
         functools.partial(first_kernel, points),
         [(neighbor, SMEM), (turned, VMEM), (correlations, VMEM)],
@@ -526,22 +540,27 @@
     for group in groups:
         acc, found = weigh(
             geometry, [u[k] for k in group], [pieces[k] for k in group], half + 16,
-            pair_weight, None, acc,
+            own_weight, None, acc,
         )
         neighbors.append(found[0])
     own = neighbors[0][0, :points]
     coarse_count = geometry.coarse_count
-    chosen, payload, first, joint = call(
-        functools.partial(first_image_kernel, geometry, coarse_pieces, count),
+    chosen, payload, first = call(
+        functools.partial(first_image_kernel, geometry, coarse_pieces),
         [(a, VMEM) for a in coarse]
         + [(acc[0], VMEM), (acc[1], VMEM), (own, SMEM), (correlations, VMEM), (turned, VMEM), (shifted, VMEM)],
         [
             shaped((points, coarse_count, band, band), jnp.bfloat16),
             shaped((half, band), jnp.bfloat16),
             shaped(turned.shape),
-            shaped((2 * columns, 2 * columns)),
         ],
         work=3.0,
+    )
+    (joint,) = call(
+        functools.partial(gram_kernel, count),
+        [(turned, VMEM), (first, VMEM)],
+        [shaped((2 * columns, 2 * columns))],
+        work=1.0,
     )
     u, _ = gather_everywhere(payload, dims, apart)
     joint = sum_everywhere(joint, dims)
@@ -549,7 +568,7 @@
     for group, found in zip(groups, neighbors):
         acc, _ = weigh(
             geometry, [u[k] for k in group], [pieces[k] for k in group], half,
-            pair_weight, found, acc,
+            own_weight, found, acc,
         )
     second, g12 = call(
         functools.partial(second_image_kernel, geometry, count),

time: 119 us -> 114 us (0.958)
  waiting for transfers between devices: 37 us -> 32.4 us
    ppermute x44, waiting for transfers between devices: 26.3 us -> 23.4 us  [permute(): return lax.ppermute(value, AXES, pairs)]
    ppermute x44, starting transfers between devices: 39.3 us -> 36.7 us  [permute(): return lax.ppermute(value, AXES, pairs)]
    ppermute x10, starting transfers between devices: 8.84 us -> 10.8 us  [exchange(): return lax.ppermute(value, AXES, pairs)]
    ppermute x10, waiting for transfers between devices: 10.8 us -> 9.05 us  [exchange(): return lax.ppermute(value, AXES, pairs)]
    pallas_call x14 -> x15, Pallas kernels: 30.4 us -> 29.4 us  [call(): pl.pallas_call(kernel, in_specs=[spec for _, spec in inputs], out_shape=o...]
  transfers between devices with their start and end apart: 54 -> 54, of which waited for: 13 -> 15; matrix products, arithmetic and copies ran while one was open for 0% -> 0% of each run, Pallas kernels for 21% -> 21%
where the time goes in v1:
time: 114 us
  starting transfers between devices  47.5 us (42%)
  waiting for transfers between devices  32.4 us (28%)
  Pallas kernels  29.4 us (26%)
  local copies, waits for them, and re-layouts  3.26 us (3%)
    ppermute x44, starting transfers between devices, permute(): return lax.ppermute(value, AXES, pairs)  36.7 us
    pallas_call x15, Pallas kernels, call(): pl.pallas_call(kernel, in_specs=[spec for _, spec in inputs], out_shape=o...  29.4 us
    ppermute x44, waiting for transfers between devices, permute(): return lax.ppermute(value, AXES, pairs)  23.4 us
    ppermute x10, starting transfers between devices, exchange(): return lax.ppermute(value, AXES, pairs)  10.8 us
    ppermute x10, waiting for transfers between devices, exchange(): return lax.ppermute(value, AXES, pairs)  9.05 us
    unnamed x23, local copies, waits for them, and re-layouts  3.22 us
  transfers between devices with their start and end apart: 54, of which 15 were waited for; matrix products, arithmetic and copies ran while one was open for 0% of the time, Pallas kernels for 21%

profile of v1, /device:TPU:0, one launch (start us, length us, event | category | flops | bytes accessed | tf_op | source)
XLA Modules:
  0.0 113.7 jit_solution(1025763803670418041)
XLA Ops:
  1.3 0.9 copy-done.1
  2.2 0.9 copy-done.3
  3.8 3.1 %collective-permute-start.10 = (bf16[272,128]{1,0:T(8,128)(2,1)S(1)}, bf16[272,128]{1,0:T(8,128)(2,1)S(1)}, u32[]{:S(2)}, u32[]{:S(2)}) collective-permute-start(bf16[272,128]{1,0:T(8,128)(2,1)S(1)} %shard_map.77.refs_0_), channel_id=1, source_target_pairs={{0,8},{1,9},{2,10},{3,11},{4,12},{5,13},{6,14},{7,15},{8,16},{9,17... | collective-permute-start | bytes 208904 | tf_op jit(solution)/shard_map/ppermute | solution.py:108
  7.0 2.1 %collective-permute-start.11 = (bf16[272,128]{1,0:T(8,128)(2,1)S(1)}, bf16[272,128]{1,0:T(8,128)(2,1)S(1)}, u32[]{:S(2)}, u32[]{:S(2)}) collective-permute-start(bf16[272,128]{1,0:T(8,128)(2,1)S(1)} %shard_map.77.refs_0_), channel_id=1, source_target_pairs={{0,24},{1,25},{2,26},{3,27},{4,28},{5,29},{6,30},{7,31},{8,0},{9,1... | collective-permute-start | bytes 208904 | tf_op jit(solution)/shard_map/ppermute | solution.py:108
  9.1 0.9 collective-permute-start.12
  10.0 1.5 %collective-permute-start.19 = (bf16[272,128]{1,0:T(8,128)(2,1)S(1)}, bf16[272,128]{1,0:T(8,128)(2,1)S(1)}, u32[]{:S(2)}, u32[]{:S(2)}) collective-permute-start(bf16[272,128]{1,0:T(8,128)(2,1)S(1)} %shard_map.77.refs_0_), channel_id=1, source_target_pairs={{0,2},{1,3},{2,0},{3,1},{4,6},{5,7},{6,4},{7,5},{8,10},{9,11},{10,... | collective-permute-start | bytes 208904 | tf_op jit(solution)/shard_map/ppermute | solution.py:108
  11.5 1.6 %collective-permute-start = (bf16[128,256]{1,0:T(8,128)(2,1)S(1)}, bf16[128,256]{1,0:T(8,128)(2,1)S(1)}, u32[]{:S(2)}, u32[]{:S(2)}) collective-permute-start(bf16[128,256]{1,0:T(8,128)(2,1)S(1)} %copy-done.6), channel_id=1, source_target_pairs={{0,8},{1,9},{2,10},{3,11},{4,12},{5,13},{6,14},{7,15},{8,16},{9,17... | collective-permute-start | bytes 196616 | tf_op jit(solution)/shard_map/ppermute | solution.py:108
  13.8 3.8 %collective-permute-done = bf16[128,256]{1,0:T(8,128)(2,1)S(1)} collective-permute-done((bf16[128,256]{1,0:T(8,128)(2,1)S(1)}, bf16[128,256]{1,0:T(8,128)(2,1)S(1)}, u32[]{:S(2)}, u32[]{:S(2)}) %collective-permute-start) | collective-permute-done | bytes 65568 | tf_op jit(solution)/shard_map/ppermute | solution.py:108
  17.6 1.5 %collective-permute-start.20 = (bf16[272,128]{1,0:T(8,128)(2,1)S(1)}, bf16[272,128]{1,0:T(8,128)(2,1)S(1)}, u32[]{:S(2)}, u32[]{:S(2)}) collective-permute-start(bf16[272,128]{1,0:T(8,128)(2,1)S(1)} %shard_map.77.refs_0_), channel_id=1, source_target_pairs={{0,4},{1,5},{2,6},{3,7},{4,0},{5,1},{6,2},{7,3},{8,12},{9,13},{10,... | collective-permute-start | bytes 208904 | tf_op jit(solution)/shard_map/ppermute | solution.py:108
  20.2 1.3 %collective-permute-start.2 = (bf16[128,256]{1,0:T(8,128)(2,1)S(1)}, bf16[128,256]{1,0:T(8,128)(2,1)S(1)}, u32[]{:S(2)}, u32[]{:S(2)}) collective-permute-start(bf16[128,256]{1,0:T(8,128)(2,1)S(1)} %copy-done.6), channel_id=1, source_target_pairs={{0,16},{1,17},{2,18},{3,19},{4,20},{5,21},{6,22},{7,23},{8,24},{9,... | collective-permute-start | bytes 196616 | tf_op jit(solution)/shard_map/ppermute | solution.py:108
  21.5 2.6 %collective-permute-done.1 = bf16[128,256]{1,0:T(8,128)(2,1)S(1)} collective-permute-done((bf16[128,256]{1,0:T(8,128)(2,1)S(1)}, bf16[128,256]{1,0:T(8,128)(2,1)S(1)}, u32[]{:S(2)}, u32[]{:S(2)}) %collective-permute-start.1) | collective-permute-done | bytes 65568 | tf_op jit(solution)/shard_map/ppermute | solution.py:108
  24.1 1.3 %collective-permute-done.2 = bf16[128,256]{1,0:T(8,128)(2,1)S(1)} collective-permute-done((bf16[128,256]{1,0:T(8,128)(2,1)S(1)}, bf16[128,256]{1,0:T(8,128)(2,1)S(1)}, u32[]{:S(2)}, u32[]{:S(2)}) %collective-permute-start.2) | collective-permute-done | bytes 65568 | tf_op jit(solution)/shard_map/ppermute | solution.py:108
  25.4 2.6 %collective-permute-start.17 = (bf16[816,128]{1,0:T(8,128)(2,1)S(1)}, bf16[816,128]{1,0:T(8,128)(2,1)S(1)}, u32[]{:S(2)}, u32[]{:S(2)}) collective-permute-start(bf16[816,128]{1,0:T(8,128)(2,1)S(1)} %constant_dynamic-update-slice_fusion.4.refs_4_), channel_id=1, source_target_pairs={{0,2},{1,3},{2,0},{3,1},{4,6},{5,7},{6,4},{7,5},{8,10},{9,11},{10,... | collective-permute-start | bytes 626696 | tf_op jit(solution)/shard_map/ppermute | solution.py:108
  28.6 1.6 %collective-permute-start.13 = (bf16[816,128]{1,0:T(8,128)(2,1)S(1)}, bf16[816,128]{1,0:T(8,128)(2,1)S(1)}, u32[]{:S(2)}, u32[]{:S(2)}) collective-permute-start(bf16[816,128]{1,0:T(8,128)(2,1)S(1)} %constant_dynamic-update-slice_fusion.4.refs_4_), channel_id=1, source_target_pairs={{0,4},{1,5},{2,6},{3,7},{4,0},{5,1},{6,2},{7,3},{8,12},{9,13},{10,... | collective-permute-start | bytes 626696 | tf_op jit(solution)/shard_map/ppermute | solution.py:108
  30.6 1.2 %collective-permute-done.25.refs_8_ = bf16[272,128]{1,0:T(8,128)(2,1)S(1)} collective-permute-done((bf16[272,128]{1,0:T(8,128)(2,1)S(1)}, bf16[272,128]{1,0:T(8,128)(2,1)S(1)}, u32[]{:S(2)}, u32[]{:S(2)}) %collective-permute-start.25) | collective-permute-done | bytes 69664 | tf_op jit(solution)/shard_map/ppermute | solution.py:108
  31.8 1.7 %collective-permute-start.3 = (bf16[512,256]{1,0:T(8,128)(2,1)S(1)}, bf16[512,256]{1,0:T(8,128)(2,1)S(1)}, u32[]{:S(2)}, u32[]{:S(2)}) collective-permute-start(bf16[512,256]{1,0:T(8,128)(2,1)S(1)} %constant_dynamic-update-slice_fusion.refs_0_), channel_id=1, source_target_pairs={{0,2},{1,3},{2,0},{3,1},{4,6},{5,7},{6,4},{7,5},{8,10},{9,11},{10,... | collective-permute-start | bytes 786440 | tf_op jit(solution)/shard_map/ppermute | solution.py:108
  33.6 1.4 %collective-permute-start.4 = (bf16[512,256]{1,0:T(8,128)(2,1)S(1)}, bf16[512,256]{1,0:T(8,128)(2,1)S(1)}, u32[]{:S(2)}, u32[]{:S(2)}) collective-permute-start(bf16[512,256]{1,0:T(8,128)(2,1)S(1)} %constant_dynamic-update-slice_fusion.refs_0_), channel_id=1, source_target_pairs={{0,4},{1,5},{2,6},{3,7},{4,0},{5,1},{6,2},{7,3},{8,12},{9,13},{10,... | collective-permute-start | bytes 786440 | tf_op jit(solution)/shard_map/ppermute | solution.py:108
  34.9 2.1 %collective-permute-start.5 = (bf16[512,256]{1,0:T(8,128)(2,1)S(1)}, bf16[512,256]{1,0:T(8,128)(2,1)S(1)}, u32[]{:S(2)}, u32[]{:S(2)}) collective-permute-start(bf16[512,256]{1,0:T(8,128)(2,1)S(1)} %constant_dynamic-update-slice_fusion.refs_0_), channel_id=1, source_target_pairs={{0,6},{1,7},{2,4},{3,5},{4,2},{5,3},{6,0},{7,1},{8,14},{9,15},{10,... | collective-permute-start | bytes 786440 | tf_op jit(solution)/shard_map/ppermute | solution.py:108
  37.1 4.1 %collective-permute-done.13.refs_0_ = bf16[816,128]{1,0:T(8,128)(2,1)S(1)} collective-permute-done((bf16[816,128]{1,0:T(8,128)(2,1)S(1)}, bf16[816,128]{1,0:T(8,128)(2,1)S(1)}, u32[]{:S(2)}, u32[]{:S(2)}) %collective-permute-start.13) | collective-permute-done | bytes 208928 | tf_op jit(solution)/shard_map/ppermute | solution.py:108
  41.7 2.0 %shard_map.78 = (f32[8,4,64,128]{3,2,1,0:T(8,128)S(1)}, f32[8,4,64,128]{3,2,1,0:T(8,128)S(1)}, s32[1,128]{1,0:T(1,128)S(1)}) custom-call(bf16[272,128]{1,0:T(8,128)(2,1)S(1)} %shard_map.77.refs_0_, bf16[272,128]{1,0:T(8,128)(2,1)S(1)} %collective-permute-done.19.refs_1_, bf16[272,128]{1,0:T(8,128)(2,1)S(1)} %collective-permute-done.20.refs_2_, ...), custom_call_target="tpu_custom_call" | custom-call | flops 2500000000 | tf_op jit(solution)/shard_map/pallas_call | solution.py:453
  44.2 7.4 %collective-permute-done.4.refs_2_ = bf16[512,256]{1,0:T(8,128)(2,1)S(1)} collective-permute-done((bf16[512,256]{1,0:T(8,128)(2,1)S(1)}, bf16[512,256]{1,0:T(8,128)(2,1)S(1)}, u32[]{:S(2)}, u32[]{:S(2)}) %collective-permute-start.4) | collective-permute-done | bytes 262176 | tf_op jit(solution)/shard_map/ppermute | solution.py:108
  52.7 1.5 %shard_map.79 = (f32[8,4,64,128]{3,2,1,0:T(8,128)S(1)}, f32[8,4,64,128]{3,2,1,0:T(8,128)S(1)}, s32[1,128]{1,0:T(1,128)S(1)}) custom-call(bf16[816,128]{1,0:T(8,128)(2,1)S(1)} %collective-permute-done.17.refs_0_, bf16[816,128]{1,0:T(8,128)(2,1)S(1)} %collective-permute-done.18.refs_1_, ...), custom_call_target="tpu_custom_call", output_to_operand_aliasing={{0}: (3, {}), {1}: (4, {})} | custom-call | flops 500000000 | tf_op jit(solution)/shard_map/pallas_call | solution.py:453
  54.3 1.9 %shard_map.80 = (f32[8,4,64,128]{3,2,1,0:T(8,128)S(1)}, f32[8,4,64,128]{3,2,1,0:T(8,128)S(1)}, s32[1,128]{1,0:T(1,128)S(1)}) custom-call(bf16[816,128]{1,0:T(8,128)(2,1)S(1)} %collective-permute-done.13.refs_0_, bf16[816,128]{1,0:T(8,128)(2,1)S(1)} %collective-permute-done.14.refs_1_, ...), custom_call_target="tpu_custom_call", output_to_operand_aliasing={{0}: (5, {}), {1}: (6, {})} | custom-call | flops 1000000000 | tf_op jit(solution)/shard_map/pallas_call | solution.py:453
  56.3 3.0 %shard_map.81 = (bf16[4,8,128,128]{3,2,1,0:T(8,128)(2,1)S(1)}, bf16[256,128]{1,0:T(8,128)(2,1)S(1)}, f32[64,512]{1,0:T(8,128)S(1)}) custom-call(bf16[512,256]{1,0:T(8,128)(2,1)S(1)} %constant_dynamic-update-slice_fusion.refs_0_, bf16[512,256]{1,0:T(8,128)(2,1)S(1)} %collective-permute-done.3.refs_1_, bf16[512,256]{1,0:T(8,128)(2,1)S(1)} %collective-permute-done.4.refs_2_, ...), custom_call_target="tpu_custom_call" | custom-call | flops 1500000000 | tf_op jit(solution)/shard_map/pallas_call | solution.py:453
  60.3 3.3 %collective-permute-start.28 = (bf16[256,128]{1,0:T(8,128)(2,1)S(1)}, bf16[256,128]{1,0:T(8,128)(2,1)S(1)}, u32[]{:S(2)}, u32[]{:S(2)}) collective-permute-start(bf16[256,128]{1,0:T(8,128)(2,1)S(1)} %get-tuple-element.35.refs_0_), channel_id=1, source_target_pairs={{0,24},{1,25},{2,26},{3,27},{4,28},{5,29},{6,30},{7,31},{8,0},{9,1... | collective-permute-start | bytes 196616 | tf_op jit(solution)/shard_map/ppermute | solution.py:108
  64.2 1.3 %collective-permute-start.37 = (bf16[256,128]{1,0:T(8,128)(2,1)S(1)}, bf16[256,128]{1,0:T(8,128)(2,1)S(1)}, u32[]{:S(2)}, u32[]{:S(2)}) collective-permute-start(bf16[256,128]{1,0:T(8,128)(2,1)S(1)} %get-tuple-element.35.refs_0_), channel_id=1, source_target_pairs={{0,4},{1,5},{2,6},{3,7},{4,0},{5,1},{6,2},{7,3},{8,12},{9,13},{10,... | collective-permute-start | bytes 196616 | tf_op jit(solution)/shard_map/ppermute | solution.py:108
  65.5 1.0 collective-permute-done.27
  66.6 1.3 %collective-permute-start.38 = (bf16[256,128]{1,0:T(8,128)(2,1)S(1)}, bf16[256,128]{1,0:T(8,128)(2,1)S(1)}, u32[]{:S(2)}, u32[]{:S(2)}) collective-permute-start(bf16[256,128]{1,0:T(8,128)(2,1)S(1)} %get-tuple-element.35.refs_0_), channel_id=1, source_target_pairs={{0,6},{1,7},{2,4},{3,5},{4,2},{5,3},{6,0},{7,1},{8,14},{9,15},{10,... | collective-permute-start | bytes 196616 | tf_op jit(solution)/shard_map/ppermute | solution.py:108
  67.9 1.7 %collective-permute-start.50 = (f32[128,128]{1,0:T(8,128)S(1)}, f32[128,128]{1,0:T(8,128)S(1)}, u32[]{:S(2)}, u32[]{:S(2)}) collective-permute-start(f32[128,128]{1,0:T(8,128)S(1)} %add.41), channel_id=1, source_target_pairs={{0,2},{1,3},{2,0},{3,1},{4,6},{5,7},{6,4},{7,5},{8,10},{9,11},{10,... | collective-permute-start | bytes 196616 | tf_op jit(solution)/shard_map/ppermute | solution.py:159
  70.2 2.3 %collective-permute-done.50 = f32[128,128]{1,0:T(8,128)S(1)} collective-permute-done((f32[128,128]{1,0:T(8,128)S(1)}, f32[128,128]{1,0:T(8,128)S(1)}, u32[]{:S(2)}, u32[]{:S(2)}) %collective-permute-start.50) | collective-permute-done | bytes 65568 | tf_op jit(solution)/shard_map/ppermute | solution.py:159
  72.6 1.5 %collective-permute-start.34 = (bf16[768,128]{1,0:T(8,128)(2,1)S(1)}, bf16[768,128]{1,0:T(8,128)(2,1)S(1)}, u32[]{:S(2)}, u32[]{:S(2)}) collective-permute-start(bf16[768,128]{1,0:T(8,128)(2,1)S(1)} %constant_dynamic-update-slice_fusion.7.refs_4_), channel_id=1, source_target_pairs={{0,2},{1,3},{2,0},{3,1},{4,6},{5,7},{6,4},{7,5},{8,10},{9,11},{10,... | collective-permute-start | bytes 589832 | tf_op jit(solution)/shard_map/ppermute | solution.py:108
  74.8 1.4 %collective-permute-start.31 = (bf16[768,128]{1,0:T(8,128)(2,1)S(1)}, bf16[768,128]{1,0:T(8,128)(2,1)S(1)}, u32[]{:S(2)}, u32[]{:S(2)}) collective-permute-start(bf16[768,128]{1,0:T(8,128)(2,1)S(1)} %constant_dynamic-update-slice_fusion.7.refs_4_), channel_id=1, source_target_pairs={{0,6},{1,7},{2,4},{3,5},{4,2},{5,3},{6,0},{7,1},{8,14},{9,15},{10,... | collective-permute-start | bytes 589832 | tf_op jit(solution)/shard_map/ppermute | solution.py:108
  76.2 0.9 collective-permute-done.51
  77.1 2.1 %collective-permute-start.52 = (f32[128,128]{1,0:T(8,128)S(1)}, f32[128,128]{1,0:T(8,128)S(1)}, u32[]{:S(2)}, u32[]{:S(2)}) collective-permute-start(f32[128,128]{1,0:T(8,128)S(1)} %add.43), channel_id=1, source_target_pairs={{0,16},{1,17},{2,18},{3,19},{4,20},{5,21},{6,22},{7,23},{8,24},{9,... | collective-permute-start | bytes 196616 | tf_op jit(solution)/shard_map/ppermute | solution.py:159
  79.2 4.8 %collective-permute-done.52 = f32[128,128]{1,0:T(8,128)S(1)} collective-permute-done((f32[128,128]{1,0:T(8,128)S(1)}, f32[128,128]{1,0:T(8,128)S(1)}, u32[]{:S(2)}, u32[]{:S(2)}) %collective-permute-start.52) | collective-permute-done | bytes 65568 | tf_op jit(solution)/shard_map/ppermute | solution.py:159
  84.0 1.2 %collective-permute-done.42.refs_8_ = bf16[256,128]{1,0:T(8,128)(2,1)S(1)} collective-permute-done((bf16[256,128]{1,0:T(8,128)(2,1)S(1)}, bf16[256,128]{1,0:T(8,128)(2,1)S(1)}, u32[]{:S(2)}, u32[]{:S(2)}) %collective-permute-start.42) | collective-permute-done | bytes 65568 | tf_op jit(solution)/shard_map/ppermute | solution.py:108
  85.2 0.9 collective-permute-start.53
  86.7 1.5 %shard_map.82 = (f32[8,4,64,128]{3,2,1,0:T(8,128)S(1)}, f32[8,4,64,128]{3,2,1,0:T(8,128)S(1)}) custom-call(bf16[256,128]{1,0:T(8,128)(2,1)S(1)} %get-tuple-element.35.refs_0_, bf16[256,128]{1,0:T(8,128)(2,1)S(1)} %collective-permute-done.36.refs_1_, bf16[256,128]{1,0:T(8,128)(2,1)S(1)} %collective-permute-done.37.refs_2_, ...), custom_call_target="tpu_custom_call" | custom-call | flops 2500000000 | tf_op jit(solution)/shard_map/pallas_call | solution.py:453
  88.2 1.2 %shard_map.83 = (f32[8,4,64,128]{3,2,1,0:T(8,128)S(1)}, f32[8,4,64,128]{3,2,1,0:T(8,128)S(1)}) custom-call(bf16[768,128]{1,0:T(8,128)(2,1)S(1)} %collective-permute-done.34.refs_0_, bf16[768,128]{1,0:T(8,128)(2,1)S(1)} %collective-permute-done.35.refs_1_, ...), custom_call_target="tpu_custom_call", output_to_operand_aliasing={{0}: (3, {}), {1}: (4, {})} | custom-call | flops 500000000 | tf_op jit(solution)/shard_map/pallas_call | solution.py:453
  89.4 1.6 %shard_map.84 = (f32[8,4,64,128]{3,2,1,0:T(8,128)S(1)}, f32[8,4,64,128]{3,2,1,0:T(8,128)S(1)}) custom-call(bf16[768,128]{1,0:T(8,128)(2,1)S(1)} %collective-permute-done.30.refs_0_, bf16[768,128]{1,0:T(8,128)(2,1)S(1)} %collective-permute-done.31.refs_1_, ...), custom_call_target="tpu_custom_call", output_to_operand_aliasing={{0}: (5, {}), {1}: (6, {})} | custom-call | flops 1000000000 | tf_op jit(solution)/shard_map/pallas_call | solution.py:453
  91.1 1.9 %shard_map.85 = (f32[64,512]{1,0:T(8,128)S(1)}, f32[64,64]{1,0:T(8,128)S(1)}) custom-call(f32[8,4,64,128]{3,2,1,0:T(8,128)S(1)} %get-tuple-element.42.acc_0, f32[8,4,64,128]{3,2,1,0:T(8,128)S(1)} %get-tuple-element.43.acc_1, bf16[4,8,128,128]{3,2,1,0:T(8,128)(2,1)S(1)} %get-tuple-element.44.chosen, bf16[4,128,128]{2,1,0:T(8,128)(2,1)S(1)} %copy-done.2, ...), custom_call_target="tpu_custom_call" | custom-call | flops 1500000000 | tf_op jit(solution)/shard_map/pallas_call | solution.py:453
  94.4 1.0 collective-permute-start.45
  95.4 2.8 %shard_map.87.given = f32[64,192]{1,0:T(8,128)S(1)} custom-call(f32[128,128]{1,0:T(8,128)S(1)} %add.45.joint), custom_call_target="tpu_custom_call" | custom-call | flops 1500000000 | tf_op jit(solution)/shard_map/pallas_call | solution.py:453
  99.1 3.0 %shard_map.88 = (f32[64,192]{1,0:T(8,128)S(1)}, f32[64,128]{1,0:T(8,128)S(1)}) custom-call(f32[128,128]{1,0:T(8,128)S(1)} %add.45.joint, f32[64,192]{1,0:T(8,128)S(1)} %shard_map.87.given), custom_call_target="tpu_custom_call" | custom-call | flops 1500000000 | tf_op jit(solution)/shard_map/pallas_call | solution.py:453
  102.2 2.9 %collective-permute-start.47 = (f32[64,64]{1,0:T(8,128)S(1)}, f32[64,64]{1,0:T(8,128)S(1)}, u32[]{:S(2)}, u32[]{:S(2)}) collective-permute-start(f32[64,64]{1,0:T(8,128)S(1)} %add.38), channel_id=1, source_target_pairs={{0,16},{1,17},{2,18},{3,19},{4,20},{5,21},{6,22},{7,23},{8,24},{9,... | collective-permute-start | bytes 49160 | tf_op jit(solution)/shard_map/ppermute | solution.py:159
  105.2 2.7 %shard_map.89.given = f32[64,128]{1,0:T(8,128)S(1)} custom-call(f32[64,128]{1,0:T(8,128)S(1)} %get-tuple-element.48.given), custom_call_target="tpu_custom_call" | custom-call | flops 1500000000 | tf_op jit(solution)/shard_map/pallas_call | solution.py:453
  108.6 3.4 %shard_map.90 = (f32[2,64,64]{2,1,0:T(8,128)S(1)}, f32[4,64,64]{2,1,0:T(8,128)S(1)}) custom-call(f32[128,128]{1,0:T(8,128)S(1)} %add.45.joint, f32[64,192]{1,0:T(8,128)S(1)} %get-tuple-element.47.one, f32[64,128]{1,0:T(8,128)S(1)} %shard_map.89.given), custom_call_target="tpu_custom_call" | custom-call | flops 1500000000 | tf_op jit(solution)/shard_map/pallas_call | solution.py:453
  112.0 1.6 %shard_map.91 = (f32[64,512]{1,0:T(8,128)}, f32[3,64,64]{2,1,0:T(8,128)}) custom-call(f32[64,64]{1,0:T(8,128)S(1)} %add.40.refs_0_, f32[2,64,64]{2,1,0:T(8,128)S(1)} %get-tuple-element.49.refs_1_, f32[4,64,64]{2,1,0:T(8,128)S(1)} %get-tuple-element.50.refs_2_, f32[64,512]{1,0:T(8,128)S(1)} %bitcast.10, f32[64,512]{1,0:T(8,128)S(1)} %get-tuple-element.45.first.image.refs_4_, ...), custom_call_target="tpu_custom_call" | custom-call | flops 1000000000 | tf_op jit(solution)/shard_map/pallas_call | solution.py:453
  (114 shorter events, 13.0 us)
Async XLA Ops:
  3.8 15.2 %collective-permute-start.10 = (bf16[272,128]{1,0:T(8,128)(2,1)S(1)}, bf16[272,128]{1,0:T(8,128)(2,1)S(1)}, u32[]{:S(2)}, u32[]{:S(2)}) collective-permute-start(bf16[272,128]{1,0:T(8,128)(2,1)S(1)} %shard_map.77.refs_0_), channel_id=1, source_target_pairs={{0,8},{1,9},{2,10},{3,11},{4,12},{5,13},{6,14},{7,15},{8,16},{9,17... | collective-permute-start | bytes 208904 | tf_op jit(solution)/shard_map/ppermute | solution.py:108
  7.0 12.8 %collective-permute-start.11 = (bf16[272,128]{1,0:T(8,128)(2,1)S(1)}, bf16[272,128]{1,0:T(8,128)(2,1)S(1)}, u32[]{:S(2)}, u32[]{:S(2)}) collective-permute-start(bf16[272,128]{1,0:T(8,128)(2,1)S(1)} %shard_map.77.refs_0_), channel_id=1, source_target_pairs={{0,24},{1,25},{2,26},{3,27},{4,28},{5,29},{6,30},{7,31},{8,0},{9,1... | collective-permute-start | bytes 208904 | tf_op jit(solution)/shard_map/ppermute | solution.py:108
  9.1 11.1 %collective-permute-start.12 = (bf16[272,128]{1,0:T(8,128)(2,1)S(1)}, bf16[272,128]{1,0:T(8,128)(2,1)S(1)}, u32[]{:S(2)}, u32[]{:S(2)}) collective-permute-start(bf16[272,128]{1,0:T(8,128)(2,1)S(1)} %shard_map.77.refs_0_), channel_id=1, source_target_pairs={{0,16},{1,17},{2,18},{3,19},{4,20},{5,21},{6,22},{7,23},{8,24},{9,... | collective-permute-start | bytes 208904 | tf_op jit(solution)/shard_map/ppermute | solution.py:108
  10.0 15.4 %collective-permute-start.19 = (bf16[272,128]{1,0:T(8,128)(2,1)S(1)}, bf16[272,128]{1,0:T(8,128)(2,1)S(1)}, u32[]{:S(2)}, u32[]{:S(2)}) collective-permute-start(bf16[272,128]{1,0:T(8,128)(2,1)S(1)} %shard_map.77.refs_0_), channel_id=1, source_target_pairs={{0,2},{1,3},{2,0},{3,1},{4,6},{5,7},{6,4},{7,5},{8,10},{9,11},{10,... | collective-permute-start | bytes 208904 | tf_op jit(solution)/shard_map/ppermute | solution.py:108
  11.5 6.1 %collective-permute-start = (bf16[128,256]{1,0:T(8,128)(2,1)S(1)}, bf16[128,256]{1,0:T(8,128)(2,1)S(1)}, u32[]{:S(2)}, u32[]{:S(2)}) collective-permute-start(bf16[128,256]{1,0:T(8,128)(2,1)S(1)} %copy-done.6), channel_id=1, source_target_pairs={{0,8},{1,9},{2,10},{3,11},{4,12},{5,13},{6,14},{7,15},{8,16},{9,17... | collective-permute-start | bytes 196616 | tf_op jit(solution)/shard_map/ppermute | solution.py:108
  17.6 10.5 %collective-permute-start.20 = (bf16[272,128]{1,0:T(8,128)(2,1)S(1)}, bf16[272,128]{1,0:T(8,128)(2,1)S(1)}, u32[]{:S(2)}, u32[]{:S(2)}) collective-permute-start(bf16[272,128]{1,0:T(8,128)(2,1)S(1)} %shard_map.77.refs_0_), channel_id=1, source_target_pairs={{0,4},{1,5},{2,6},{3,7},{4,0},{5,1},{6,2},{7,3},{8,12},{9,13},{10,... | collective-permute-start | bytes 208904 | tf_op jit(solution)/shard_map/ppermute | solution.py:108
  19.1 9.2 %collective-permute-start.21 = (bf16[272,128]{1,0:T(8,128)(2,1)S(1)}, bf16[272,128]{1,0:T(8,128)(2,1)S(1)}, u32[]{:S(2)}, u32[]{:S(2)}) collective-permute-start(bf16[272,128]{1,0:T(8,128)(2,1)S(1)} %shard_map.77.refs_0_), channel_id=1, source_target_pairs={{0,6},{1,7},{2,4},{3,5},{4,2},{5,3},{6,0},{7,1},{8,14},{9,15},{10,... | collective-permute-start | bytes 208904 | tf_op jit(solution)/shard_map/ppermute | solution.py:108
  19.7 4.3 %collective-permute-start.1 = (bf16[128,256]{1,0:T(8,128)(2,1)S(1)}, bf16[128,256]{1,0:T(8,128)(2,1)S(1)}, u32[]{:S(2)}, u32[]{:S(2)}) collective-permute-start(bf16[128,256]{1,0:T(8,128)(2,1)S(1)} %copy-done.6), channel_id=1, source_target_pairs={{0,24},{1,25},{2,26},{3,27},{4,28},{5,29},{6,30},{7,31},{8,0},{9,1... | collective-permute-start | bytes 196616 | tf_op jit(solution)/shard_map/ppermute | solution.py:108
  20.2 5.2 %collective-permute-start.2 = (bf16[128,256]{1,0:T(8,128)(2,1)S(1)}, bf16[128,256]{1,0:T(8,128)(2,1)S(1)}, u32[]{:S(2)}, u32[]{:S(2)}) collective-permute-start(bf16[128,256]{1,0:T(8,128)(2,1)S(1)} %copy-done.6), channel_id=1, source_target_pairs={{0,16},{1,17},{2,18},{3,19},{4,20},{5,21},{6,22},{7,23},{8,24},{9,... | collective-permute-start | bytes 196616 | tf_op jit(solution)/shard_map/ppermute | solution.py:108
  24.1 4.5 %collective-permute-start.22 = (bf16[272,128]{1,0:T(8,128)(2,1)S(1)}, bf16[272,128]{1,0:T(8,128)(2,1)S(1)}, u32[]{:S(2)}, u32[]{:S(2)}) collective-permute-start(bf16[272,128]{1,0:T(8,128)(2,1)S(1)} %shard_map.77.refs_0_), channel_id=1, source_target_pairs={{0,1},{1,0},{2,3},{3,2},{4,5},{5,4},{6,7},{7,6},{8,9},{9,8},{10,11... | collective-permute-start | bytes 208904 | tf_op jit(solution)/shard_map/ppermute | solution.py:108
  25.4 8.2 %collective-permute-start.26 = (bf16[816,128]{1,0:T(8,128)(2,1)S(1)}, bf16[816,128]{1,0:T(8,128)(2,1)S(1)}, u32[]{:S(2)}, u32[]{:S(2)}) collective-permute-start(bf16[816,128]{1,0:T(8,128)(2,1)S(1)} %constant_dynamic-update-slice_fusion.4.refs_4_), channel_id=1, source_target_pairs={{0,1},{1,0},{2,3},{3,2},{4,5},{5,4},{6,7},{7,6},{8,9},{9,8},{10,11... | collective-permute-start | bytes 626696 | tf_op jit(solution)/shard_map/ppermute | solution.py:108
  25.4 9.5 %collective-permute-start.17 = (bf16[816,128]{1,0:T(8,128)(2,1)S(1)}, bf16[816,128]{1,0:T(8,128)(2,1)S(1)}, u32[]{:S(2)}, u32[]{:S(2)}) collective-permute-start(bf16[816,128]{1,0:T(8,128)(2,1)S(1)} %constant_dynamic-update-slice_fusion.4.refs_4_), channel_id=1, source_target_pairs={{0,2},{1,3},{2,0},{3,1},{4,6},{5,7},{6,4},{7,5},{8,10},{9,11},{10,... | collective-permute-start | bytes 626696 | tf_op jit(solution)/shard_map/ppermute | solution.py:108
  28.6 12.6 %collective-permute-start.13 = (bf16[816,128]{1,0:T(8,128)(2,1)S(1)}, bf16[816,128]{1,0:T(8,128)(2,1)S(1)}, u32[]{:S(2)}, u32[]{:S(2)}) collective-permute-start(bf16[816,128]{1,0:T(8,128)(2,1)S(1)} %constant_dynamic-update-slice_fusion.4.refs_4_), channel_id=1, source_target_pairs={{0,4},{1,5},{2,6},{3,7},{4,0},{5,1},{6,2},{7,3},{8,12},{9,13},{10,... | collective-permute-start | bytes 626696 | tf_op jit(solution)/shard_map/ppermute | solution.py:108
  30.2 11.0 %collective-permute-start.14 = (bf16[816,128]{1,0:T(8,128)(2,1)S(1)}, bf16[816,128]{1,0:T(8,128)(2,1)S(1)}, u32[]{:S(2)}, u32[]{:S(2)}) collective-permute-start(bf16[816,128]{1,0:T(8,128)(2,1)S(1)} %constant_dynamic-update-slice_fusion.4.refs_4_), channel_id=1, source_target_pairs={{0,6},{1,7},{2,4},{3,5},{4,2},{5,3},{6,0},{7,1},{8,14},{9,15},{10,... | collective-permute-start | bytes 626696 | tf_op jit(solution)/shard_map/ppermute | solution.py:108
  31.8 12.4 %collective-permute-start.3 = (bf16[512,256]{1,0:T(8,128)(2,1)S(1)}, bf16[512,256]{1,0:T(8,128)(2,1)S(1)}, u32[]{:S(2)}, u32[]{:S(2)}) collective-permute-start(bf16[512,256]{1,0:T(8,128)(2,1)S(1)} %constant_dynamic-update-slice_fusion.refs_0_), channel_id=1, source_target_pairs={{0,2},{1,3},{2,0},{3,1},{4,6},{5,7},{6,4},{7,5},{8,10},{9,11},{10,... | collective-permute-start | bytes 786440 | tf_op jit(solution)/shard_map/ppermute | solution.py:108
  33.6 18.1 %collective-permute-start.4 = (bf16[512,256]{1,0:T(8,128)(2,1)S(1)}, bf16[512,256]{1,0:T(8,128)(2,1)S(1)}, u32[]{:S(2)}, u32[]{:S(2)}) collective-permute-start(bf16[512,256]{1,0:T(8,128)(2,1)S(1)} %constant_dynamic-update-slice_fusion.refs_0_), channel_id=1, source_target_pairs={{0,4},{1,5},{2,6},{3,7},{4,0},{5,1},{6,2},{7,3},{8,12},{9,13},{10,... | collective-permute-start | bytes 786440 | tf_op jit(solution)/shard_map/ppermute | solution.py:108
  34.9 16.7 %collective-permute-start.5 = (bf16[512,256]{1,0:T(8,128)(2,1)S(1)}, bf16[512,256]{1,0:T(8,128)(2,1)S(1)}, u32[]{:S(2)}, u32[]{:S(2)}) collective-permute-start(bf16[512,256]{1,0:T(8,128)(2,1)S(1)} %constant_dynamic-update-slice_fusion.refs_0_), channel_id=1, source_target_pairs={{0,6},{1,7},{2,4},{3,5},{4,2},{5,3},{6,0},{7,1},{8,14},{9,15},{10,... | collective-permute-start | bytes 786440 | tf_op jit(solution)/shard_map/ppermute | solution.py:108
  41.2 11.0 %collective-permute-start.18 = (bf16[816,128]{1,0:T(8,128)(2,1)S(1)}, bf16[816,128]{1,0:T(8,128)(2,1)S(1)}, u32[]{:S(2)}, u32[]{:S(2)}) collective-permute-start(bf16[816,128]{1,0:T(8,128)(2,1)S(1)} %collective-permute-done.17.refs_0_), channel_id=1, source_target_pairs={{0,1},{1,0},{2,3},{3,2},{4,5},{5,4},{6,7},{7,6},{8,9},{9,8},{10,11... | collective-permute-start | bytes 626696 | tf_op jit(solution)/shard_map/ppermute | solution.py:108
  41.2 11.1 %collective-permute-start.15 = (bf16[816,128]{1,0:T(8,128)(2,1)S(1)}, bf16[816,128]{1,0:T(8,128)(2,1)S(1)}, u32[]{:S(2)}, u32[]{:S(2)}) collective-permute-start(bf16[816,128]{1,0:T(8,128)(2,1)S(1)} %collective-permute-done.13.refs_0_), channel_id=1, source_target_pairs={{0,1},{1,0},{2,3},{3,2},{4,5},{5,4},{6,7},{7,6},{8,9},{9,8},{10,11... | collective-permute-start | bytes 626696 | tf_op jit(solution)/shard_map/ppermute | solution.py:108
  44.2 12.0 %collective-permute-start.6 = (bf16[512,256]{1,0:T(8,128)(2,1)S(1)}, bf16[512,256]{1,0:T(8,128)(2,1)S(1)}, u32[]{:S(2)}, u32[]{:S(2)}) collective-permute-start(bf16[512,256]{1,0:T(8,128)(2,1)S(1)} %constant_dynamic-update-slice_fusion.refs_0_), channel_id=1, source_target_pairs={{0,1},{1,0},{2,3},{3,2},{4,5},{5,4},{6,7},{7,6},{8,9},{9,8},{10,11... | collective-permute-start | bytes 786440 | tf_op jit(solution)/shard_map/ppermute | solution.py:108
  51.7 2.6 %collective-permute-start.16 = (bf16[816,128]{1,0:T(8,128)(2,1)S(1)}, bf16[816,128]{1,0:T(8,128)(2,1)S(1)}, u32[]{:S(2)}, u32[]{:S(2)}) collective-permute-start(bf16[816,128]{1,0:T(8,128)(2,1)S(1)} %collective-permute-done.14.refs_1_), channel_id=1, source_target_pairs={{0,1},{1,0},{2,3},{3,2},{4,5},{5,4},{6,7},{7,6},{8,9},{9,8},{10,11... | collective-permute-start | bytes 626696 | tf_op jit(solution)/shard_map/ppermute | solution.py:108
  51.7 4.6 %collective-permute-start.7 = (bf16[512,256]{1,0:T(8,128)(2,1)S(1)}, bf16[512,256]{1,0:T(8,128)(2,1)S(1)}, u32[]{:S(2)}, u32[]{:S(2)}) collective-permute-start(bf16[512,256]{1,0:T(8,128)(2,1)S(1)} %collective-permute-done.3.refs_1_), channel_id=1, source_target_pairs={{0,1},{1,0},{2,3},{3,2},{4,5},{5,4},{6,7},{7,6},{8,9},{9,8},{10,11... | collective-permute-start | bytes 786440 | tf_op jit(solution)/shard_map/ppermute | solution.py:108
  52.2 4.1 %collective-permute-start.8 = (bf16[512,256]{1,0:T(8,128)(2,1)S(1)}, bf16[512,256]{1,0:T(8,128)(2,1)S(1)}, u32[]{:S(2)}, u32[]{:S(2)}) collective-permute-start(bf16[512,256]{1,0:T(8,128)(2,1)S(1)} %collective-permute-done.4.refs_2_), channel_id=1, source_target_pairs={{0,1},{1,0},{2,3},{3,2},{4,5},{5,4},{6,7},{7,6},{8,9},{9,8},{10,11... | collective-permute-start | bytes 786440 | tf_op jit(solution)/shard_map/ppermute | solution.py:108
  52.3 4.0 %collective-permute-start.9 = (bf16[512,256]{1,0:T(8,128)(2,1)S(1)}, bf16[512,256]{1,0:T(8,128)(2,1)S(1)}, u32[]{:S(2)}, u32[]{:S(2)}) collective-permute-start(bf16[512,256]{1,0:T(8,128)(2,1)S(1)} %collective-permute-done.5.refs_3_), channel_id=1, source_target_pairs={{0,1},{1,0},{2,3},{3,2},{4,5},{5,4},{6,7},{7,6},{8,9},{9,8},{10,11... | collective-permute-start | bytes 786440 | tf_op jit(solution)/shard_map/ppermute | solution.py:108
  59.7 4.6 %collective-permute-start.49 = (f32[128,128]{1,0:T(8,128)S(1)}, f32[128,128]{1,0:T(8,128)S(1)}, u32[]{:S(2)}, u32[]{:S(2)}) collective-permute-start(f32[128,128]{1,0:T(8,128)S(1)} %shard_map.86), channel_id=1, source_target_pairs={{0,1},{1,0},{2,3},{3,2},{4,5},{5,4},{6,7},{7,6},{8,9},{9,8},{10,11... | collective-permute-start | bytes 196616 | tf_op jit(solution)/shard_map/ppermute | solution.py:159
  59.8 6.8 %collective-permute-start.27 = (bf16[256,128]{1,0:T(8,128)(2,1)S(1)}, bf16[256,128]{1,0:T(8,128)(2,1)S(1)}, u32[]{:S(2)}, u32[]{:S(2)}) collective-permute-start(bf16[256,128]{1,0:T(8,128)(2,1)S(1)} %get-tuple-element.35.refs_0_), channel_id=1, source_target_pairs={{0,8},{1,9},{2,10},{3,11},{4,12},{5,13},{6,14},{7,15},{8,16},{9,17... | collective-permute-start | bytes 196616 | tf_op jit(solution)/shard_map/ppermute | solution.py:108
  60.3 7.6 %collective-permute-start.28 = (bf16[256,128]{1,0:T(8,128)(2,1)S(1)}, bf16[256,128]{1,0:T(8,128)(2,1)S(1)}, u32[]{:S(2)}, u32[]{:S(2)}) collective-permute-start(bf16[256,128]{1,0:T(8,128)(2,1)S(1)} %get-tuple-element.35.refs_0_), channel_id=1, source_target_pairs={{0,24},{1,25},{2,26},{3,27},{4,28},{5,29},{6,30},{7,31},{8,0},{9,1... | collective-permute-start | bytes 196616 | tf_op jit(solution)/shard_map/ppermute | solution.py:108
  63.6 8.9 %collective-permute-start.29 = (bf16[256,128]{1,0:T(8,128)(2,1)S(1)}, bf16[256,128]{1,0:T(8,128)(2,1)S(1)}, u32[]{:S(2)}, u32[]{:S(2)}) collective-permute-start(bf16[256,128]{1,0:T(8,128)(2,1)S(1)} %get-tuple-element.35.refs_0_), channel_id=1, source_target_pairs={{0,16},{1,17},{2,18},{3,19},{4,20},{5,21},{6,22},{7,23},{8,24},{9,... | collective-permute-start | bytes 196616 | tf_op jit(solution)/shard_map/ppermute | solution.py:108
  63.6 6.0 %collective-permute-start.36 = (bf16[256,128]{1,0:T(8,128)(2,1)S(1)}, bf16[256,128]{1,0:T(8,128)(2,1)S(1)}, u32[]{:S(2)}, u32[]{:S(2)}) collective-permute-start(bf16[256,128]{1,0:T(8,128)(2,1)S(1)} %get-tuple-element.35.refs_0_), channel_id=1, source_target_pairs={{0,2},{1,3},{2,0},{3,1},{4,6},{5,7},{6,4},{7,5},{8,10},{9,11},{10,... | collective-permute-start | bytes 196616 | tf_op jit(solution)/shard_map/ppermute | solution.py:108
  64.2 5.5 %collective-permute-start.37 = (bf16[256,128]{1,0:T(8,128)(2,1)S(1)}, bf16[256,128]{1,0:T(8,128)(2,1)S(1)}, u32[]{:S(2)}, u32[]{:S(2)}) collective-permute-start(bf16[256,128]{1,0:T(8,128)(2,1)S(1)} %get-tuple-element.35.refs_0_), channel_id=1, source_target_pairs={{0,4},{1,5},{2,6},{3,7},{4,0},{5,1},{6,2},{7,3},{8,12},{9,13},{10,... | collective-permute-start | bytes 196616 | tf_op jit(solution)/shard_map/ppermute | solution.py:108
  66.6 6.1 %collective-permute-start.38 = (bf16[256,128]{1,0:T(8,128)(2,1)S(1)}, bf16[256,128]{1,0:T(8,128)(2,1)S(1)}, u32[]{:S(2)}, u32[]{:S(2)}) collective-permute-start(bf16[256,128]{1,0:T(8,128)(2,1)S(1)} %get-tuple-element.35.refs_0_), channel_id=1, source_target_pairs={{0,6},{1,7},{2,4},{3,5},{4,2},{5,3},{6,0},{7,1},{8,14},{9,15},{10,... | collective-permute-start | bytes 196616 | tf_op jit(solution)/shard_map/ppermute | solution.py:108
  67.9 4.6 %collective-permute-start.50 = (f32[128,128]{1,0:T(8,128)S(1)}, f32[128,128]{1,0:T(8,128)S(1)}, u32[]{:S(2)}, u32[]{:S(2)}) collective-permute-start(f32[128,128]{1,0:T(8,128)S(1)} %add.41), channel_id=1, source_target_pairs={{0,2},{1,3},{2,0},{3,1},{4,6},{5,7},{6,4},{7,5},{8,10},{9,11},{10,... | collective-permute-start | bytes 196616 | tf_op jit(solution)/shard_map/ppermute | solution.py:159
  69.6 4.4 %collective-permute-start.39 = (bf16[256,128]{1,0:T(8,128)(2,1)S(1)}, bf16[256,128]{1,0:T(8,128)(2,1)S(1)}, u32[]{:S(2)}, u32[]{:S(2)}) collective-permute-start(bf16[256,128]{1,0:T(8,128)(2,1)S(1)} %get-tuple-element.35.refs_0_), channel_id=1, source_target_pairs={{0,1},{1,0},{2,3},{3,2},{4,5},{5,4},{6,7},{7,6},{8,9},{9,8},{10,11... | collective-permute-start | bytes 196616 | tf_op jit(solution)/shard_map/ppermute | solution.py:108
  69.7 5.1 %collective-permute-start.40 = (bf16[256,128]{1,0:T(8,128)(2,1)S(1)}, bf16[256,128]{1,0:T(8,128)(2,1)S(1)}, u32[]{:S(2)}, u32[]{:S(2)}) collective-permute-start(bf16[256,128]{1,0:T(8,128)(2,1)S(1)} %collective-permute-done.36.refs_1_), channel_id=1, source_target_pairs={{0,1},{1,0},{2,3},{3,2},{4,5},{5,4},{6,7},{7,6},{8,9},{9,8},{10,11... | collective-permute-start | bytes 196616 | tf_op jit(solution)/shard_map/ppermute | solution.py:108
  72.5 4.6 %collective-permute-start.41 = (bf16[256,128]{1,0:T(8,128)(2,1)S(1)}, bf16[256,128]{1,0:T(8,128)(2,1)S(1)}, u32[]{:S(2)}, u32[]{:S(2)}) collective-permute-start(bf16[256,128]{1,0:T(8,128)(2,1)S(1)} %collective-permute-done.37.refs_2_), channel_id=1, source_target_pairs={{0,1},{1,0},{2,3},{3,2},{4,5},{5,4},{6,7},{7,6},{8,9},{9,8},{10,11... | collective-permute-start | bytes 196616 | tf_op jit(solution)/shard_map/ppermute | solution.py:108
  72.5 4.6 %collective-permute-start.51 = (f32[128,128]{1,0:T(8,128)S(1)}, f32[128,128]{1,0:T(8,128)S(1)}, u32[]{:S(2)}, u32[]{:S(2)}) collective-permute-start(f32[128,128]{1,0:T(8,128)S(1)} %add.42), channel_id=1, source_target_pairs={{0,8},{1,9},{2,10},{3,11},{4,12},{5,13},{6,14},{7,15},{8,0},{9,1},... | collective-permute-start | bytes 196616 | tf_op jit(solution)/shard_map/ppermute | solution.py:159
  72.6 13.5 %collective-permute-start.34 = (bf16[768,128]{1,0:T(8,128)(2,1)S(1)}, bf16[768,128]{1,0:T(8,128)(2,1)S(1)}, u32[]{:S(2)}, u32[]{:S(2)}) collective-permute-start(bf16[768,128]{1,0:T(8,128)(2,1)S(1)} %constant_dynamic-update-slice_fusion.7.refs_4_), channel_id=1, source_target_pairs={{0,2},{1,3},{2,0},{3,1},{4,6},{5,7},{6,4},{7,5},{8,10},{9,11},{10,... | collective-permute-start | bytes 589832 | tf_op jit(solution)/shard_map/ppermute | solution.py:108
  74.1 12.0 %collective-permute-start.30 = (bf16[768,128]{1,0:T(8,128)(2,1)S(1)}, bf16[768,128]{1,0:T(8,128)(2,1)S(1)}, u32[]{:S(2)}, u32[]{:S(2)}) collective-permute-start(bf16[768,128]{1,0:T(8,128)(2,1)S(1)} %constant_dynamic-update-slice_fusion.7.refs_4_), channel_id=1, source_target_pairs={{0,4},{1,5},{2,6},{3,7},{4,0},{5,1},{6,2},{7,3},{8,12},{9,13},{10,... | collective-permute-start | bytes 589832 | tf_op jit(solution)/shard_map/ppermute | solution.py:108
  74.8 11.8 %collective-permute-start.31 = (bf16[768,128]{1,0:T(8,128)(2,1)S(1)}, bf16[768,128]{1,0:T(8,128)(2,1)S(1)}, u32[]{:S(2)}, u32[]{:S(2)}) collective-permute-start(bf16[768,128]{1,0:T(8,128)(2,1)S(1)} %constant_dynamic-update-slice_fusion.7.refs_4_), channel_id=1, source_target_pairs={{0,6},{1,7},{2,4},{3,5},{4,2},{5,3},{6,0},{7,1},{8,14},{9,15},{10,... | collective-permute-start | bytes 589832 | tf_op jit(solution)/shard_map/ppermute | solution.py:108
  77.1 9.6 %collective-permute-start.43 = (bf16[768,128]{1,0:T(8,128)(2,1)S(1)}, bf16[768,128]{1,0:T(8,128)(2,1)S(1)}, u32[]{:S(2)}, u32[]{:S(2)}) collective-permute-start(bf16[768,128]{1,0:T(8,128)(2,1)S(1)} %constant_dynamic-update-slice_fusion.7.refs_4_), channel_id=1, source_target_pairs={{0,1},{1,0},{2,3},{3,2},{4,5},{5,4},{6,7},{7,6},{8,9},{9,8},{10,11... | collective-permute-start | bytes 589832 | tf_op jit(solution)/shard_map/ppermute | solution.py:108
  77.1 6.9 %collective-permute-start.52 = (f32[128,128]{1,0:T(8,128)S(1)}, f32[128,128]{1,0:T(8,128)S(1)}, u32[]{:S(2)}, u32[]{:S(2)}) collective-permute-start(f32[128,128]{1,0:T(8,128)S(1)} %add.43), channel_id=1, source_target_pairs={{0,16},{1,17},{2,18},{3,19},{4,20},{5,21},{6,22},{7,23},{8,24},{9,... | collective-permute-start | bytes 196616 | tf_op jit(solution)/shard_map/ppermute | solution.py:159
  85.2 8.3 %collective-permute-start.53 = (f32[128,128]{1,0:T(8,128)S(1)}, f32[128,128]{1,0:T(8,128)S(1)}, u32[]{:S(2)}, u32[]{:S(2)}) collective-permute-start(f32[128,128]{1,0:T(8,128)S(1)} %add.44), channel_id=1, source_target_pairs={{0,4},{1,5},{2,6},{3,7},{4,0},{5,1},{6,2},{7,3},{8,12},{9,13},{10,... | collective-permute-start | bytes 196616 | tf_op jit(solution)/shard_map/ppermute | solution.py:159
  86.1 3.3 %collective-permute-start.32 = (bf16[768,128]{1,0:T(8,128)(2,1)S(1)}, bf16[768,128]{1,0:T(8,128)(2,1)S(1)}, u32[]{:S(2)}, u32[]{:S(2)}) collective-permute-start(bf16[768,128]{1,0:T(8,128)(2,1)S(1)} %collective-permute-done.30.refs_0_), channel_id=1, source_target_pairs={{0,1},{1,0},{2,3},{3,2},{4,5},{5,4},{6,7},{7,6},{8,9},{9,8},{10,11... | collective-permute-start | bytes 589832 | tf_op jit(solution)/shard_map/ppermute | solution.py:108
  86.6 2.8 %collective-permute-start.33 = (bf16[768,128]{1,0:T(8,128)(2,1)S(1)}, bf16[768,128]{1,0:T(8,128)(2,1)S(1)}, u32[]{:S(2)}, u32[]{:S(2)}) collective-permute-start(bf16[768,128]{1,0:T(8,128)(2,1)S(1)} %collective-permute-done.31.refs_1_), channel_id=1, source_target_pairs={{0,1},{1,0},{2,3},{3,2},{4,5},{5,4},{6,7},{7,6},{8,9},{9,8},{10,11... | collective-permute-start | bytes 589832 | tf_op jit(solution)/shard_map/ppermute | solution.py:108
  94.4 3.9 %collective-permute-start.45 = (f32[64,64]{1,0:T(8,128)S(1)}, f32[64,64]{1,0:T(8,128)S(1)}, u32[]{:S(2)}, u32[]{:S(2)}) collective-permute-start(f32[64,64]{1,0:T(8,128)S(1)} %add.36), channel_id=1, source_target_pairs={{0,2},{1,3},{2,0},{3,1},{4,6},{5,7},{6,4},{7,5},{8,10},{9,11},{10,... | collective-permute-start | bytes 49160 | tf_op jit(solution)/shard_map/ppermute | solution.py:159
  98.3 3.9 %collective-permute-start.46 = (f32[64,64]{1,0:T(8,128)S(1)}, f32[64,64]{1,0:T(8,128)S(1)}, u32[]{:S(2)}, u32[]{:S(2)}) collective-permute-start(f32[64,64]{1,0:T(8,128)S(1)} %add.37), channel_id=1, source_target_pairs={{0,8},{1,9},{2,10},{3,11},{4,12},{5,13},{6,14},{7,15},{8,0},{9,1},... | collective-permute-start | bytes 49160 | tf_op jit(solution)/shard_map/ppermute | solution.py:159
  102.2 5.6 %collective-permute-start.47 = (f32[64,64]{1,0:T(8,128)S(1)}, f32[64,64]{1,0:T(8,128)S(1)}, u32[]{:S(2)}, u32[]{:S(2)}) collective-permute-start(f32[64,64]{1,0:T(8,128)S(1)} %add.38), channel_id=1, source_target_pairs={{0,16},{1,17},{2,18},{3,19},{4,20},{5,21},{6,22},{7,23},{8,24},{9,... | collective-permute-start | bytes 49160 | tf_op jit(solution)/shard_map/ppermute | solution.py:159
  107.9 4.1 %collective-permute-start.48 = (f32[64,64]{1,0:T(8,128)S(1)}, f32[64,64]{1,0:T(8,128)S(1)}, u32[]{:S(2)}, u32[]{:S(2)}) collective-permute-start(f32[64,64]{1,0:T(8,128)S(1)} %add.39), channel_id=1, source_target_pairs={{0,4},{1,5},{2,6},{3,7},{4,0},{5,1},{6,2},{7,3},{8,12},{9,13},{10,... | collective-permute-start | bytes 49160 | tf_op jit(solution)/shard_map/ppermute | solution.py:159
  (14 other events, 62.3 us)

commit v2 on v1

--- a/solution.py
+++ b/solution.py
@@ -10,6 +10,7 @@
 
 highest = lax.Precision.HIGHEST
 AXES = ("row", "col")
+GRID = "zyxc"
 SHIFT = 1.25
 HALVES = False
 FLOPS_PER_US = 5e8
@@ -159,23 +160,21 @@
     return lax.ppermute(value, AXES, pairs)
 
 
-def sum_everywhere(value, dims):
-    for axis in (3, 2, 0, 1):
+def sum_everywhere(value, dims, order, keep_last=False):
+    other = None
+    for name in order:
+        axis = GRID.index(name)
         n = dims[axis]
-        if n & (n - 1) == 0:
-            bit = 1
-            while bit < n:
+        bits = [1 << k for k in range(n.bit_length() - 1)] if n & (n - 1) == 0 else [0]
+        for bit in bits:
+            if other is not None:
+                value = value + other
+            if bit:
                 other = exchange(value, dims, axis, bit)
-                value = value + other
-                bit *= 2
-        else:
-            total = value
-            for s in range(1, n):
-                step = [0, 0, 0, 0]
-                step[axis] = s
-                total = total + permute(value, dims, tuple(step))
-            value = total
-    return value
+            else:
+                steps = [[s if k == axis else 0 for k in range(4)] for s in range(1, n)]
+                other = sum(permute(value, dims, tuple(step)) for step in steps)
+    return (value, other) if keep_last else value + other
 
 
 def split(value):
@@ -365,14 +364,30 @@
     gram[...] = nt(first[...], image[...]) * (1.0 / count)
 
 
+PANEL = 8
+
+
 def eliminate(work, begin, end):
-    rows = lax.broadcasted_iota(jnp.int32, (work.shape[0], 1), 0)
-    for k in range(begin, end):
-        scale = lax.rsqrt(work[k : k + 1, k : k + 1])
-        pivot = work[k : k + 1, :] * scale
-        column = jnp.where(rows > k, work[:, k : k + 1] * scale, 0.0)
-        work = jnp.where(rows == k, pivot, work - column * pivot)
-    return work
+    n, width = work.shape
+    lanes = 128
+    rows = lax.broadcasted_iota(jnp.int32, (n, lanes), 0)
+    parts = [work[:, k : min(k + lanes, width)] for k in range(0, width, lanes)]
+    for at in range(begin, end, PANEL):
+        stop = min(at + PANEL, end)
+        spread = {
+            k: jnp.broadcast_to(parts[k // lanes][:, k % lanes : k % lanes + 1], (n, lanes))
+            for k in range(at, stop)
+        }
+        for k in range(at, stop):
+            scale = lax.rsqrt(spread[k][k : k + 1, :])
+            column = jnp.where(rows > k, spread[k] * scale, 0.0)
+            for j in range(k + 1, stop):
+                spread[j] = spread[j] - column * (spread[j][k : k + 1, :] * scale)
+            for i, part in enumerate(parts):
+                w = part.shape[1]
+                pivot = part[k : k + 1, :] * scale[:, :w]
+                parts[i] = jnp.where(rows[:, :w] == k, pivot, part - column[:, :w] * pivot)
+    return parts[0] if len(parts) == 1 else jnp.concatenate(parts, axis=1)
 
 
 def unit(m):
@@ -400,7 +415,7 @@
     out[...] = eliminate(given[...], 0, m // 2)
 
 
-def eliminate_kernel_4(joint, one, given, first_two, parts):
+def eliminate_kernel_4(joint, one, given, turned, first, second, first_two, parts, known, basis):
     m = given.shape[0]
     work = eliminate(given[...], m // 2, m)
     keep = lax.broadcasted_iota(jnp.int32, (m, m), 0) <= lax.broadcasted_iota(jnp.int32, (m, m), 1)
@@ -412,28 +427,25 @@
     first_two[1] = nn(inverse_first, upper.T)
     t_s = -nn(t_x, nn(z1.T, inverse_first))
     p_s = nn(t_s, g01) + nn(t_x, g11)
-    parts[0] = t_s
-    parts[1] = t_x
-    parts[2] = nt(p_s, t_s) + nt(nn(t_s, g11), t_x)
-    parts[3] = nn(nn(upper, inverse_first.T), inverse_first)
-
-
-def last_kernel(*refs):
-    n = len(refs) - 7
-    (first_two, parts, turned, first, second, residual, coefficients) = refs[n:]
-    g12 = refs[0][...]
-    for k in range(1, n):
-        g12 += refs[k][...]
+    parts[0] = t_x
+    parts[1] = nt(p_s, t_s) + nt(nn(t_s, g11), t_x)
+    back = nn(nn(upper, inverse_first.T), inverse_first)
+    basis[...] = nn(jnp.concatenate([t_s, t_x], axis=1), jnp.concatenate([turned[...], first[...]]))
+    known[...] = nn(
+        jnp.concatenate([t_s, t_x, -back], axis=1),
+        jnp.concatenate([first[...], second[...], turned[...]]),
+    )
+
+
+def last_kernel(gram, other, first_two, parts, known, basis, residual, coefficients):
+    g12 = gram[...] + other[...]
     m = g12.shape[0]
-    t_s, t_x = parts[0], parts[1]
-    alpha_next = parts[2] + nt(nn(t_x, g12), t_x)
-    on_start = -parts[3] - nn(alpha_next, t_s)
-    on_first = t_s - nn(alpha_next, t_x)
+    t_x = parts[0]
+    alpha_next = parts[1] + nt(nn(t_x, g12), t_x)
+    residual[...] = known[...] - nn(alpha_next, basis[...])
     coefficients[0] = first_two[0]
     coefficients[1] = first_two[1]
     coefficients[2] = alpha_next + SHIFT * unit(m)
-    factors = jnp.concatenate([on_start, on_first, t_x], axis=1)
-    residual[...] = nn(factors, jnp.concatenate([turned[...], first[...], second[...]]))
 
 
 VMEM = pl.BlockSpec(memory_space=pltpu.VMEM)
@@ -563,7 +575,7 @@
         work=1.0,
     )
     u, _ = gather_everywhere(payload, dims, apart)
-    joint = sum_everywhere(joint, dims)
+    joint = sum_everywhere(joint, dims, "czxy")
     acc = None
     for group, found in zip(groups, neighbors):
         acc, _ = weigh(
@@ -583,15 +595,17 @@
         [shaped((m, 3 * m)), shaped((m, 2 * m))], work=3.0,
     )
     (two,) = call(eliminate_kernel_3, [(schur, VMEM)], [shaped((m, 2 * m))], work=3.0)
-    first_two, parts = call(
-        eliminate_kernel_4, [(joint, VMEM), (one, VMEM), (two, VMEM)],
-        [shaped((2, m, m)), shaped((4, m, m))], work=3.0,
-    )
-    g12 = sum_everywhere(g12, dims)
+    first_two, parts, known, basis = call(
+        eliminate_kernel_4,
+        [(joint, VMEM), (one, VMEM), (two, VMEM), (turned, VMEM), (first, VMEM), (second, VMEM)],
+        [shaped((2, m, m)), shaped((2, m, m)), shaped(turned.shape), shaped(turned.shape)],
+        work=3.0,
+    )
+    g12, other = sum_everywhere(g12, dims, "cxzy", keep_last=True)
     residual, coefficients = call(
         last_kernel,
-        [(g12, VMEM), (first_two, VMEM), (parts, VMEM), (turned, VMEM), (first, VMEM),
-         (second, VMEM)],
+        [(g12, VMEM), (other, VMEM), (first_two, VMEM), (parts, VMEM), (known, VMEM),
+         (basis, VMEM)],
         [shaped(turned.shape), shaped((3, columns, columns))],
         work=2.0,
     )

time: 114 us -> 117 us (1.026)
  waiting for transfers between devices: 32.4 us -> 46.4 us
  Pallas kernels: 29.4 us -> 21.6 us
  starting transfers between devices: 47.5 us -> 44.2 us
    ppermute x10, waiting for transfers between devices: 9.05 us -> 22.6 us  [exchange(): return lax.ppermute(value, AXES, pairs)]
    pallas_call x15, Pallas kernels: 29.4 us -> 21.6 us  [call(): pl.pallas_call(kernel, in_specs=[spec for _, spec in inputs], out_shape=o...]
    ppermute x10, starting transfers between devices: 10.8 us -> 7.92 us  [exchange(): return lax.ppermute(value, AXES, pairs)]
  transfers between devices with their start and end apart: 54 -> 54, of which waited for: 15 -> 18; matrix products, arithmetic and copies ran while one was open for 0% -> 0% of each run, Pallas kernels for 21% -> 14%
where the time goes in v2:
time: 117 us
  waiting for transfers between devices  46.4 us (40%)
  starting transfers between devices  44.2 us (38%)
  Pallas kernels  21.6 us (18%)
  local copies, waits for them, and re-layouts  3.26 us (3%)
    ppermute x44, starting transfers between devices, permute(): return lax.ppermute(value, AXES, pairs)  36.3 us
    ppermute x44, waiting for transfers between devices, permute(): return lax.ppermute(value, AXES, pairs)  23.8 us
    ppermute x10, waiting for transfers between devices, exchange(): return lax.ppermute(value, AXES, pairs)  22.6 us
    pallas_call x15, Pallas kernels, call(): pl.pallas_call(kernel, in_specs=[spec for _, spec in inputs], out_shape=o...  21.6 us
    ppermute x10, starting transfers between devices, exchange(): return lax.ppermute(value, AXES, pairs)  7.92 us
    unnamed x23, local copies, waits for them, and re-layouts  3.22 us
  transfers between devices with their start and end apart: 54, of which 18 were waited for; matrix products, arithmetic and copies ran while one was open for 0% of the time, Pallas kernels for 14%

profile of v2, /device:TPU:0, one launch (start us, length us, event | category | flops | bytes accessed | tf_op | source)
XLA Modules:
  0.0 116.6 jit_solution(2521823689865946711)
XLA Ops:
  1.3 0.9 copy-done.1
  2.2 0.9 copy-done.3
  3.8 3.1 %collective-permute-start.10 = (bf16[272,128]{1,0:T(8,128)(2,1)S(1)}, bf16[272,128]{1,0:T(8,128)(2,1)S(1)}, u32[]{:S(2)}, u32[]{:S(2)}) collective-permute-start(bf16[272,128]{1,0:T(8,128)(2,1)S(1)} %shard_map.77.refs_0_), channel_id=1, source_target_pairs={{0,8},{1,9},{2,10},{3,11},{4,12},{5,13},{6,14},{7,15},{8,16},{9,17... | collective-permute-start | bytes 208904 | tf_op jit(solution)/shard_map/ppermute | solution.py:109
  7.0 2.1 %collective-permute-start.11 = (bf16[272,128]{1,0:T(8,128)(2,1)S(1)}, bf16[272,128]{1,0:T(8,128)(2,1)S(1)}, u32[]{:S(2)}, u32[]{:S(2)}) collective-permute-start(bf16[272,128]{1,0:T(8,128)(2,1)S(1)} %shard_map.77.refs_0_), channel_id=1, source_target_pairs={{0,24},{1,25},{2,26},{3,27},{4,28},{5,29},{6,30},{7,31},{8,0},{9,1... | collective-permute-start | bytes 208904 | tf_op jit(solution)/shard_map/ppermute | solution.py:109
  9.1 0.9 collective-permute-start.12
  10.0 1.5 %collective-permute-start.19 = (bf16[272,128]{1,0:T(8,128)(2,1)S(1)}, bf16[272,128]{1,0:T(8,128)(2,1)S(1)}, u32[]{:S(2)}, u32[]{:S(2)}) collective-permute-start(bf16[272,128]{1,0:T(8,128)(2,1)S(1)} %shard_map.77.refs_0_), channel_id=1, source_target_pairs={{0,2},{1,3},{2,0},{3,1},{4,6},{5,7},{6,4},{7,5},{8,10},{9,11},{10,... | collective-permute-start | bytes 208904 | tf_op jit(solution)/shard_map/ppermute | solution.py:109
  11.5 1.6 %collective-permute-start = (bf16[128,256]{1,0:T(8,128)(2,1)S(1)}, bf16[128,256]{1,0:T(8,128)(2,1)S(1)}, u32[]{:S(2)}, u32[]{:S(2)}) collective-permute-start(bf16[128,256]{1,0:T(8,128)(2,1)S(1)} %copy-done.6), channel_id=1, source_target_pairs={{0,8},{1,9},{2,10},{3,11},{4,12},{5,13},{6,14},{7,15},{8,16},{9,17... | collective-permute-start | bytes 196616 | tf_op jit(solution)/shard_map/ppermute | solution.py:109
  13.8 3.8 %collective-permute-done = bf16[128,256]{1,0:T(8,128)(2,1)S(1)} collective-permute-done((bf16[128,256]{1,0:T(8,128)(2,1)S(1)}, bf16[128,256]{1,0:T(8,128)(2,1)S(1)}, u32[]{:S(2)}, u32[]{:S(2)}) %collective-permute-start) | collective-permute-done | bytes 65568 | tf_op jit(solution)/shard_map/ppermute | solution.py:109
  17.6 1.5 %collective-permute-start.20 = (bf16[272,128]{1,0:T(8,128)(2,1)S(1)}, bf16[272,128]{1,0:T(8,128)(2,1)S(1)}, u32[]{:S(2)}, u32[]{:S(2)}) collective-permute-start(bf16[272,128]{1,0:T(8,128)(2,1)S(1)} %shard_map.77.refs_0_), channel_id=1, source_target_pairs={{0,4},{1,5},{2,6},{3,7},{4,0},{5,1},{6,2},{7,3},{8,12},{9,13},{10,... | collective-permute-start | bytes 208904 | tf_op jit(solution)/shard_map/ppermute | solution.py:109
  20.2 1.3 %collective-permute-start.2 = (bf16[128,256]{1,0:T(8,128)(2,1)S(1)}, bf16[128,256]{1,0:T(8,128)(2,1)S(1)}, u32[]{:S(2)}, u32[]{:S(2)}) collective-permute-start(bf16[128,256]{1,0:T(8,128)(2,1)S(1)} %copy-done.6), channel_id=1, source_target_pairs={{0,16},{1,17},{2,18},{3,19},{4,20},{5,21},{6,22},{7,23},{8,24},{9,... | collective-permute-start | bytes 196616 | tf_op jit(solution)/shard_map/ppermute | solution.py:109
  21.5 2.6 %collective-permute-done.1 = bf16[128,256]{1,0:T(8,128)(2,1)S(1)} collective-permute-done((bf16[128,256]{1,0:T(8,128)(2,1)S(1)}, bf16[128,256]{1,0:T(8,128)(2,1)S(1)}, u32[]{:S(2)}, u32[]{:S(2)}) %collective-permute-start.1) | collective-permute-done | bytes 65568 | tf_op jit(solution)/shard_map/ppermute | solution.py:109
  24.1 1.3 %collective-permute-done.2 = bf16[128,256]{1,0:T(8,128)(2,1)S(1)} collective-permute-done((bf16[128,256]{1,0:T(8,128)(2,1)S(1)}, bf16[128,256]{1,0:T(8,128)(2,1)S(1)}, u32[]{:S(2)}, u32[]{:S(2)}) %collective-permute-start.2) | collective-permute-done | bytes 65568 | tf_op jit(solution)/shard_map/ppermute | solution.py:109
  25.4 2.6 %collective-permute-start.17 = (bf16[816,128]{1,0:T(8,128)(2,1)S(1)}, bf16[816,128]{1,0:T(8,128)(2,1)S(1)}, u32[]{:S(2)}, u32[]{:S(2)}) collective-permute-start(bf16[816,128]{1,0:T(8,128)(2,1)S(1)} %constant_dynamic-update-slice_fusion.4.refs_4_), channel_id=1, source_target_pairs={{0,2},{1,3},{2,0},{3,1},{4,6},{5,7},{6,4},{7,5},{8,10},{9,11},{10,... | collective-permute-start | bytes 626696 | tf_op jit(solution)/shard_map/ppermute | solution.py:109
  28.6 1.6 %collective-permute-start.13 = (bf16[816,128]{1,0:T(8,128)(2,1)S(1)}, bf16[816,128]{1,0:T(8,128)(2,1)S(1)}, u32[]{:S(2)}, u32[]{:S(2)}) collective-permute-start(bf16[816,128]{1,0:T(8,128)(2,1)S(1)} %constant_dynamic-update-slice_fusion.4.refs_4_), channel_id=1, source_target_pairs={{0,4},{1,5},{2,6},{3,7},{4,0},{5,1},{6,2},{7,3},{8,12},{9,13},{10,... | collective-permute-start | bytes 626696 | tf_op jit(solution)/shard_map/ppermute | solution.py:109
  30.6 1.2 %collective-permute-done.25.refs_8_ = bf16[272,128]{1,0:T(8,128)(2,1)S(1)} collective-permute-done((bf16[272,128]{1,0:T(8,128)(2,1)S(1)}, bf16[272,128]{1,0:T(8,128)(2,1)S(1)}, u32[]{:S(2)}, u32[]{:S(2)}) %collective-permute-start.25) | collective-permute-done | bytes 69664 | tf_op jit(solution)/shard_map/ppermute | solution.py:109
  31.8 1.7 %collective-permute-start.3 = (bf16[512,256]{1,0:T(8,128)(2,1)S(1)}, bf16[512,256]{1,0:T(8,128)(2,1)S(1)}, u32[]{:S(2)}, u32[]{:S(2)}) collective-permute-start(bf16[512,256]{1,0:T(8,128)(2,1)S(1)} %constant_dynamic-update-slice_fusion.refs_0_), channel_id=1, source_target_pairs={{0,2},{1,3},{2,0},{3,1},{4,6},{5,7},{6,4},{7,5},{8,10},{9,11},{10,... | collective-permute-start | bytes 786440 | tf_op jit(solution)/shard_map/ppermute | solution.py:109
  33.6 1.4 %collective-permute-start.4 = (bf16[512,256]{1,0:T(8,128)(2,1)S(1)}, bf16[512,256]{1,0:T(8,128)(2,1)S(1)}, u32[]{:S(2)}, u32[]{:S(2)}) collective-permute-start(bf16[512,256]{1,0:T(8,128)(2,1)S(1)} %constant_dynamic-update-slice_fusion.refs_0_), channel_id=1, source_target_pairs={{0,4},{1,5},{2,6},{3,7},{4,0},{5,1},{6,2},{7,3},{8,12},{9,13},{10,... | collective-permute-start | bytes 786440 | tf_op jit(solution)/shard_map/ppermute | solution.py:109
  34.9 2.1 %collective-permute-start.5 = (bf16[512,256]{1,0:T(8,128)(2,1)S(1)}, bf16[512,256]{1,0:T(8,128)(2,1)S(1)}, u32[]{:S(2)}, u32[]{:S(2)}) collective-permute-start(bf16[512,256]{1,0:T(8,128)(2,1)S(1)} %constant_dynamic-update-slice_fusion.refs_0_), channel_id=1, source_target_pairs={{0,6},{1,7},{2,4},{3,5},{4,2},{5,3},{6,0},{7,1},{8,14},{9,15},{10,... | collective-permute-start | bytes 786440 | tf_op jit(solution)/shard_map/ppermute | solution.py:109
  37.1 4.1 %collective-permute-done.13.refs_0_ = bf16[816,128]{1,0:T(8,128)(2,1)S(1)} collective-permute-done((bf16[816,128]{1,0:T(8,128)(2,1)S(1)}, bf16[816,128]{1,0:T(8,128)(2,1)S(1)}, u32[]{:S(2)}, u32[]{:S(2)}) %collective-permute-start.13) | collective-permute-done | bytes 208928 | tf_op jit(solution)/shard_map/ppermute | solution.py:109
  41.7 2.0 %shard_map.78 = (f32[8,4,64,128]{3,2,1,0:T(8,128)S(1)}, f32[8,4,64,128]{3,2,1,0:T(8,128)S(1)}, s32[1,128]{1,0:T(1,128)S(1)}) custom-call(bf16[272,128]{1,0:T(8,128)(2,1)S(1)} %shard_map.77.refs_0_, bf16[272,128]{1,0:T(8,128)(2,1)S(1)} %collective-permute-done.19.refs_1_, bf16[272,128]{1,0:T(8,128)(2,1)S(1)} %collective-permute-done.20.refs_2_, ...), custom_call_target="tpu_custom_call" | custom-call | flops 2500000000 | tf_op jit(solution)/shard_map/pallas_call | solution.py:465
  44.2 7.4 %collective-permute-done.4.refs_2_ = bf16[512,256]{1,0:T(8,128)(2,1)S(1)} collective-permute-done((bf16[512,256]{1,0:T(8,128)(2,1)S(1)}, bf16[512,256]{1,0:T(8,128)(2,1)S(1)}, u32[]{:S(2)}, u32[]{:S(2)}) %collective-permute-start.4) | collective-permute-done | bytes 262176 | tf_op jit(solution)/shard_map/ppermute | solution.py:109
  52.7 1.5 %shard_map.79 = (f32[8,4,64,128]{3,2,1,0:T(8,128)S(1)}, f32[8,4,64,128]{3,2,1,0:T(8,128)S(1)}, s32[1,128]{1,0:T(1,128)S(1)}) custom-call(bf16[816,128]{1,0:T(8,128)(2,1)S(1)} %collective-permute-done.17.refs_0_, bf16[816,128]{1,0:T(8,128)(2,1)S(1)} %collective-permute-done.18.refs_1_, ...), custom_call_target="tpu_custom_call", output_to_operand_aliasing={{0}: (3, {}), {1}: (4, {})} | custom-call | flops 500000000 | tf_op jit(solution)/shard_map/pallas_call | solution.py:465
  54.3 1.9 %shard_map.80 = (f32[8,4,64,128]{3,2,1,0:T(8,128)S(1)}, f32[8,4,64,128]{3,2,1,0:T(8,128)S(1)}, s32[1,128]{1,0:T(1,128)S(1)}) custom-call(bf16[816,128]{1,0:T(8,128)(2,1)S(1)} %collective-permute-done.13.refs_0_, bf16[816,128]{1,0:T(8,128)(2,1)S(1)} %collective-permute-done.14.refs_1_, ...), custom_call_target="tpu_custom_call", output_to_operand_aliasing={{0}: (5, {}), {1}: (6, {})} | custom-call | flops 1000000000 | tf_op jit(solution)/shard_map/pallas_call | solution.py:465
  56.3 3.0 %shard_map.81 = (bf16[4,8,128,128]{3,2,1,0:T(8,128)(2,1)S(1)}, bf16[256,128]{1,0:T(8,128)(2,1)S(1)}, f32[64,512]{1,0:T(8,128)S(1)}) custom-call(bf16[512,256]{1,0:T(8,128)(2,1)S(1)} %constant_dynamic-update-slice_fusion.refs_0_, bf16[512,256]{1,0:T(8,128)(2,1)S(1)} %collective-permute-done.3.refs_1_, bf16[512,256]{1,0:T(8,128)(2,1)S(1)} %collective-permute-done.4.refs_2_, ...), custom_call_target="tpu_custom_call" | custom-call | flops 1500000000 | tf_op jit(solution)/shard_map/pallas_call | solution.py:465
  60.3 3.3 %collective-permute-start.28 = (bf16[256,128]{1,0:T(8,128)(2,1)S(1)}, bf16[256,128]{1,0:T(8,128)(2,1)S(1)}, u32[]{:S(2)}, u32[]{:S(2)}) collective-permute-start(bf16[256,128]{1,0:T(8,128)(2,1)S(1)} %get-tuple-element.37.refs_0_), channel_id=1, source_target_pairs={{0,24},{1,25},{2,26},{3,27},{4,28},{5,29},{6,30},{7,31},{8,0},{9,1... | collective-permute-start | bytes 196616 | tf_op jit(solution)/shard_map/ppermute | solution.py:109
  64.2 1.3 %collective-permute-start.37 = (bf16[256,128]{1,0:T(8,128)(2,1)S(1)}, bf16[256,128]{1,0:T(8,128)(2,1)S(1)}, u32[]{:S(2)}, u32[]{:S(2)}) collective-permute-start(bf16[256,128]{1,0:T(8,128)(2,1)S(1)} %get-tuple-element.37.refs_0_), channel_id=1, source_target_pairs={{0,4},{1,5},{2,6},{3,7},{4,0},{5,1},{6,2},{7,3},{8,12},{9,13},{10,... | collective-permute-start | bytes 196616 | tf_op jit(solution)/shard_map/ppermute | solution.py:109
  65.5 1.0 collective-permute-done.27
  66.6 1.3 %collective-permute-start.38 = (bf16[256,128]{1,0:T(8,128)(2,1)S(1)}, bf16[256,128]{1,0:T(8,128)(2,1)S(1)}, u32[]{:S(2)}, u32[]{:S(2)}) collective-permute-start(bf16[256,128]{1,0:T(8,128)(2,1)S(1)} %get-tuple-element.37.refs_0_), channel_id=1, source_target_pairs={{0,6},{1,7},{2,4},{3,5},{4,2},{5,3},{6,0},{7,1},{8,14},{9,15},{10,... | collective-permute-start | bytes 196616 | tf_op jit(solution)/shard_map/ppermute | solution.py:109
  68.6 3.6 %collective-permute-done.50 = f32[128,128]{1,0:T(8,128)S(1)} collective-permute-done((f32[128,128]{1,0:T(8,128)S(1)}, f32[128,128]{1,0:T(8,128)S(1)}, u32[]{:S(2)}, u32[]{:S(2)}) %collective-permute-start.50) | collective-permute-done | bytes 65568 | tf_op jit(solution)/shard_map/ppermute | solution.py:160
  72.2 2.3 %collective-permute-start.51 = (f32[128,128]{1,0:T(8,128)S(1)}, f32[128,128]{1,0:T(8,128)S(1)}, u32[]{:S(2)}, u32[]{:S(2)}) collective-permute-start(f32[128,128]{1,0:T(8,128)S(1)} %add.38), channel_id=1, source_target_pairs={{0,16},{1,17},{2,18},{3,19},{4,20},{5,21},{6,22},{7,23},{8,24},{9,... | collective-permute-start | bytes 196616 | tf_op jit(solution)/shard_map/ppermute | solution.py:160
  75.3 1.3 %collective-permute-start.30 = (bf16[768,128]{1,0:T(8,128)(2,1)S(1)}, bf16[768,128]{1,0:T(8,128)(2,1)S(1)}, u32[]{:S(2)}, u32[]{:S(2)}) collective-permute-start(bf16[768,128]{1,0:T(8,128)(2,1)S(1)} %constant_dynamic-update-slice_fusion.7.refs_4_), channel_id=1, source_target_pairs={{0,4},{1,5},{2,6},{3,7},{4,0},{5,1},{6,2},{7,3},{8,12},{9,13},{10,... | collective-permute-start | bytes 589832 | tf_op jit(solution)/shard_map/ppermute | solution.py:109
  76.5 1.6 %collective-permute-start.31 = (bf16[768,128]{1,0:T(8,128)(2,1)S(1)}, bf16[768,128]{1,0:T(8,128)(2,1)S(1)}, u32[]{:S(2)}, u32[]{:S(2)}) collective-permute-start(bf16[768,128]{1,0:T(8,128)(2,1)S(1)} %constant_dynamic-update-slice_fusion.7.refs_4_), channel_id=1, source_target_pairs={{0,6},{1,7},{2,4},{3,5},{4,2},{5,3},{6,0},{7,1},{8,14},{9,15},{10,... | collective-permute-start | bytes 589832 | tf_op jit(solution)/shard_map/ppermute | solution.py:109
  79.0 1.4 %collective-permute-start.52 = (f32[128,128]{1,0:T(8,128)S(1)}, f32[128,128]{1,0:T(8,128)S(1)}, u32[]{:S(2)}, u32[]{:S(2)}) collective-permute-start(f32[128,128]{1,0:T(8,128)S(1)} %add.39), channel_id=1, source_target_pairs={{0,2},{1,3},{2,0},{3,1},{4,6},{5,7},{6,4},{7,5},{8,10},{9,11},{10,... | collective-permute-start | bytes 196616 | tf_op jit(solution)/shard_map/ppermute | solution.py:160
  80.4 7.0 %collective-permute-done.52 = f32[128,128]{1,0:T(8,128)S(1)} collective-permute-done((f32[128,128]{1,0:T(8,128)S(1)}, f32[128,128]{1,0:T(8,128)S(1)}, u32[]{:S(2)}, u32[]{:S(2)}) %collective-permute-start.52) | collective-permute-done | bytes 65568 | tf_op jit(solution)/shard_map/ppermute | solution.py:160
  87.4 1.2 %collective-permute-done.42.refs_8_ = bf16[256,128]{1,0:T(8,128)(2,1)S(1)} collective-permute-done((bf16[256,128]{1,0:T(8,128)(2,1)S(1)}, bf16[256,128]{1,0:T(8,128)(2,1)S(1)}, u32[]{:S(2)}, u32[]{:S(2)}) %collective-permute-start.42) | collective-permute-done | bytes 65568 | tf_op jit(solution)/shard_map/ppermute | solution.py:109
  88.6 1.5 %collective-permute-start.53 = (f32[128,128]{1,0:T(8,128)S(1)}, f32[128,128]{1,0:T(8,128)S(1)}, u32[]{:S(2)}, u32[]{:S(2)}) collective-permute-start(f32[128,128]{1,0:T(8,128)S(1)} %add.40), channel_id=1, source_target_pairs={{0,4},{1,5},{2,6},{3,7},{4,0},{5,1},{6,2},{7,3},{8,12},{9,13},{10,... | collective-permute-start | bytes 196616 | tf_op jit(solution)/shard_map/ppermute | solution.py:160
  90.7 1.5 %shard_map.82 = (f32[8,4,64,128]{3,2,1,0:T(8,128)S(1)}, f32[8,4,64,128]{3,2,1,0:T(8,128)S(1)}) custom-call(bf16[256,128]{1,0:T(8,128)(2,1)S(1)} %get-tuple-element.37.refs_0_, bf16[256,128]{1,0:T(8,128)(2,1)S(1)} %collective-permute-done.36.refs_1_, bf16[256,128]{1,0:T(8,128)(2,1)S(1)} %collective-permute-done.37.refs_2_, ...), custom_call_target="tpu_custom_call" | custom-call | flops 2500000000 | tf_op jit(solution)/shard_map/pallas_call | solution.py:465
  92.1 1.2 %shard_map.83 = (f32[8,4,64,128]{3,2,1,0:T(8,128)S(1)}, f32[8,4,64,128]{3,2,1,0:T(8,128)S(1)}) custom-call(bf16[768,128]{1,0:T(8,128)(2,1)S(1)} %collective-permute-done.34.refs_0_, bf16[768,128]{1,0:T(8,128)(2,1)S(1)} %collective-permute-done.35.refs_1_, ...), custom_call_target="tpu_custom_call", output_to_operand_aliasing={{0}: (3, {}), {1}: (4, {})} | custom-call | flops 500000000 | tf_op jit(solution)/shard_map/pallas_call | solution.py:465
  93.4 1.6 %shard_map.84 = (f32[8,4,64,128]{3,2,1,0:T(8,128)S(1)}, f32[8,4,64,128]{3,2,1,0:T(8,128)S(1)}) custom-call(bf16[768,128]{1,0:T(8,128)(2,1)S(1)} %collective-permute-done.30.refs_0_, bf16[768,128]{1,0:T(8,128)(2,1)S(1)} %collective-permute-done.31.refs_1_, ...), custom_call_target="tpu_custom_call", output_to_operand_aliasing={{0}: (5, {}), {1}: (6, {})} | custom-call | flops 1000000000 | tf_op jit(solution)/shard_map/pallas_call | solution.py:465
  95.1 1.9 %shard_map.85 = (f32[64,512]{1,0:T(8,128)S(1)}, f32[64,64]{1,0:T(8,128)S(1)}) custom-call(f32[8,4,64,128]{3,2,1,0:T(8,128)S(1)} %get-tuple-element.44.acc_0, f32[8,4,64,128]{3,2,1,0:T(8,128)S(1)} %get-tuple-element.45.acc_1, bf16[4,8,128,128]{3,2,1,0:T(8,128)(2,1)S(1)} %get-tuple-element.46.chosen, bf16[4,128,128]{2,1,0:T(8,128)(2,1)S(1)} %copy-done.2, ...), custom_call_target="tpu_custom_call" | custom-call | flops 1500000000 | tf_op jit(solution)/shard_map/pallas_call | solution.py:465
  98.8 0.9 shard_map.87.given
  99.7 2.6 %collective-permute-done.45 = f32[64,64]{1,0:T(8,128)S(1)} collective-permute-done((f32[64,64]{1,0:T(8,128)S(1)}, f32[64,64]{1,0:T(8,128)S(1)}, u32[]{:S(2)}, u32[]{:S(2)}) %collective-permute-start.45) | collective-permute-done | bytes 16416 | tf_op jit(solution)/shard_map/ppermute | solution.py:160
  103.0 1.0 shard_map.88
  104.1 2.1 %collective-permute-done.46 = f32[64,64]{1,0:T(8,128)S(1)} collective-permute-done((f32[64,64]{1,0:T(8,128)S(1)}, f32[64,64]{1,0:T(8,128)S(1)}, u32[]{:S(2)}, u32[]{:S(2)}) %collective-permute-start.46) | collective-permute-done | bytes 16416 | tf_op jit(solution)/shard_map/ppermute | solution.py:160
  107.4 4.0 %collective-permute-done.47 = f32[64,64]{1,0:T(8,128)S(1)} collective-permute-done((f32[64,64]{1,0:T(8,128)S(1)}, f32[64,64]{1,0:T(8,128)S(1)}, u32[]{:S(2)}, u32[]{:S(2)}) %collective-permute-start.47) | collective-permute-done | bytes 16416 | tf_op jit(solution)/shard_map/ppermute | solution.py:160
  111.9 1.7 %shard_map.90 = (f32[2,64,64]{2,1,0:T(8,128)S(1)}, f32[2,64,64]{2,1,0:T(8,128)S(1)}, f32[64,512]{1,0:T(8,128)S(1)}, f32[64,512]{1,0:T(8,128)S(1)}) custom-call(f32[128,128]{1,0:T(8,128)S(1)} %add.41.joint, f32[64,192]{1,0:T(8,128)S(1)} %get-tuple-element.49.one, f32[64,128]{1,0:T(8,128)S(1)} %shard_map.89.given, f32[64,512]{1,0:T(8,128)S(1)} %bitcast.10, ...), custom_call_target="tpu_custom_call" | custom-call | flops 1500000000 | tf_op jit(solution)/shard_map/pallas_call | solution.py:465
  113.7 1.6 %collective-permute-done.48.other = f32[64,64]{1,0:T(8,128)S(1)} collective-permute-done((f32[64,64]{1,0:T(8,128)S(1)}, f32[64,64]{1,0:T(8,128)S(1)}, u32[]{:S(2)}, u32[]{:S(2)}) %collective-permute-start.48) | collective-permute-done | bytes 16416 | tf_op jit(solution)/shard_map/ppermute | solution.py:160
  115.3 1.3 %shard_map.91 = (f32[64,512]{1,0:T(8,128)}, f32[3,64,64]{2,1,0:T(8,128)}) custom-call(f32[64,64]{1,0:T(8,128)S(1)} %add.36.gram, f32[64,64]{1,0:T(8,128)S(1)} %collective-permute-done.48.other, f32[2,64,64]{2,1,0:T(8,128)S(1)} %get-tuple-element.52.first_two, f32[2,64,64]{2,1,0:T(8,128)S(1)} %get-tuple-element.53.parts, ...), custom_call_target="tpu_custom_call" | custom-call | flops 1000000000 | tf_op jit(solution)/shard_map/pallas_call | solution.py:465
  (113 shorter events, 14.9 us)
Async XLA Ops:
  3.8 15.2 %collective-permute-start.10 = (bf16[272,128]{1,0:T(8,128)(2,1)S(1)}, bf16[272,128]{1,0:T(8,128)(2,1)S(1)}, u32[]{:S(2)}, u32[]{:S(2)}) collective-permute-start(bf16[272,128]{1,0:T(8,128)(2,1)S(1)} %shard_map.77.refs_0_), channel_id=1, source_target_pairs={{0,8},{1,9},{2,10},{3,11},{4,12},{5,13},{6,14},{7,15},{8,16},{9,17... | collective-permute-start | bytes 208904 | tf_op jit(solution)/shard_map/ppermute | solution.py:109
  7.0 12.8 %collective-permute-start.11 = (bf16[272,128]{1,0:T(8,128)(2,1)S(1)}, bf16[272,128]{1,0:T(8,128)(2,1)S(1)}, u32[]{:S(2)}, u32[]{:S(2)}) collective-permute-start(bf16[272,128]{1,0:T(8,128)(2,1)S(1)} %shard_map.77.refs_0_), channel_id=1, source_target_pairs={{0,24},{1,25},{2,26},{3,27},{4,28},{5,29},{6,30},{7,31},{8,0},{9,1... | collective-permute-start | bytes 208904 | tf_op jit(solution)/shard_map/ppermute | solution.py:109
  9.1 11.1 %collective-permute-start.12 = (bf16[272,128]{1,0:T(8,128)(2,1)S(1)}, bf16[272,128]{1,0:T(8,128)(2,1)S(1)}, u32[]{:S(2)}, u32[]{:S(2)}) collective-permute-start(bf16[272,128]{1,0:T(8,128)(2,1)S(1)} %shard_map.77.refs_0_), channel_id=1, source_target_pairs={{0,16},{1,17},{2,18},{3,19},{4,20},{5,21},{6,22},{7,23},{8,24},{9,... | collective-permute-start | bytes 208904 | tf_op jit(solution)/shard_map/ppermute | solution.py:109
  10.0 15.4 %collective-permute-start.19 = (bf16[272,128]{1,0:T(8,128)(2,1)S(1)}, bf16[272,128]{1,0:T(8,128)(2,1)S(1)}, u32[]{:S(2)}, u32[]{:S(2)}) collective-permute-start(bf16[272,128]{1,0:T(8,128)(2,1)S(1)} %shard_map.77.refs_0_), channel_id=1, source_target_pairs={{0,2},{1,3},{2,0},{3,1},{4,6},{5,7},{6,4},{7,5},{8,10},{9,11},{10,... | collective-permute-start | bytes 208904 | tf_op jit(solution)/shard_map/ppermute | solution.py:109
  11.5 6.1 %collective-permute-start = (bf16[128,256]{1,0:T(8,128)(2,1)S(1)}, bf16[128,256]{1,0:T(8,128)(2,1)S(1)}, u32[]{:S(2)}, u32[]{:S(2)}) collective-permute-start(bf16[128,256]{1,0:T(8,128)(2,1)S(1)} %copy-done.6), channel_id=1, source_target_pairs={{0,8},{1,9},{2,10},{3,11},{4,12},{5,13},{6,14},{7,15},{8,16},{9,17... | collective-permute-start | bytes 196616 | tf_op jit(solution)/shard_map/ppermute | solution.py:109
  17.6 10.5 %collective-permute-start.20 = (bf16[272,128]{1,0:T(8,128)(2,1)S(1)}, bf16[272,128]{1,0:T(8,128)(2,1)S(1)}, u32[]{:S(2)}, u32[]{:S(2)}) collective-permute-start(bf16[272,128]{1,0:T(8,128)(2,1)S(1)} %shard_map.77.refs_0_), channel_id=1, source_target_pairs={{0,4},{1,5},{2,6},{3,7},{4,0},{5,1},{6,2},{7,3},{8,12},{9,13},{10,... | collective-permute-start | bytes 208904 | tf_op jit(solution)/shard_map/ppermute | solution.py:109
  19.1 9.2 %collective-permute-start.21 = (bf16[272,128]{1,0:T(8,128)(2,1)S(1)}, bf16[272,128]{1,0:T(8,128)(2,1)S(1)}, u32[]{:S(2)}, u32[]{:S(2)}) collective-permute-start(bf16[272,128]{1,0:T(8,128)(2,1)S(1)} %shard_map.77.refs_0_), channel_id=1, source_target_pairs={{0,6},{1,7},{2,4},{3,5},{4,2},{5,3},{6,0},{7,1},{8,14},{9,15},{10,... | collective-permute-start | bytes 208904 | tf_op jit(solution)/shard_map/ppermute | solution.py:109
  19.7 4.3 %collective-permute-start.1 = (bf16[128,256]{1,0:T(8,128)(2,1)S(1)}, bf16[128,256]{1,0:T(8,128)(2,1)S(1)}, u32[]{:S(2)}, u32[]{:S(2)}) collective-permute-start(bf16[128,256]{1,0:T(8,128)(2,1)S(1)} %copy-done.6), channel_id=1, source_target_pairs={{0,24},{1,25},{2,26},{3,27},{4,28},{5,29},{6,30},{7,31},{8,0},{9,1... | collective-permute-start | bytes 196616 | tf_op jit(solution)/shard_map/ppermute | solution.py:109
  20.2 5.2 %collective-permute-start.2 = (bf16[128,256]{1,0:T(8,128)(2,1)S(1)}, bf16[128,256]{1,0:T(8,128)(2,1)S(1)}, u32[]{:S(2)}, u32[]{:S(2)}) collective-permute-start(bf16[128,256]{1,0:T(8,128)(2,1)S(1)} %copy-done.6), channel_id=1, source_target_pairs={{0,16},{1,17},{2,18},{3,19},{4,20},{5,21},{6,22},{7,23},{8,24},{9,... | collective-permute-start | bytes 196616 | tf_op jit(solution)/shard_map/ppermute | solution.py:109
  24.1 4.5 %collective-permute-start.22 = (bf16[272,128]{1,0:T(8,128)(2,1)S(1)}, bf16[272,128]{1,0:T(8,128)(2,1)S(1)}, u32[]{:S(2)}, u32[]{:S(2)}) collective-permute-start(bf16[272,128]{1,0:T(8,128)(2,1)S(1)} %shard_map.77.refs_0_), channel_id=1, source_target_pairs={{0,1},{1,0},{2,3},{3,2},{4,5},{5,4},{6,7},{7,6},{8,9},{9,8},{10,11... | collective-permute-start | bytes 208904 | tf_op jit(solution)/shard_map/ppermute | solution.py:109
  25.4 8.2 %collective-permute-start.26 = (bf16[816,128]{1,0:T(8,128)(2,1)S(1)}, bf16[816,128]{1,0:T(8,128)(2,1)S(1)}, u32[]{:S(2)}, u32[]{:S(2)}) collective-permute-start(bf16[816,128]{1,0:T(8,128)(2,1)S(1)} %constant_dynamic-update-slice_fusion.4.refs_4_), channel_id=1, source_target_pairs={{0,1},{1,0},{2,3},{3,2},{4,5},{5,4},{6,7},{7,6},{8,9},{9,8},{10,11... | collective-permute-start | bytes 626696 | tf_op jit(solution)/shard_map/ppermute | solution.py:109
  25.4 9.5 %collective-permute-start.17 = (bf16[816,128]{1,0:T(8,128)(2,1)S(1)}, bf16[816,128]{1,0:T(8,128)(2,1)S(1)}, u32[]{:S(2)}, u32[]{:S(2)}) collective-permute-start(bf16[816,128]{1,0:T(8,128)(2,1)S(1)} %constant_dynamic-update-slice_fusion.4.refs_4_), channel_id=1, source_target_pairs={{0,2},{1,3},{2,0},{3,1},{4,6},{5,7},{6,4},{7,5},{8,10},{9,11},{10,... | collective-permute-start | bytes 626696 | tf_op jit(solution)/shard_map/ppermute | solution.py:109
  28.6 12.6 %collective-permute-start.13 = (bf16[816,128]{1,0:T(8,128)(2,1)S(1)}, bf16[816,128]{1,0:T(8,128)(2,1)S(1)}, u32[]{:S(2)}, u32[]{:S(2)}) collective-permute-start(bf16[816,128]{1,0:T(8,128)(2,1)S(1)} %constant_dynamic-update-slice_fusion.4.refs_4_), channel_id=1, source_target_pairs={{0,4},{1,5},{2,6},{3,7},{4,0},{5,1},{6,2},{7,3},{8,12},{9,13},{10,... | collective-permute-start | bytes 626696 | tf_op jit(solution)/shard_map/ppermute | solution.py:109
  30.2 11.0 %collective-permute-start.14 = (bf16[816,128]{1,0:T(8,128)(2,1)S(1)}, bf16[816,128]{1,0:T(8,128)(2,1)S(1)}, u32[]{:S(2)}, u32[]{:S(2)}) collective-permute-start(bf16[816,128]{1,0:T(8,128)(2,1)S(1)} %constant_dynamic-update-slice_fusion.4.refs_4_), channel_id=1, source_target_pairs={{0,6},{1,7},{2,4},{3,5},{4,2},{5,3},{6,0},{7,1},{8,14},{9,15},{10,... | collective-permute-start | bytes 626696 | tf_op jit(solution)/shard_map/ppermute | solution.py:109
  31.8 12.4 %collective-permute-start.3 = (bf16[512,256]{1,0:T(8,128)(2,1)S(1)}, bf16[512,256]{1,0:T(8,128)(2,1)S(1)}, u32[]{:S(2)}, u32[]{:S(2)}) collective-permute-start(bf16[512,256]{1,0:T(8,128)(2,1)S(1)} %constant_dynamic-update-slice_fusion.refs_0_), channel_id=1, source_target_pairs={{0,2},{1,3},{2,0},{3,1},{4,6},{5,7},{6,4},{7,5},{8,10},{9,11},{10,... | collective-permute-start | bytes 786440 | tf_op jit(solution)/shard_map/ppermute | solution.py:109
  33.6 18.1 %collective-permute-start.4 = (bf16[512,256]{1,0:T(8,128)(2,1)S(1)}, bf16[512,256]{1,0:T(8,128)(2,1)S(1)}, u32[]{:S(2)}, u32[]{:S(2)}) collective-permute-start(bf16[512,256]{1,0:T(8,128)(2,1)S(1)} %constant_dynamic-update-slice_fusion.refs_0_), channel_id=1, source_target_pairs={{0,4},{1,5},{2,6},{3,7},{4,0},{5,1},{6,2},{7,3},{8,12},{9,13},{10,... | collective-permute-start | bytes 786440 | tf_op jit(solution)/shard_map/ppermute | solution.py:109
  34.9 16.7 %collective-permute-start.5 = (bf16[512,256]{1,0:T(8,128)(2,1)S(1)}, bf16[512,256]{1,0:T(8,128)(2,1)S(1)}, u32[]{:S(2)}, u32[]{:S(2)}) collective-permute-start(bf16[512,256]{1,0:T(8,128)(2,1)S(1)} %constant_dynamic-update-slice_fusion.refs_0_), channel_id=1, source_target_pairs={{0,6},{1,7},{2,4},{3,5},{4,2},{5,3},{6,0},{7,1},{8,14},{9,15},{10,... | collective-permute-start | bytes 786440 | tf_op jit(solution)/shard_map/ppermute | solution.py:109
  41.2 11.0 %collective-permute-start.18 = (bf16[816,128]{1,0:T(8,128)(2,1)S(1)}, bf16[816,128]{1,0:T(8,128)(2,1)S(1)}, u32[]{:S(2)}, u32[]{:S(2)}) collective-permute-start(bf16[816,128]{1,0:T(8,128)(2,1)S(1)} %collective-permute-done.17.refs_0_), channel_id=1, source_target_pairs={{0,1},{1,0},{2,3},{3,2},{4,5},{5,4},{6,7},{7,6},{8,9},{9,8},{10,11... | collective-permute-start | bytes 626696 | tf_op jit(solution)/shard_map/ppermute | solution.py:109
  41.2 11.1 %collective-permute-start.15 = (bf16[816,128]{1,0:T(8,128)(2,1)S(1)}, bf16[816,128]{1,0:T(8,128)(2,1)S(1)}, u32[]{:S(2)}, u32[]{:S(2)}) collective-permute-start(bf16[816,128]{1,0:T(8,128)(2,1)S(1)} %collective-permute-done.13.refs_0_), channel_id=1, source_target_pairs={{0,1},{1,0},{2,3},{3,2},{4,5},{5,4},{6,7},{7,6},{8,9},{9,8},{10,11... | collective-permute-start | bytes 626696 | tf_op jit(solution)/shard_map/ppermute | solution.py:109
  44.2 12.0 %collective-permute-start.6 = (bf16[512,256]{1,0:T(8,128)(2,1)S(1)}, bf16[512,256]{1,0:T(8,128)(2,1)S(1)}, u32[]{:S(2)}, u32[]{:S(2)}) collective-permute-start(bf16[512,256]{1,0:T(8,128)(2,1)S(1)} %constant_dynamic-update-slice_fusion.refs_0_), channel_id=1, source_target_pairs={{0,1},{1,0},{2,3},{3,2},{4,5},{5,4},{6,7},{7,6},{8,9},{9,8},{10,11... | collective-permute-start | bytes 786440 | tf_op jit(solution)/shard_map/ppermute | solution.py:109
  51.7 2.6 %collective-permute-start.16 = (bf16[816,128]{1,0:T(8,128)(2,1)S(1)}, bf16[816,128]{1,0:T(8,128)(2,1)S(1)}, u32[]{:S(2)}, u32[]{:S(2)}) collective-permute-start(bf16[816,128]{1,0:T(8,128)(2,1)S(1)} %collective-permute-done.14.refs_1_), channel_id=1, source_target_pairs={{0,1},{1,0},{2,3},{3,2},{4,5},{5,4},{6,7},{7,6},{8,9},{9,8},{10,11... | collective-permute-start | bytes 626696 | tf_op jit(solution)/shard_map/ppermute | solution.py:109
  51.7 4.6 %collective-permute-start.7 = (bf16[512,256]{1,0:T(8,128)(2,1)S(1)}, bf16[512,256]{1,0:T(8,128)(2,1)S(1)}, u32[]{:S(2)}, u32[]{:S(2)}) collective-permute-start(bf16[512,256]{1,0:T(8,128)(2,1)S(1)} %collective-permute-done.3.refs_1_), channel_id=1, source_target_pairs={{0,1},{1,0},{2,3},{3,2},{4,5},{5,4},{6,7},{7,6},{8,9},{9,8},{10,11... | collective-permute-start | bytes 786440 | tf_op jit(solution)/shard_map/ppermute | solution.py:109
  52.2 4.1 %collective-permute-start.8 = (bf16[512,256]{1,0:T(8,128)(2,1)S(1)}, bf16[512,256]{1,0:T(8,128)(2,1)S(1)}, u32[]{:S(2)}, u32[]{:S(2)}) collective-permute-start(bf16[512,256]{1,0:T(8,128)(2,1)S(1)} %collective-permute-done.4.refs_2_), channel_id=1, source_target_pairs={{0,1},{1,0},{2,3},{3,2},{4,5},{5,4},{6,7},{7,6},{8,9},{9,8},{10,11... | collective-permute-start | bytes 786440 | tf_op jit(solution)/shard_map/ppermute | solution.py:109
  52.3 4.0 %collective-permute-start.9 = (bf16[512,256]{1,0:T(8,128)(2,1)S(1)}, bf16[512,256]{1,0:T(8,128)(2,1)S(1)}, u32[]{:S(2)}, u32[]{:S(2)}) collective-permute-start(bf16[512,256]{1,0:T(8,128)(2,1)S(1)} %collective-permute-done.5.refs_3_), channel_id=1, source_target_pairs={{0,1},{1,0},{2,3},{3,2},{4,5},{5,4},{6,7},{7,6},{8,9},{9,8},{10,11... | collective-permute-start | bytes 786440 | tf_op jit(solution)/shard_map/ppermute | solution.py:109
  59.7 4.6 %collective-permute-start.49 = (f32[128,128]{1,0:T(8,128)S(1)}, f32[128,128]{1,0:T(8,128)S(1)}, u32[]{:S(2)}, u32[]{:S(2)}) collective-permute-start(f32[128,128]{1,0:T(8,128)S(1)} %shard_map.86), channel_id=1, source_target_pairs={{0,1},{1,0},{2,3},{3,2},{4,5},{5,4},{6,7},{7,6},{8,9},{9,8},{10,11... | collective-permute-start | bytes 196616 | tf_op jit(solution)/shard_map/ppermute | solution.py:160
  59.8 6.8 %collective-permute-start.27 = (bf16[256,128]{1,0:T(8,128)(2,1)S(1)}, bf16[256,128]{1,0:T(8,128)(2,1)S(1)}, u32[]{:S(2)}, u32[]{:S(2)}) collective-permute-start(bf16[256,128]{1,0:T(8,128)(2,1)S(1)} %get-tuple-element.37.refs_0_), channel_id=1, source_target_pairs={{0,8},{1,9},{2,10},{3,11},{4,12},{5,13},{6,14},{7,15},{8,16},{9,17... | collective-permute-start | bytes 196616 | tf_op jit(solution)/shard_map/ppermute | solution.py:109
  60.3 7.6 %collective-permute-start.28 = (bf16[256,128]{1,0:T(8,128)(2,1)S(1)}, bf16[256,128]{1,0:T(8,128)(2,1)S(1)}, u32[]{:S(2)}, u32[]{:S(2)}) collective-permute-start(bf16[256,128]{1,0:T(8,128)(2,1)S(1)} %get-tuple-element.37.refs_0_), channel_id=1, source_target_pairs={{0,24},{1,25},{2,26},{3,27},{4,28},{5,29},{6,30},{7,31},{8,0},{9,1... | collective-permute-start | bytes 196616 | tf_op jit(solution)/shard_map/ppermute | solution.py:109
  63.6 8.6 %collective-permute-start.29 = (bf16[256,128]{1,0:T(8,128)(2,1)S(1)}, bf16[256,128]{1,0:T(8,128)(2,1)S(1)}, u32[]{:S(2)}, u32[]{:S(2)}) collective-permute-start(bf16[256,128]{1,0:T(8,128)(2,1)S(1)} %get-tuple-element.37.refs_0_), channel_id=1, source_target_pairs={{0,16},{1,17},{2,18},{3,19},{4,20},{5,21},{6,22},{7,23},{8,24},{9,... | collective-permute-start | bytes 196616 | tf_op jit(solution)/shard_map/ppermute | solution.py:109
  63.6 4.4 %collective-permute-start.36 = (bf16[256,128]{1,0:T(8,128)(2,1)S(1)}, bf16[256,128]{1,0:T(8,128)(2,1)S(1)}, u32[]{:S(2)}, u32[]{:S(2)}) collective-permute-start(bf16[256,128]{1,0:T(8,128)(2,1)S(1)} %get-tuple-element.37.refs_0_), channel_id=1, source_target_pairs={{0,2},{1,3},{2,0},{3,1},{4,6},{5,7},{6,4},{7,5},{8,10},{9,11},{10,... | collective-permute-start | bytes 196616 | tf_op jit(solution)/shard_map/ppermute | solution.py:109
  64.2 4.3 %collective-permute-start.37 = (bf16[256,128]{1,0:T(8,128)(2,1)S(1)}, bf16[256,128]{1,0:T(8,128)(2,1)S(1)}, u32[]{:S(2)}, u32[]{:S(2)}) collective-permute-start(bf16[256,128]{1,0:T(8,128)(2,1)S(1)} %get-tuple-element.37.refs_0_), channel_id=1, source_target_pairs={{0,4},{1,5},{2,6},{3,7},{4,0},{5,1},{6,2},{7,3},{8,12},{9,13},{10,... | collective-permute-start | bytes 196616 | tf_op jit(solution)/shard_map/ppermute | solution.py:109
  66.6 8.0 %collective-permute-start.38 = (bf16[256,128]{1,0:T(8,128)(2,1)S(1)}, bf16[256,128]{1,0:T(8,128)(2,1)S(1)}, u32[]{:S(2)}, u32[]{:S(2)}) collective-permute-start(bf16[256,128]{1,0:T(8,128)(2,1)S(1)} %get-tuple-element.37.refs_0_), channel_id=1, source_target_pairs={{0,6},{1,7},{2,4},{3,5},{4,2},{5,3},{6,0},{7,1},{8,14},{9,15},{10,... | collective-permute-start | bytes 196616 | tf_op jit(solution)/shard_map/ppermute | solution.py:109
  67.9 4.3 %collective-permute-start.50 = (f32[128,128]{1,0:T(8,128)S(1)}, f32[128,128]{1,0:T(8,128)S(1)}, u32[]{:S(2)}, u32[]{:S(2)}) collective-permute-start(f32[128,128]{1,0:T(8,128)S(1)} %add.37), channel_id=1, source_target_pairs={{0,8},{1,9},{2,10},{3,11},{4,12},{5,13},{6,14},{7,15},{8,0},{9,1},... | collective-permute-start | bytes 196616 | tf_op jit(solution)/shard_map/ppermute | solution.py:160
  68.0 7.3 %collective-permute-start.39 = (bf16[256,128]{1,0:T(8,128)(2,1)S(1)}, bf16[256,128]{1,0:T(8,128)(2,1)S(1)}, u32[]{:S(2)}, u32[]{:S(2)}) collective-permute-start(bf16[256,128]{1,0:T(8,128)(2,1)S(1)} %get-tuple-element.37.refs_0_), channel_id=1, source_target_pairs={{0,1},{1,0},{2,3},{3,2},{4,5},{5,4},{6,7},{7,6},{8,9},{9,8},{10,11... | collective-permute-start | bytes 196616 | tf_op jit(solution)/shard_map/ppermute | solution.py:109
  68.5 8.0 %collective-permute-start.40 = (bf16[256,128]{1,0:T(8,128)(2,1)S(1)}, bf16[256,128]{1,0:T(8,128)(2,1)S(1)}, u32[]{:S(2)}, u32[]{:S(2)}) collective-permute-start(bf16[256,128]{1,0:T(8,128)(2,1)S(1)} %collective-permute-done.36.refs_1_), channel_id=1, source_target_pairs={{0,1},{1,0},{2,3},{3,2},{4,5},{5,4},{6,7},{7,6},{8,9},{9,8},{10,11... | collective-permute-start | bytes 196616 | tf_op jit(solution)/shard_map/ppermute | solution.py:109
  72.2 6.8 %collective-permute-start.41 = (bf16[256,128]{1,0:T(8,128)(2,1)S(1)}, bf16[256,128]{1,0:T(8,128)(2,1)S(1)}, u32[]{:S(2)}, u32[]{:S(2)}) collective-permute-start(bf16[256,128]{1,0:T(8,128)(2,1)S(1)} %collective-permute-done.37.refs_2_), channel_id=1, source_target_pairs={{0,1},{1,0},{2,3},{3,2},{4,5},{5,4},{6,7},{7,6},{8,9},{9,8},{10,11... | collective-permute-start | bytes 196616 | tf_op jit(solution)/shard_map/ppermute | solution.py:109
  72.2 6.7 %collective-permute-start.51 = (f32[128,128]{1,0:T(8,128)S(1)}, f32[128,128]{1,0:T(8,128)S(1)}, u32[]{:S(2)}, u32[]{:S(2)}) collective-permute-start(f32[128,128]{1,0:T(8,128)S(1)} %add.38), channel_id=1, source_target_pairs={{0,16},{1,17},{2,18},{3,19},{4,20},{5,21},{6,22},{7,23},{8,24},{9,... | collective-permute-start | bytes 196616 | tf_op jit(solution)/shard_map/ppermute | solution.py:160
  74.6 15.5 %collective-permute-start.34 = (bf16[768,128]{1,0:T(8,128)(2,1)S(1)}, bf16[768,128]{1,0:T(8,128)(2,1)S(1)}, u32[]{:S(2)}, u32[]{:S(2)}) collective-permute-start(bf16[768,128]{1,0:T(8,128)(2,1)S(1)} %constant_dynamic-update-slice_fusion.7.refs_4_), channel_id=1, source_target_pairs={{0,2},{1,3},{2,0},{3,1},{4,6},{5,7},{6,4},{7,5},{8,10},{9,11},{10,... | collective-permute-start | bytes 589832 | tf_op jit(solution)/shard_map/ppermute | solution.py:109
  75.3 14.8 %collective-permute-start.30 = (bf16[768,128]{1,0:T(8,128)(2,1)S(1)}, bf16[768,128]{1,0:T(8,128)(2,1)S(1)}, u32[]{:S(2)}, u32[]{:S(2)}) collective-permute-start(bf16[768,128]{1,0:T(8,128)(2,1)S(1)} %constant_dynamic-update-slice_fusion.7.refs_4_), channel_id=1, source_target_pairs={{0,4},{1,5},{2,6},{3,7},{4,0},{5,1},{6,2},{7,3},{8,12},{9,13},{10,... | collective-permute-start | bytes 589832 | tf_op jit(solution)/shard_map/ppermute | solution.py:109
  76.5 14.1 %collective-permute-start.31 = (bf16[768,128]{1,0:T(8,128)(2,1)S(1)}, bf16[768,128]{1,0:T(8,128)(2,1)S(1)}, u32[]{:S(2)}, u32[]{:S(2)}) collective-permute-start(bf16[768,128]{1,0:T(8,128)(2,1)S(1)} %constant_dynamic-update-slice_fusion.7.refs_4_), channel_id=1, source_target_pairs={{0,6},{1,7},{2,4},{3,5},{4,2},{5,3},{6,0},{7,1},{8,14},{9,15},{10,... | collective-permute-start | bytes 589832 | tf_op jit(solution)/shard_map/ppermute | solution.py:109
  78.9 11.8 %collective-permute-start.43 = (bf16[768,128]{1,0:T(8,128)(2,1)S(1)}, bf16[768,128]{1,0:T(8,128)(2,1)S(1)}, u32[]{:S(2)}, u32[]{:S(2)}) collective-permute-start(bf16[768,128]{1,0:T(8,128)(2,1)S(1)} %constant_dynamic-update-slice_fusion.7.refs_4_), channel_id=1, source_target_pairs={{0,1},{1,0},{2,3},{3,2},{4,5},{5,4},{6,7},{7,6},{8,9},{9,8},{10,11... | collective-permute-start | bytes 589832 | tf_op jit(solution)/shard_map/ppermute | solution.py:109
  79.0 8.3 %collective-permute-start.52 = (f32[128,128]{1,0:T(8,128)S(1)}, f32[128,128]{1,0:T(8,128)S(1)}, u32[]{:S(2)}, u32[]{:S(2)}) collective-permute-start(f32[128,128]{1,0:T(8,128)S(1)} %add.39), channel_id=1, source_target_pairs={{0,2},{1,3},{2,0},{3,1},{4,6},{5,7},{6,4},{7,5},{8,10},{9,11},{10,... | collective-permute-start | bytes 196616 | tf_op jit(solution)/shard_map/ppermute | solution.py:160
  88.6 8.9 %collective-permute-start.53 = (f32[128,128]{1,0:T(8,128)S(1)}, f32[128,128]{1,0:T(8,128)S(1)}, u32[]{:S(2)}, u32[]{:S(2)}) collective-permute-start(f32[128,128]{1,0:T(8,128)S(1)} %add.40), channel_id=1, source_target_pairs={{0,4},{1,5},{2,6},{3,7},{4,0},{5,1},{6,2},{7,3},{8,12},{9,13},{10,... | collective-permute-start | bytes 196616 | tf_op jit(solution)/shard_map/ppermute | solution.py:160
  90.1 3.3 %collective-permute-start.32 = (bf16[768,128]{1,0:T(8,128)(2,1)S(1)}, bf16[768,128]{1,0:T(8,128)(2,1)S(1)}, u32[]{:S(2)}, u32[]{:S(2)}) collective-permute-start(bf16[768,128]{1,0:T(8,128)(2,1)S(1)} %collective-permute-done.30.refs_0_), channel_id=1, source_target_pairs={{0,1},{1,0},{2,3},{3,2},{4,5},{5,4},{6,7},{7,6},{8,9},{9,8},{10,11... | collective-permute-start | bytes 589832 | tf_op jit(solution)/shard_map/ppermute | solution.py:109
  90.6 2.8 %collective-permute-start.33 = (bf16[768,128]{1,0:T(8,128)(2,1)S(1)}, bf16[768,128]{1,0:T(8,128)(2,1)S(1)}, u32[]{:S(2)}, u32[]{:S(2)}) collective-permute-start(bf16[768,128]{1,0:T(8,128)(2,1)S(1)} %collective-permute-done.31.refs_1_), channel_id=1, source_target_pairs={{0,1},{1,0},{2,3},{3,2},{4,5},{5,4},{6,7},{7,6},{8,9},{9,8},{10,11... | collective-permute-start | bytes 589832 | tf_op jit(solution)/shard_map/ppermute | solution.py:109
  98.4 3.9 %collective-permute-start.45 = (f32[64,64]{1,0:T(8,128)S(1)}, f32[64,64]{1,0:T(8,128)S(1)}, u32[]{:S(2)}, u32[]{:S(2)}) collective-permute-start(f32[64,64]{1,0:T(8,128)S(1)} %add.33), channel_id=1, source_target_pairs={{0,2},{1,3},{2,0},{3,1},{4,6},{5,7},{6,4},{7,5},{8,10},{9,11},{10,... | collective-permute-start | bytes 49160 | tf_op jit(solution)/shard_map/ppermute | solution.py:160
  102.3 3.9 %collective-permute-start.46 = (f32[64,64]{1,0:T(8,128)S(1)}, f32[64,64]{1,0:T(8,128)S(1)}, u32[]{:S(2)}, u32[]{:S(2)}) collective-permute-start(f32[64,64]{1,0:T(8,128)S(1)} %add.34), channel_id=1, source_target_pairs={{0,8},{1,9},{2,10},{3,11},{4,12},{5,13},{6,14},{7,15},{8,0},{9,1},... | collective-permute-start | bytes 49160 | tf_op jit(solution)/shard_map/ppermute | solution.py:160
  106.2 5.2 %collective-permute-start.47 = (f32[64,64]{1,0:T(8,128)S(1)}, f32[64,64]{1,0:T(8,128)S(1)}, u32[]{:S(2)}, u32[]{:S(2)}) collective-permute-start(f32[64,64]{1,0:T(8,128)S(1)} %add.35), channel_id=1, source_target_pairs={{0,16},{1,17},{2,18},{3,19},{4,20},{5,21},{6,22},{7,23},{8,24},{9,... | collective-permute-start | bytes 49160 | tf_op jit(solution)/shard_map/ppermute | solution.py:160
  111.4 3.9 %collective-permute-start.48 = (f32[64,64]{1,0:T(8,128)S(1)}, f32[64,64]{1,0:T(8,128)S(1)}, u32[]{:S(2)}, u32[]{:S(2)}) collective-permute-start(f32[64,64]{1,0:T(8,128)S(1)} %add.36.gram), channel_id=1, source_target_pairs={{0,4},{1,5},{2,6},{3,7},{4,0},{5,1},{6,2},{7,3},{8,12},{9,13},{10,... | collective-permute-start | bytes 49160 | tf_op jit(solution)/shard_map/ppermute | solution.py:160
  (14 other events, 62.3 us)

commit v3 on v2

--- a/solution.py
+++ b/solution.py
@@ -324,13 +324,25 @@
                         else:
                             hit = (dy == piece[0]) & (line >= lo) & (line < hi)
                             block = jnp.where(hit, other, block)
-                    chosen[p, owner_col * per_col + k] = block
+                    chosen[p, owner_col, :, k * band : (k + 1) * band] = block
 
 
 def image_of(acc_0, acc_1, chosen, correlation, p):
-    total = times(acc_0[0, p] + acc_1[0, p], chosen[p, 0], True)
-    for j in range(1, acc_0.shape[0]):
-        total += times(acc_0[j, p] + acc_1[j, p], chosen[p, j], True)
+    total = None
+    groups = chosen.shape[1]
+    per_col = acc_0.shape[0] // groups
+    for g in range(groups):
+        sums = [
+            (acc_0[j, p] + acc_1[j, p]).astype(jnp.bfloat16)
+            for j in range(g * per_col, (g + 1) * per_col)
+        ]
+        part = lax.dot_general(
+            sums[0] if per_col == 1 else jnp.concatenate(sums, axis=1),
+            chosen[p, g],
+            (((1,), (1,)), ((), ())),
+            preferred_element_type=jnp.float32,
+        )
+        total = part if total is None else total + part
     return times(total, correlation[p], False)
 
 
@@ -427,9 +439,10 @@
     first_two[1] = nn(inverse_first, upper.T)
     t_s = -nn(t_x, nn(z1.T, inverse_first))
     p_s = nn(t_s, g01) + nn(t_x, g11)
+    back = nn(nn(upper, inverse_first.T), inverse_first)
+    across = nn(t_s, joint[:m, :m]) + nn(t_x, joint[m:, :m])
     parts[0] = t_x
-    parts[1] = nt(p_s, t_s) + nt(nn(t_s, g11), t_x)
-    back = nn(nn(upper, inverse_first.T), inverse_first)
+    parts[1] = nt(p_s, t_s) + nt(nn(t_s, g11), t_x) - nt(across, back)
     basis[...] = nn(jnp.concatenate([t_s, t_x], axis=1), jnp.concatenate([turned[...], first[...]]))
     known[...] = nn(
         jnp.concatenate([t_s, t_x, -back], axis=1),
@@ -556,13 +569,12 @@
         )
         neighbors.append(found[0])
     own = neighbors[0][0, :points]
-    coarse_count = geometry.coarse_count
     chosen, payload, first = call(
         functools.partial(first_image_kernel, geometry, coarse_pieces),
         [(a, VMEM) for a in coarse]
         + [(acc[0], VMEM), (acc[1], VMEM), (own, SMEM), (correlations, VMEM), (turned, VMEM), (shifted, VMEM)],
         [
-            shaped((points, coarse_count, band, band), jnp.bfloat16),
+            shaped((points, cols, band, per_col * band), jnp.bfloat16),
             shaped((half, band), jnp.bfloat16),
             shaped(turned.shape),
         ],

time: 117 us -> 116 us (level)
  no operation moved by 1% of the time
where the time goes in v3:
time: 116 us; the launch traced here: 115 us
  waiting for transfers between devices  46.3 us (40%)
  starting transfers between devices  44.3 us (38%)
  Pallas kernels  20.6 us (18%)
  local copies, waits for them, and re-layouts  3.26 us (3%)
    ppermute x44, starting transfers between devices, permute(): return lax.ppermute(value, AXES, pairs)  36.3 us
    ppermute x44, waiting for transfers between devices, permute(): return lax.ppermute(value, AXES, pairs)  23.8 us
    ppermute x10, waiting for transfers between devices, exchange(): return lax.ppermute(value, AXES, pairs)  22.5 us
    pallas_call x15, Pallas kernels, call(): pl.pallas_call(kernel, in_specs=[spec for _, spec in inputs], out_shape=o...  20.6 us
    ppermute x10, starting transfers between devices, exchange(): return lax.ppermute(value, AXES, pairs)  7.93 us
    unnamed x23, local copies, waits for them, and re-layouts  3.22 us
  transfers between devices with their start and end apart: 54, of which 18 were waited for; matrix products, arithmetic and copies ran while one was open for 0% of the time, Pallas kernels for 14%

profile of v3, /device:TPU:0, one launch (start us, length us, event | category | flops | bytes accessed | tf_op | source)
XLA Modules:
  0.0 115.5 jit_solution(18050613220217085693)
XLA Ops:
  1.3 0.9 copy-done.1
  2.2 0.9 copy-done.3
  3.8 3.1 %collective-permute-start.10 = (bf16[272,128]{1,0:T(8,128)(2,1)S(1)}, bf16[272,128]{1,0:T(8,128)(2,1)S(1)}, u32[]{:S(2)}, u32[]{:S(2)}) collective-permute-start(bf16[272,128]{1,0:T(8,128)(2,1)S(1)} %shard_map.77.refs_0_), channel_id=1, source_target_pairs={{0,8},{1,9},{2,10},{3,11},{4,12},{5,13},{6,14},{7,15},{8,16},{9,17... | collective-permute-start | bytes 208904 | tf_op jit(solution)/shard_map/ppermute | solution.py:109
  7.0 2.1 %collective-permute-start.11 = (bf16[272,128]{1,0:T(8,128)(2,1)S(1)}, bf16[272,128]{1,0:T(8,128)(2,1)S(1)}, u32[]{:S(2)}, u32[]{:S(2)}) collective-permute-start(bf16[272,128]{1,0:T(8,128)(2,1)S(1)} %shard_map.77.refs_0_), channel_id=1, source_target_pairs={{0,24},{1,25},{2,26},{3,27},{4,28},{5,29},{6,30},{7,31},{8,0},{9,1... | collective-permute-start | bytes 208904 | tf_op jit(solution)/shard_map/ppermute | solution.py:109
  9.1 0.9 collective-permute-start.12
  10.0 1.5 %collective-permute-start.19 = (bf16[272,128]{1,0:T(8,128)(2,1)S(1)}, bf16[272,128]{1,0:T(8,128)(2,1)S(1)}, u32[]{:S(2)}, u32[]{:S(2)}) collective-permute-start(bf16[272,128]{1,0:T(8,128)(2,1)S(1)} %shard_map.77.refs_0_), channel_id=1, source_target_pairs={{0,2},{1,3},{2,0},{3,1},{4,6},{5,7},{6,4},{7,5},{8,10},{9,11},{10,... | collective-permute-start | bytes 208904 | tf_op jit(solution)/shard_map/ppermute | solution.py:109
  11.5 1.6 %collective-permute-start = (bf16[128,256]{1,0:T(8,128)(2,1)S(1)}, bf16[128,256]{1,0:T(8,128)(2,1)S(1)}, u32[]{:S(2)}, u32[]{:S(2)}) collective-permute-start(bf16[128,256]{1,0:T(8,128)(2,1)S(1)} %copy-done.6), channel_id=1, source_target_pairs={{0,8},{1,9},{2,10},{3,11},{4,12},{5,13},{6,14},{7,15},{8,16},{9,17... | collective-permute-start | bytes 196616 | tf_op jit(solution)/shard_map/ppermute | solution.py:109
  13.8 3.8 %collective-permute-done = bf16[128,256]{1,0:T(8,128)(2,1)S(1)} collective-permute-done((bf16[128,256]{1,0:T(8,128)(2,1)S(1)}, bf16[128,256]{1,0:T(8,128)(2,1)S(1)}, u32[]{:S(2)}, u32[]{:S(2)}) %collective-permute-start) | collective-permute-done | bytes 65568 | tf_op jit(solution)/shard_map/ppermute | solution.py:109
  17.6 1.5 %collective-permute-start.20 = (bf16[272,128]{1,0:T(8,128)(2,1)S(1)}, bf16[272,128]{1,0:T(8,128)(2,1)S(1)}, u32[]{:S(2)}, u32[]{:S(2)}) collective-permute-start(bf16[272,128]{1,0:T(8,128)(2,1)S(1)} %shard_map.77.refs_0_), channel_id=1, source_target_pairs={{0,4},{1,5},{2,6},{3,7},{4,0},{5,1},{6,2},{7,3},{8,12},{9,13},{10,... | collective-permute-start | bytes 208904 | tf_op jit(solution)/shard_map/ppermute | solution.py:109
  20.2 1.3 %collective-permute-start.2 = (bf16[128,256]{1,0:T(8,128)(2,1)S(1)}, bf16[128,256]{1,0:T(8,128)(2,1)S(1)}, u32[]{:S(2)}, u32[]{:S(2)}) collective-permute-start(bf16[128,256]{1,0:T(8,128)(2,1)S(1)} %copy-done.6), channel_id=1, source_target_pairs={{0,16},{1,17},{2,18},{3,19},{4,20},{5,21},{6,22},{7,23},{8,24},{9,... | collective-permute-start | bytes 196616 | tf_op jit(solution)/shard_map/ppermute | solution.py:109
  21.5 2.6 %collective-permute-done.1 = bf16[128,256]{1,0:T(8,128)(2,1)S(1)} collective-permute-done((bf16[128,256]{1,0:T(8,128)(2,1)S(1)}, bf16[128,256]{1,0:T(8,128)(2,1)S(1)}, u32[]{:S(2)}, u32[]{:S(2)}) %collective-permute-start.1) | collective-permute-done | bytes 65568 | tf_op jit(solution)/shard_map/ppermute | solution.py:109
  24.1 1.3 %collective-permute-done.2 = bf16[128,256]{1,0:T(8,128)(2,1)S(1)} collective-permute-done((bf16[128,256]{1,0:T(8,128)(2,1)S(1)}, bf16[128,256]{1,0:T(8,128)(2,1)S(1)}, u32[]{:S(2)}, u32[]{:S(2)}) %collective-permute-start.2) | collective-permute-done | bytes 65568 | tf_op jit(solution)/shard_map/ppermute | solution.py:109
  25.4 2.6 %collective-permute-start.17 = (bf16[816,128]{1,0:T(8,128)(2,1)S(1)}, bf16[816,128]{1,0:T(8,128)(2,1)S(1)}, u32[]{:S(2)}, u32[]{:S(2)}) collective-permute-start(bf16[816,128]{1,0:T(8,128)(2,1)S(1)} %constant_dynamic-update-slice_fusion.4.refs_4_), channel_id=1, source_target_pairs={{0,2},{1,3},{2,0},{3,1},{4,6},{5,7},{6,4},{7,5},{8,10},{9,11},{10,... | collective-permute-start | bytes 626696 | tf_op jit(solution)/shard_map/ppermute | solution.py:109
  28.6 1.6 %collective-permute-start.13 = (bf16[816,128]{1,0:T(8,128)(2,1)S(1)}, bf16[816,128]{1,0:T(8,128)(2,1)S(1)}, u32[]{:S(2)}, u32[]{:S(2)}) collective-permute-start(bf16[816,128]{1,0:T(8,128)(2,1)S(1)} %constant_dynamic-update-slice_fusion.4.refs_4_), channel_id=1, source_target_pairs={{0,4},{1,5},{2,6},{3,7},{4,0},{5,1},{6,2},{7,3},{8,12},{9,13},{10,... | collective-permute-start | bytes 626696 | tf_op jit(solution)/shard_map/ppermute | solution.py:109
  30.6 1.2 %collective-permute-done.25.refs_8_ = bf16[272,128]{1,0:T(8,128)(2,1)S(1)} collective-permute-done((bf16[272,128]{1,0:T(8,128)(2,1)S(1)}, bf16[272,128]{1,0:T(8,128)(2,1)S(1)}, u32[]{:S(2)}, u32[]{:S(2)}) %collective-permute-start.25) | collective-permute-done | bytes 69664 | tf_op jit(solution)/shard_map/ppermute | solution.py:109
  31.8 1.7 %collective-permute-start.3 = (bf16[512,256]{1,0:T(8,128)(2,1)S(1)}, bf16[512,256]{1,0:T(8,128)(2,1)S(1)}, u32[]{:S(2)}, u32[]{:S(2)}) collective-permute-start(bf16[512,256]{1,0:T(8,128)(2,1)S(1)} %constant_dynamic-update-slice_fusion.refs_0_), channel_id=1, source_target_pairs={{0,2},{1,3},{2,0},{3,1},{4,6},{5,7},{6,4},{7,5},{8,10},{9,11},{10,... | collective-permute-start | bytes 786440 | tf_op jit(solution)/shard_map/ppermute | solution.py:109
  33.6 1.4 %collective-permute-start.4 = (bf16[512,256]{1,0:T(8,128)(2,1)S(1)}, bf16[512,256]{1,0:T(8,128)(2,1)S(1)}, u32[]{:S(2)}, u32[]{:S(2)}) collective-permute-start(bf16[512,256]{1,0:T(8,128)(2,1)S(1)} %constant_dynamic-update-slice_fusion.refs_0_), channel_id=1, source_target_pairs={{0,4},{1,5},{2,6},{3,7},{4,0},{5,1},{6,2},{7,3},{8,12},{9,13},{10,... | collective-permute-start | bytes 786440 | tf_op jit(solution)/shard_map/ppermute | solution.py:109
  34.9 2.1 %collective-permute-start.5 = (bf16[512,256]{1,0:T(8,128)(2,1)S(1)}, bf16[512,256]{1,0:T(8,128)(2,1)S(1)}, u32[]{:S(2)}, u32[]{:S(2)}) collective-permute-start(bf16[512,256]{1,0:T(8,128)(2,1)S(1)} %constant_dynamic-update-slice_fusion.refs_0_), channel_id=1, source_target_pairs={{0,6},{1,7},{2,4},{3,5},{4,2},{5,3},{6,0},{7,1},{8,14},{9,15},{10,... | collective-permute-start | bytes 786440 | tf_op jit(solution)/shard_map/ppermute | solution.py:109
  37.1 4.1 %collective-permute-done.13.refs_0_ = bf16[816,128]{1,0:T(8,128)(2,1)S(1)} collective-permute-done((bf16[816,128]{1,0:T(8,128)(2,1)S(1)}, bf16[816,128]{1,0:T(8,128)(2,1)S(1)}, u32[]{:S(2)}, u32[]{:S(2)}) %collective-permute-start.13) | collective-permute-done | bytes 208928 | tf_op jit(solution)/shard_map/ppermute | solution.py:109
  41.7 2.0 %shard_map.78 = (f32[8,4,64,128]{3,2,1,0:T(8,128)S(1)}, f32[8,4,64,128]{3,2,1,0:T(8,128)S(1)}, s32[1,128]{1,0:T(1,128)S(1)}) custom-call(bf16[272,128]{1,0:T(8,128)(2,1)S(1)} %shard_map.77.refs_0_, bf16[272,128]{1,0:T(8,128)(2,1)S(1)} %collective-permute-done.19.refs_1_, bf16[272,128]{1,0:T(8,128)(2,1)S(1)} %collective-permute-done.20.refs_2_, ...), custom_call_target="tpu_custom_call" | custom-call | flops 2500000000 | tf_op jit(solution)/shard_map/pallas_call | solution.py:478
  44.2 7.4 %collective-permute-done.4.refs_2_ = bf16[512,256]{1,0:T(8,128)(2,1)S(1)} collective-permute-done((bf16[512,256]{1,0:T(8,128)(2,1)S(1)}, bf16[512,256]{1,0:T(8,128)(2,1)S(1)}, u32[]{:S(2)}, u32[]{:S(2)}) %collective-permute-start.4) | collective-permute-done | bytes 262176 | tf_op jit(solution)/shard_map/ppermute | solution.py:109
  52.7 1.5 %shard_map.79 = (f32[8,4,64,128]{3,2,1,0:T(8,128)S(1)}, f32[8,4,64,128]{3,2,1,0:T(8,128)S(1)}, s32[1,128]{1,0:T(1,128)S(1)}) custom-call(bf16[816,128]{1,0:T(8,128)(2,1)S(1)} %collective-permute-done.17.refs_0_, bf16[816,128]{1,0:T(8,128)(2,1)S(1)} %collective-permute-done.18.refs_1_, ...), custom_call_target="tpu_custom_call", output_to_operand_aliasing={{0}: (3, {}), {1}: (4, {})} | custom-call | flops 500000000 | tf_op jit(solution)/shard_map/pallas_call | solution.py:478
  54.3 1.9 %shard_map.80 = (f32[8,4,64,128]{3,2,1,0:T(8,128)S(1)}, f32[8,4,64,128]{3,2,1,0:T(8,128)S(1)}, s32[1,128]{1,0:T(1,128)S(1)}) custom-call(bf16[816,128]{1,0:T(8,128)(2,1)S(1)} %collective-permute-done.13.refs_0_, bf16[816,128]{1,0:T(8,128)(2,1)S(1)} %collective-permute-done.14.refs_1_, ...), custom_call_target="tpu_custom_call", output_to_operand_aliasing={{0}: (5, {}), {1}: (6, {})} | custom-call | flops 1000000000 | tf_op jit(solution)/shard_map/pallas_call | solution.py:478
  56.3 2.4 %shard_map.81 = (bf16[4,4,128,256]{3,2,1,0:T(8,128)(2,1)S(1)}, bf16[256,128]{1,0:T(8,128)(2,1)S(1)}, f32[64,512]{1,0:T(8,128)S(1)}) custom-call(bf16[512,256]{1,0:T(8,128)(2,1)S(1)} %constant_dynamic-update-slice_fusion.refs_0_, bf16[512,256]{1,0:T(8,128)(2,1)S(1)} %collective-permute-done.3.refs_1_, bf16[512,256]{1,0:T(8,128)(2,1)S(1)} %collective-permute-done.4.refs_2_, ...), custom_call_target="tpu_custom_call" | custom-call | flops 1500000000 | tf_op jit(solution)/shard_map/pallas_call | solution.py:478
  59.8 3.3 %collective-permute-start.28 = (bf16[256,128]{1,0:T(8,128)(2,1)S(1)}, bf16[256,128]{1,0:T(8,128)(2,1)S(1)}, u32[]{:S(2)}, u32[]{:S(2)}) collective-permute-start(bf16[256,128]{1,0:T(8,128)(2,1)S(1)} %get-tuple-element.37.refs_0_), channel_id=1, source_target_pairs={{0,24},{1,25},{2,26},{3,27},{4,28},{5,29},{6,30},{7,31},{8,0},{9,1... | collective-permute-start | bytes 196616 | tf_op jit(solution)/shard_map/ppermute | solution.py:109
  63.7 1.3 %collective-permute-start.37 = (bf16[256,128]{1,0:T(8,128)(2,1)S(1)}, bf16[256,128]{1,0:T(8,128)(2,1)S(1)}, u32[]{:S(2)}, u32[]{:S(2)}) collective-permute-start(bf16[256,128]{1,0:T(8,128)(2,1)S(1)} %get-tuple-element.37.refs_0_), channel_id=1, source_target_pairs={{0,4},{1,5},{2,6},{3,7},{4,0},{5,1},{6,2},{7,3},{8,12},{9,13},{10,... | collective-permute-start | bytes 196616 | tf_op jit(solution)/shard_map/ppermute | solution.py:109
  65.0 1.0 collective-permute-done.27
  66.0 1.3 %collective-permute-start.38 = (bf16[256,128]{1,0:T(8,128)(2,1)S(1)}, bf16[256,128]{1,0:T(8,128)(2,1)S(1)}, u32[]{:S(2)}, u32[]{:S(2)}) collective-permute-start(bf16[256,128]{1,0:T(8,128)(2,1)S(1)} %get-tuple-element.37.refs_0_), channel_id=1, source_target_pairs={{0,6},{1,7},{2,4},{3,5},{4,2},{5,3},{6,0},{7,1},{8,14},{9,15},{10,... | collective-permute-start | bytes 196616 | tf_op jit(solution)/shard_map/ppermute | solution.py:109
  68.0 3.6 %collective-permute-done.50 = f32[128,128]{1,0:T(8,128)S(1)} collective-permute-done((f32[128,128]{1,0:T(8,128)S(1)}, f32[128,128]{1,0:T(8,128)S(1)}, u32[]{:S(2)}, u32[]{:S(2)}) %collective-permute-start.50) | collective-permute-done | bytes 65568 | tf_op jit(solution)/shard_map/ppermute | solution.py:160
  71.7 2.3 %collective-permute-start.51 = (f32[128,128]{1,0:T(8,128)S(1)}, f32[128,128]{1,0:T(8,128)S(1)}, u32[]{:S(2)}, u32[]{:S(2)}) collective-permute-start(f32[128,128]{1,0:T(8,128)S(1)} %add.38), channel_id=1, source_target_pairs={{0,16},{1,17},{2,18},{3,19},{4,20},{5,21},{6,22},{7,23},{8,24},{9,... | collective-permute-start | bytes 196616 | tf_op jit(solution)/shard_map/ppermute | solution.py:160
  74.7 1.3 %collective-permute-start.30 = (bf16[768,128]{1,0:T(8,128)(2,1)S(1)}, bf16[768,128]{1,0:T(8,128)(2,1)S(1)}, u32[]{:S(2)}, u32[]{:S(2)}) collective-permute-start(bf16[768,128]{1,0:T(8,128)(2,1)S(1)} %constant_dynamic-update-slice_fusion.7.refs_4_), channel_id=1, source_target_pairs={{0,4},{1,5},{2,6},{3,7},{4,0},{5,1},{6,2},{7,3},{8,12},{9,13},{10,... | collective-permute-start | bytes 589832 | tf_op jit(solution)/shard_map/ppermute | solution.py:109
  76.0 1.6 %collective-permute-start.31 = (bf16[768,128]{1,0:T(8,128)(2,1)S(1)}, bf16[768,128]{1,0:T(8,128)(2,1)S(1)}, u32[]{:S(2)}, u32[]{:S(2)}) collective-permute-start(bf16[768,128]{1,0:T(8,128)(2,1)S(1)} %constant_dynamic-update-slice_fusion.7.refs_4_), channel_id=1, source_target_pairs={{0,6},{1,7},{2,4},{3,5},{4,2},{5,3},{6,0},{7,1},{8,14},{9,15},{10,... | collective-permute-start | bytes 589832 | tf_op jit(solution)/shard_map/ppermute | solution.py:109
  78.4 1.4 %collective-permute-start.52 = (f32[128,128]{1,0:T(8,128)S(1)}, f32[128,128]{1,0:T(8,128)S(1)}, u32[]{:S(2)}, u32[]{:S(2)}) collective-permute-start(f32[128,128]{1,0:T(8,128)S(1)} %add.39), channel_id=1, source_target_pairs={{0,2},{1,3},{2,0},{3,1},{4,6},{5,7},{6,4},{7,5},{8,10},{9,11},{10,... | collective-permute-start | bytes 196616 | tf_op jit(solution)/shard_map/ppermute | solution.py:160
  79.8 7.0 %collective-permute-done.52 = f32[128,128]{1,0:T(8,128)S(1)} collective-permute-done((f32[128,128]{1,0:T(8,128)S(1)}, f32[128,128]{1,0:T(8,128)S(1)}, u32[]{:S(2)}, u32[]{:S(2)}) %collective-permute-start.52) | collective-permute-done | bytes 65568 | tf_op jit(solution)/shard_map/ppermute | solution.py:160
  86.8 1.2 %collective-permute-done.42.refs_8_ = bf16[256,128]{1,0:T(8,128)(2,1)S(1)} collective-permute-done((bf16[256,128]{1,0:T(8,128)(2,1)S(1)}, bf16[256,128]{1,0:T(8,128)(2,1)S(1)}, u32[]{:S(2)}, u32[]{:S(2)}) %collective-permute-start.42) | collective-permute-done | bytes 65568 | tf_op jit(solution)/shard_map/ppermute | solution.py:109
  88.1 1.5 %collective-permute-start.53 = (f32[128,128]{1,0:T(8,128)S(1)}, f32[128,128]{1,0:T(8,128)S(1)}, u32[]{:S(2)}, u32[]{:S(2)}) collective-permute-start(f32[128,128]{1,0:T(8,128)S(1)} %add.40), channel_id=1, source_target_pairs={{0,4},{1,5},{2,6},{3,7},{4,0},{5,1},{6,2},{7,3},{8,12},{9,13},{10,... | collective-permute-start | bytes 196616 | tf_op jit(solution)/shard_map/ppermute | solution.py:160
  90.1 1.5 %shard_map.82 = (f32[8,4,64,128]{3,2,1,0:T(8,128)S(1)}, f32[8,4,64,128]{3,2,1,0:T(8,128)S(1)}) custom-call(bf16[256,128]{1,0:T(8,128)(2,1)S(1)} %get-tuple-element.37.refs_0_, bf16[256,128]{1,0:T(8,128)(2,1)S(1)} %collective-permute-done.36.refs_1_, bf16[256,128]{1,0:T(8,128)(2,1)S(1)} %collective-permute-done.37.refs_2_, ...), custom_call_target="tpu_custom_call" | custom-call | flops 2500000000 | tf_op jit(solution)/shard_map/pallas_call | solution.py:478
  91.6 1.2 %shard_map.83 = (f32[8,4,64,128]{3,2,1,0:T(8,128)S(1)}, f32[8,4,64,128]{3,2,1,0:T(8,128)S(1)}) custom-call(bf16[768,128]{1,0:T(8,128)(2,1)S(1)} %collective-permute-done.34.refs_0_, bf16[768,128]{1,0:T(8,128)(2,1)S(1)} %collective-permute-done.35.refs_1_, ...), custom_call_target="tpu_custom_call", output_to_operand_aliasing={{0}: (3, {}), {1}: (4, {})} | custom-call | flops 500000000 | tf_op jit(solution)/shard_map/pallas_call | solution.py:478
  92.9 1.6 %shard_map.84 = (f32[8,4,64,128]{3,2,1,0:T(8,128)S(1)}, f32[8,4,64,128]{3,2,1,0:T(8,128)S(1)}) custom-call(bf16[768,128]{1,0:T(8,128)(2,1)S(1)} %collective-permute-done.30.refs_0_, bf16[768,128]{1,0:T(8,128)(2,1)S(1)} %collective-permute-done.31.refs_1_, ...), custom_call_target="tpu_custom_call", output_to_operand_aliasing={{0}: (5, {}), {1}: (6, {})} | custom-call | flops 1000000000 | tf_op jit(solution)/shard_map/pallas_call | solution.py:478
  94.5 1.4 %shard_map.85 = (f32[64,512]{1,0:T(8,128)S(1)}, f32[64,64]{1,0:T(8,128)S(1)}) custom-call(f32[8,4,64,128]{3,2,1,0:T(8,128)S(1)} %get-tuple-element.44.acc_0, f32[8,4,64,128]{3,2,1,0:T(8,128)S(1)} %get-tuple-element.45.acc_1, bf16[4,4,128,256]{3,2,1,0:T(8,128)(2,1)S(1)} %get-tuple-element.46.chosen, bf16[4,128,128]{2,1,0:T(8,128)(2,1)S(1)} %copy-done.2, ...), custom_call_target="tpu_custom_call" | custom-call | flops 1500000000 | tf_op jit(solution)/shard_map/pallas_call | solution.py:478
  97.7 0.9 shard_map.87.given
  98.6 2.6 %collective-permute-done.45 = f32[64,64]{1,0:T(8,128)S(1)} collective-permute-done((f32[64,64]{1,0:T(8,128)S(1)}, f32[64,64]{1,0:T(8,128)S(1)}, u32[]{:S(2)}, u32[]{:S(2)}) %collective-permute-start.45) | collective-permute-done | bytes 16416 | tf_op jit(solution)/shard_map/ppermute | solution.py:160
  101.9 1.0 shard_map.88
  103.0 2.1 %collective-permute-done.46 = f32[64,64]{1,0:T(8,128)S(1)} collective-permute-done((f32[64,64]{1,0:T(8,128)S(1)}, f32[64,64]{1,0:T(8,128)S(1)}, u32[]{:S(2)}, u32[]{:S(2)}) %collective-permute-start.46) | collective-permute-done | bytes 16416 | tf_op jit(solution)/shard_map/ppermute | solution.py:160
  106.2 4.0 %collective-permute-done.47 = f32[64,64]{1,0:T(8,128)S(1)} collective-permute-done((f32[64,64]{1,0:T(8,128)S(1)}, f32[64,64]{1,0:T(8,128)S(1)}, u32[]{:S(2)}, u32[]{:S(2)}) %collective-permute-start.47) | collective-permute-done | bytes 16416 | tf_op jit(solution)/shard_map/ppermute | solution.py:160
  110.8 1.8 %shard_map.90 = (f32[2,64,64]{2,1,0:T(8,128)S(1)}, f32[2,64,64]{2,1,0:T(8,128)S(1)}, f32[64,512]{1,0:T(8,128)S(1)}, f32[64,512]{1,0:T(8,128)S(1)}) custom-call(f32[128,128]{1,0:T(8,128)S(1)} %add.41.joint, f32[64,192]{1,0:T(8,128)S(1)} %get-tuple-element.49.one, f32[64,128]{1,0:T(8,128)S(1)} %shard_map.89.given, f32[64,512]{1,0:T(8,128)S(1)} %bitcast.10, ...), custom_call_target="tpu_custom_call" | custom-call | flops 1500000000 | tf_op jit(solution)/shard_map/pallas_call | solution.py:478
  112.7 1.5 %collective-permute-done.48.other = f32[64,64]{1,0:T(8,128)S(1)} collective-permute-done((f32[64,64]{1,0:T(8,128)S(1)}, f32[64,64]{1,0:T(8,128)S(1)}, u32[]{:S(2)}, u32[]{:S(2)}) %collective-permute-start.48) | collective-permute-done | bytes 16416 | tf_op jit(solution)/shard_map/ppermute | solution.py:160
  114.2 1.3 %shard_map.91 = (f32[64,512]{1,0:T(8,128)}, f32[3,64,64]{2,1,0:T(8,128)}) custom-call(f32[64,64]{1,0:T(8,128)S(1)} %add.36.gram, f32[64,64]{1,0:T(8,128)S(1)} %collective-permute-done.48.other, f32[2,64,64]{2,1,0:T(8,128)S(1)} %get-tuple-element.52.first_two, f32[2,64,64]{2,1,0:T(8,128)S(1)} %get-tuple-element.53.parts, ...), custom_call_target="tpu_custom_call" | custom-call | flops 1000000000 | tf_op jit(solution)/shard_map/pallas_call | solution.py:478
  (113 shorter events, 14.9 us)
Async XLA Ops:
  3.8 15.2 %collective-permute-start.10 = (bf16[272,128]{1,0:T(8,128)(2,1)S(1)}, bf16[272,128]{1,0:T(8,128)(2,1)S(1)}, u32[]{:S(2)}, u32[]{:S(2)}) collective-permute-start(bf16[272,128]{1,0:T(8,128)(2,1)S(1)} %shard_map.77.refs_0_), channel_id=1, source_target_pairs={{0,8},{1,9},{2,10},{3,11},{4,12},{5,13},{6,14},{7,15},{8,16},{9,17... | collective-permute-start | bytes 208904 | tf_op jit(solution)/shard_map/ppermute | solution.py:109
  7.0 12.8 %collective-permute-start.11 = (bf16[272,128]{1,0:T(8,128)(2,1)S(1)}, bf16[272,128]{1,0:T(8,128)(2,1)S(1)}, u32[]{:S(2)}, u32[]{:S(2)}) collective-permute-start(bf16[272,128]{1,0:T(8,128)(2,1)S(1)} %shard_map.77.refs_0_), channel_id=1, source_target_pairs={{0,24},{1,25},{2,26},{3,27},{4,28},{5,29},{6,30},{7,31},{8,0},{9,1... | collective-permute-start | bytes 208904 | tf_op jit(solution)/shard_map/ppermute | solution.py:109
  9.1 11.1 %collective-permute-start.12 = (bf16[272,128]{1,0:T(8,128)(2,1)S(1)}, bf16[272,128]{1,0:T(8,128)(2,1)S(1)}, u32[]{:S(2)}, u32[]{:S(2)}) collective-permute-start(bf16[272,128]{1,0:T(8,128)(2,1)S(1)} %shard_map.77.refs_0_), channel_id=1, source_target_pairs={{0,16},{1,17},{2,18},{3,19},{4,20},{5,21},{6,22},{7,23},{8,24},{9,... | collective-permute-start | bytes 208904 | tf_op jit(solution)/shard_map/ppermute | solution.py:109
  10.0 15.4 %collective-permute-start.19 = (bf16[272,128]{1,0:T(8,128)(2,1)S(1)}, bf16[272,128]{1,0:T(8,128)(2,1)S(1)}, u32[]{:S(2)}, u32[]{:S(2)}) collective-permute-start(bf16[272,128]{1,0:T(8,128)(2,1)S(1)} %shard_map.77.refs_0_), channel_id=1, source_target_pairs={{0,2},{1,3},{2,0},{3,1},{4,6},{5,7},{6,4},{7,5},{8,10},{9,11},{10,... | collective-permute-start | bytes 208904 | tf_op jit(solution)/shard_map/ppermute | solution.py:109
  11.5 6.1 %collective-permute-start = (bf16[128,256]{1,0:T(8,128)(2,1)S(1)}, bf16[128,256]{1,0:T(8,128)(2,1)S(1)}, u32[]{:S(2)}, u32[]{:S(2)}) collective-permute-start(bf16[128,256]{1,0:T(8,128)(2,1)S(1)} %copy-done.6), channel_id=1, source_target_pairs={{0,8},{1,9},{2,10},{3,11},{4,12},{5,13},{6,14},{7,15},{8,16},{9,17... | collective-permute-start | bytes 196616 | tf_op jit(solution)/shard_map/ppermute | solution.py:109
  17.6 10.5 %collective-permute-start.20 = (bf16[272,128]{1,0:T(8,128)(2,1)S(1)}, bf16[272,128]{1,0:T(8,128)(2,1)S(1)}, u32[]{:S(2)}, u32[]{:S(2)}) collective-permute-start(bf16[272,128]{1,0:T(8,128)(2,1)S(1)} %shard_map.77.refs_0_), channel_id=1, source_target_pairs={{0,4},{1,5},{2,6},{3,7},{4,0},{5,1},{6,2},{7,3},{8,12},{9,13},{10,... | collective-permute-start | bytes 208904 | tf_op jit(solution)/shard_map/ppermute | solution.py:109
  19.1 9.2 %collective-permute-start.21 = (bf16[272,128]{1,0:T(8,128)(2,1)S(1)}, bf16[272,128]{1,0:T(8,128)(2,1)S(1)}, u32[]{:S(2)}, u32[]{:S(2)}) collective-permute-start(bf16[272,128]{1,0:T(8,128)(2,1)S(1)} %shard_map.77.refs_0_), channel_id=1, source_target_pairs={{0,6},{1,7},{2,4},{3,5},{4,2},{5,3},{6,0},{7,1},{8,14},{9,15},{10,... | collective-permute-start | bytes 208904 | tf_op jit(solution)/shard_map/ppermute | solution.py:109
  19.7 4.3 %collective-permute-start.1 = (bf16[128,256]{1,0:T(8,128)(2,1)S(1)}, bf16[128,256]{1,0:T(8,128)(2,1)S(1)}, u32[]{:S(2)}, u32[]{:S(2)}) collective-permute-start(bf16[128,256]{1,0:T(8,128)(2,1)S(1)} %copy-done.6), channel_id=1, source_target_pairs={{0,24},{1,25},{2,26},{3,27},{4,28},{5,29},{6,30},{7,31},{8,0},{9,1... | collective-permute-start | bytes 196616 | tf_op jit(solution)/shard_map/ppermute | solution.py:109
  20.2 5.2 %collective-permute-start.2 = (bf16[128,256]{1,0:T(8,128)(2,1)S(1)}, bf16[128,256]{1,0:T(8,128)(2,1)S(1)}, u32[]{:S(2)}, u32[]{:S(2)}) collective-permute-start(bf16[128,256]{1,0:T(8,128)(2,1)S(1)} %copy-done.6), channel_id=1, source_target_pairs={{0,16},{1,17},{2,18},{3,19},{4,20},{5,21},{6,22},{7,23},{8,24},{9,... | collective-permute-start | bytes 196616 | tf_op jit(solution)/shard_map/ppermute | solution.py:109
  24.1 4.5 %collective-permute-start.22 = (bf16[272,128]{1,0:T(8,128)(2,1)S(1)}, bf16[272,128]{1,0:T(8,128)(2,1)S(1)}, u32[]{:S(2)}, u32[]{:S(2)}) collective-permute-start(bf16[272,128]{1,0:T(8,128)(2,1)S(1)} %shard_map.77.refs_0_), channel_id=1, source_target_pairs={{0,1},{1,0},{2,3},{3,2},{4,5},{5,4},{6,7},{7,6},{8,9},{9,8},{10,11... | collective-permute-start | bytes 208904 | tf_op jit(solution)/shard_map/ppermute | solution.py:109
  25.4 8.2 %collective-permute-start.26 = (bf16[816,128]{1,0:T(8,128)(2,1)S(1)}, bf16[816,128]{1,0:T(8,128)(2,1)S(1)}, u32[]{:S(2)}, u32[]{:S(2)}) collective-permute-start(bf16[816,128]{1,0:T(8,128)(2,1)S(1)} %constant_dynamic-update-slice_fusion.4.refs_4_), channel_id=1, source_target_pairs={{0,1},{1,0},{2,3},{3,2},{4,5},{5,4},{6,7},{7,6},{8,9},{9,8},{10,11... | collective-permute-start | bytes 626696 | tf_op jit(solution)/shard_map/ppermute | solution.py:109
  25.4 9.5 %collective-permute-start.17 = (bf16[816,128]{1,0:T(8,128)(2,1)S(1)}, bf16[816,128]{1,0:T(8,128)(2,1)S(1)}, u32[]{:S(2)}, u32[]{:S(2)}) collective-permute-start(bf16[816,128]{1,0:T(8,128)(2,1)S(1)} %constant_dynamic-update-slice_fusion.4.refs_4_), channel_id=1, source_target_pairs={{0,2},{1,3},{2,0},{3,1},{4,6},{5,7},{6,4},{7,5},{8,10},{9,11},{10,... | collective-permute-start | bytes 626696 | tf_op jit(solution)/shard_map/ppermute | solution.py:109
  28.6 12.6 %collective-permute-start.13 = (bf16[816,128]{1,0:T(8,128)(2,1)S(1)}, bf16[816,128]{1,0:T(8,128)(2,1)S(1)}, u32[]{:S(2)}, u32[]{:S(2)}) collective-permute-start(bf16[816,128]{1,0:T(8,128)(2,1)S(1)} %constant_dynamic-update-slice_fusion.4.refs_4_), channel_id=1, source_target_pairs={{0,4},{1,5},{2,6},{3,7},{4,0},{5,1},{6,2},{7,3},{8,12},{9,13},{10,... | collective-permute-start | bytes 626696 | tf_op jit(solution)/shard_map/ppermute | solution.py:109
  30.2 11.0 %collective-permute-start.14 = (bf16[816,128]{1,0:T(8,128)(2,1)S(1)}, bf16[816,128]{1,0:T(8,128)(2,1)S(1)}, u32[]{:S(2)}, u32[]{:S(2)}) collective-permute-start(bf16[816,128]{1,0:T(8,128)(2,1)S(1)} %constant_dynamic-update-slice_fusion.4.refs_4_), channel_id=1, source_target_pairs={{0,6},{1,7},{2,4},{3,5},{4,2},{5,3},{6,0},{7,1},{8,14},{9,15},{10,... | collective-permute-start | bytes 626696 | tf_op jit(solution)/shard_map/ppermute | solution.py:109
  31.8 12.4 %collective-permute-start.3 = (bf16[512,256]{1,0:T(8,128)(2,1)S(1)}, bf16[512,256]{1,0:T(8,128)(2,1)S(1)}, u32[]{:S(2)}, u32[]{:S(2)}) collective-permute-start(bf16[512,256]{1,0:T(8,128)(2,1)S(1)} %constant_dynamic-update-slice_fusion.refs_0_), channel_id=1, source_target_pairs={{0,2},{1,3},{2,0},{3,1},{4,6},{5,7},{6,4},{7,5},{8,10},{9,11},{10,... | collective-permute-start | bytes 786440 | tf_op jit(solution)/shard_map/ppermute | solution.py:109
  33.6 18.1 %collective-permute-start.4 = (bf16[512,256]{1,0:T(8,128)(2,1)S(1)}, bf16[512,256]{1,0:T(8,128)(2,1)S(1)}, u32[]{:S(2)}, u32[]{:S(2)}) collective-permute-start(bf16[512,256]{1,0:T(8,128)(2,1)S(1)} %constant_dynamic-update-slice_fusion.refs_0_), channel_id=1, source_target_pairs={{0,4},{1,5},{2,6},{3,7},{4,0},{5,1},{6,2},{7,3},{8,12},{9,13},{10,... | collective-permute-start | bytes 786440 | tf_op jit(solution)/shard_map/ppermute | solution.py:109
  34.9 16.7 %collective-permute-start.5 = (bf16[512,256]{1,0:T(8,128)(2,1)S(1)}, bf16[512,256]{1,0:T(8,128)(2,1)S(1)}, u32[]{:S(2)}, u32[]{:S(2)}) collective-permute-start(bf16[512,256]{1,0:T(8,128)(2,1)S(1)} %constant_dynamic-update-slice_fusion.refs_0_), channel_id=1, source_target_pairs={{0,6},{1,7},{2,4},{3,5},{4,2},{5,3},{6,0},{7,1},{8,14},{9,15},{10,... | collective-permute-start | bytes 786440 | tf_op jit(solution)/shard_map/ppermute | solution.py:109
  41.2 11.0 %collective-permute-start.18 = (bf16[816,128]{1,0:T(8,128)(2,1)S(1)}, bf16[816,128]{1,0:T(8,128)(2,1)S(1)}, u32[]{:S(2)}, u32[]{:S(2)}) collective-permute-start(bf16[816,128]{1,0:T(8,128)(2,1)S(1)} %collective-permute-done.17.refs_0_), channel_id=1, source_target_pairs={{0,1},{1,0},{2,3},{3,2},{4,5},{5,4},{6,7},{7,6},{8,9},{9,8},{10,11... | collective-permute-start | bytes 626696 | tf_op jit(solution)/shard_map/ppermute | solution.py:109
  41.2 11.1 %collective-permute-start.15 = (bf16[816,128]{1,0:T(8,128)(2,1)S(1)}, bf16[816,128]{1,0:T(8,128)(2,1)S(1)}, u32[]{:S(2)}, u32[]{:S(2)}) collective-permute-start(bf16[816,128]{1,0:T(8,128)(2,1)S(1)} %collective-permute-done.13.refs_0_), channel_id=1, source_target_pairs={{0,1},{1,0},{2,3},{3,2},{4,5},{5,4},{6,7},{7,6},{8,9},{9,8},{10,11... | collective-permute-start | bytes 626696 | tf_op jit(solution)/shard_map/ppermute | solution.py:109
  44.2 12.0 %collective-permute-start.6 = (bf16[512,256]{1,0:T(8,128)(2,1)S(1)}, bf16[512,256]{1,0:T(8,128)(2,1)S(1)}, u32[]{:S(2)}, u32[]{:S(2)}) collective-permute-start(bf16[512,256]{1,0:T(8,128)(2,1)S(1)} %constant_dynamic-update-slice_fusion.refs_0_), channel_id=1, source_target_pairs={{0,1},{1,0},{2,3},{3,2},{4,5},{5,4},{6,7},{7,6},{8,9},{9,8},{10,11... | collective-permute-start | bytes 786440 | tf_op jit(solution)/shard_map/ppermute | solution.py:109
  51.7 2.6 %collective-permute-start.16 = (bf16[816,128]{1,0:T(8,128)(2,1)S(1)}, bf16[816,128]{1,0:T(8,128)(2,1)S(1)}, u32[]{:S(2)}, u32[]{:S(2)}) collective-permute-start(bf16[816,128]{1,0:T(8,128)(2,1)S(1)} %collective-permute-done.14.refs_1_), channel_id=1, source_target_pairs={{0,1},{1,0},{2,3},{3,2},{4,5},{5,4},{6,7},{7,6},{8,9},{9,8},{10,11... | collective-permute-start | bytes 626696 | tf_op jit(solution)/shard_map/ppermute | solution.py:109
  51.7 4.6 %collective-permute-start.7 = (bf16[512,256]{1,0:T(8,128)(2,1)S(1)}, bf16[512,256]{1,0:T(8,128)(2,1)S(1)}, u32[]{:S(2)}, u32[]{:S(2)}) collective-permute-start(bf16[512,256]{1,0:T(8,128)(2,1)S(1)} %collective-permute-done.3.refs_1_), channel_id=1, source_target_pairs={{0,1},{1,0},{2,3},{3,2},{4,5},{5,4},{6,7},{7,6},{8,9},{9,8},{10,11... | collective-permute-start | bytes 786440 | tf_op jit(solution)/shard_map/ppermute | solution.py:109
  52.2 4.1 %collective-permute-start.8 = (bf16[512,256]{1,0:T(8,128)(2,1)S(1)}, bf16[512,256]{1,0:T(8,128)(2,1)S(1)}, u32[]{:S(2)}, u32[]{:S(2)}) collective-permute-start(bf16[512,256]{1,0:T(8,128)(2,1)S(1)} %collective-permute-done.4.refs_2_), channel_id=1, source_target_pairs={{0,1},{1,0},{2,3},{3,2},{4,5},{5,4},{6,7},{7,6},{8,9},{9,8},{10,11... | collective-permute-start | bytes 786440 | tf_op jit(solution)/shard_map/ppermute | solution.py:109
  52.3 4.0 %collective-permute-start.9 = (bf16[512,256]{1,0:T(8,128)(2,1)S(1)}, bf16[512,256]{1,0:T(8,128)(2,1)S(1)}, u32[]{:S(2)}, u32[]{:S(2)}) collective-permute-start(bf16[512,256]{1,0:T(8,128)(2,1)S(1)} %collective-permute-done.5.refs_3_), channel_id=1, source_target_pairs={{0,1},{1,0},{2,3},{3,2},{4,5},{5,4},{6,7},{7,6},{8,9},{9,8},{10,11... | collective-permute-start | bytes 786440 | tf_op jit(solution)/shard_map/ppermute | solution.py:109
  59.1 4.6 %collective-permute-start.49 = (f32[128,128]{1,0:T(8,128)S(1)}, f32[128,128]{1,0:T(8,128)S(1)}, u32[]{:S(2)}, u32[]{:S(2)}) collective-permute-start(f32[128,128]{1,0:T(8,128)S(1)} %shard_map.86), channel_id=1, source_target_pairs={{0,1},{1,0},{2,3},{3,2},{4,5},{5,4},{6,7},{7,6},{8,9},{9,8},{10,11... | collective-permute-start | bytes 196616 | tf_op jit(solution)/shard_map/ppermute | solution.py:160
  59.2 6.8 %collective-permute-start.27 = (bf16[256,128]{1,0:T(8,128)(2,1)S(1)}, bf16[256,128]{1,0:T(8,128)(2,1)S(1)}, u32[]{:S(2)}, u32[]{:S(2)}) collective-permute-start(bf16[256,128]{1,0:T(8,128)(2,1)S(1)} %get-tuple-element.37.refs_0_), channel_id=1, source_target_pairs={{0,8},{1,9},{2,10},{3,11},{4,12},{5,13},{6,14},{7,15},{8,16},{9,17... | collective-permute-start | bytes 196616 | tf_op jit(solution)/shard_map/ppermute | solution.py:109
  59.8 7.6 %collective-permute-start.28 = (bf16[256,128]{1,0:T(8,128)(2,1)S(1)}, bf16[256,128]{1,0:T(8,128)(2,1)S(1)}, u32[]{:S(2)}, u32[]{:S(2)}) collective-permute-start(bf16[256,128]{1,0:T(8,128)(2,1)S(1)} %get-tuple-element.37.refs_0_), channel_id=1, source_target_pairs={{0,24},{1,25},{2,26},{3,27},{4,28},{5,29},{6,30},{7,31},{8,0},{9,1... | collective-permute-start | bytes 196616 | tf_op jit(solution)/shard_map/ppermute | solution.py:109
  63.1 8.6 %collective-permute-start.29 = (bf16[256,128]{1,0:T(8,128)(2,1)S(1)}, bf16[256,128]{1,0:T(8,128)(2,1)S(1)}, u32[]{:S(2)}, u32[]{:S(2)}) collective-permute-start(bf16[256,128]{1,0:T(8,128)(2,1)S(1)} %get-tuple-element.37.refs_0_), channel_id=1, source_target_pairs={{0,16},{1,17},{2,18},{3,19},{4,20},{5,21},{6,22},{7,23},{8,24},{9,... | collective-permute-start | bytes 196616 | tf_op jit(solution)/shard_map/ppermute | solution.py:109
  63.1 4.4 %collective-permute-start.36 = (bf16[256,128]{1,0:T(8,128)(2,1)S(1)}, bf16[256,128]{1,0:T(8,128)(2,1)S(1)}, u32[]{:S(2)}, u32[]{:S(2)}) collective-permute-start(bf16[256,128]{1,0:T(8,128)(2,1)S(1)} %get-tuple-element.37.refs_0_), channel_id=1, source_target_pairs={{0,2},{1,3},{2,0},{3,1},{4,6},{5,7},{6,4},{7,5},{8,10},{9,11},{10,... | collective-permute-start | bytes 196616 | tf_op jit(solution)/shard_map/ppermute | solution.py:109
  63.7 4.3 %collective-permute-start.37 = (bf16[256,128]{1,0:T(8,128)(2,1)S(1)}, bf16[256,128]{1,0:T(8,128)(2,1)S(1)}, u32[]{:S(2)}, u32[]{:S(2)}) collective-permute-start(bf16[256,128]{1,0:T(8,128)(2,1)S(1)} %get-tuple-element.37.refs_0_), channel_id=1, source_target_pairs={{0,4},{1,5},{2,6},{3,7},{4,0},{5,1},{6,2},{7,3},{8,12},{9,13},{10,... | collective-permute-start | bytes 196616 | tf_op jit(solution)/shard_map/ppermute | solution.py:109
  66.0 8.0 %collective-permute-start.38 = (bf16[256,128]{1,0:T(8,128)(2,1)S(1)}, bf16[256,128]{1,0:T(8,128)(2,1)S(1)}, u32[]{:S(2)}, u32[]{:S(2)}) collective-permute-start(bf16[256,128]{1,0:T(8,128)(2,1)S(1)} %get-tuple-element.37.refs_0_), channel_id=1, source_target_pairs={{0,6},{1,7},{2,4},{3,5},{4,2},{5,3},{6,0},{7,1},{8,14},{9,15},{10,... | collective-permute-start | bytes 196616 | tf_op jit(solution)/shard_map/ppermute | solution.py:109
  67.3 4.3 %collective-permute-start.50 = (f32[128,128]{1,0:T(8,128)S(1)}, f32[128,128]{1,0:T(8,128)S(1)}, u32[]{:S(2)}, u32[]{:S(2)}) collective-permute-start(f32[128,128]{1,0:T(8,128)S(1)} %add.37), channel_id=1, source_target_pairs={{0,8},{1,9},{2,10},{3,11},{4,12},{5,13},{6,14},{7,15},{8,0},{9,1},... | collective-permute-start | bytes 196616 | tf_op jit(solution)/shard_map/ppermute | solution.py:160
  67.4 7.3 %collective-permute-start.39 = (bf16[256,128]{1,0:T(8,128)(2,1)S(1)}, bf16[256,128]{1,0:T(8,128)(2,1)S(1)}, u32[]{:S(2)}, u32[]{:S(2)}) collective-permute-start(bf16[256,128]{1,0:T(8,128)(2,1)S(1)} %get-tuple-element.37.refs_0_), channel_id=1, source_target_pairs={{0,1},{1,0},{2,3},{3,2},{4,5},{5,4},{6,7},{7,6},{8,9},{9,8},{10,11... | collective-permute-start | bytes 196616 | tf_op jit(solution)/shard_map/ppermute | solution.py:109
  68.0 8.0 %collective-permute-start.40 = (bf16[256,128]{1,0:T(8,128)(2,1)S(1)}, bf16[256,128]{1,0:T(8,128)(2,1)S(1)}, u32[]{:S(2)}, u32[]{:S(2)}) collective-permute-start(bf16[256,128]{1,0:T(8,128)(2,1)S(1)} %collective-permute-done.36.refs_1_), channel_id=1, source_target_pairs={{0,1},{1,0},{2,3},{3,2},{4,5},{5,4},{6,7},{7,6},{8,9},{9,8},{10,11... | collective-permute-start | bytes 196616 | tf_op jit(solution)/shard_map/ppermute | solution.py:109
  71.7 6.8 %collective-permute-start.41 = (bf16[256,128]{1,0:T(8,128)(2,1)S(1)}, bf16[256,128]{1,0:T(8,128)(2,1)S(1)}, u32[]{:S(2)}, u32[]{:S(2)}) collective-permute-start(bf16[256,128]{1,0:T(8,128)(2,1)S(1)} %collective-permute-done.37.refs_2_), channel_id=1, source_target_pairs={{0,1},{1,0},{2,3},{3,2},{4,5},{5,4},{6,7},{7,6},{8,9},{9,8},{10,11... | collective-permute-start | bytes 196616 | tf_op jit(solution)/shard_map/ppermute | solution.py:109
  71.7 6.7 %collective-permute-start.51 = (f32[128,128]{1,0:T(8,128)S(1)}, f32[128,128]{1,0:T(8,128)S(1)}, u32[]{:S(2)}, u32[]{:S(2)}) collective-permute-start(f32[128,128]{1,0:T(8,128)S(1)} %add.38), channel_id=1, source_target_pairs={{0,16},{1,17},{2,18},{3,19},{4,20},{5,21},{6,22},{7,23},{8,24},{9,... | collective-permute-start | bytes 196616 | tf_op jit(solution)/shard_map/ppermute | solution.py:160
  74.0 15.5 %collective-permute-start.34 = (bf16[768,128]{1,0:T(8,128)(2,1)S(1)}, bf16[768,128]{1,0:T(8,128)(2,1)S(1)}, u32[]{:S(2)}, u32[]{:S(2)}) collective-permute-start(bf16[768,128]{1,0:T(8,128)(2,1)S(1)} %constant_dynamic-update-slice_fusion.7.refs_4_), channel_id=1, source_target_pairs={{0,2},{1,3},{2,0},{3,1},{4,6},{5,7},{6,4},{7,5},{8,10},{9,11},{10,... | collective-permute-start | bytes 589832 | tf_op jit(solution)/shard_map/ppermute | solution.py:109
  74.7 14.8 %collective-permute-start.30 = (bf16[768,128]{1,0:T(8,128)(2,1)S(1)}, bf16[768,128]{1,0:T(8,128)(2,1)S(1)}, u32[]{:S(2)}, u32[]{:S(2)}) collective-permute-start(bf16[768,128]{1,0:T(8,128)(2,1)S(1)} %constant_dynamic-update-slice_fusion.7.refs_4_), channel_id=1, source_target_pairs={{0,4},{1,5},{2,6},{3,7},{4,0},{5,1},{6,2},{7,3},{8,12},{9,13},{10,... | collective-permute-start | bytes 589832 | tf_op jit(solution)/shard_map/ppermute | solution.py:109
  76.0 14.1 %collective-permute-start.31 = (bf16[768,128]{1,0:T(8,128)(2,1)S(1)}, bf16[768,128]{1,0:T(8,128)(2,1)S(1)}, u32[]{:S(2)}, u32[]{:S(2)}) collective-permute-start(bf16[768,128]{1,0:T(8,128)(2,1)S(1)} %constant_dynamic-update-slice_fusion.7.refs_4_), channel_id=1, source_target_pairs={{0,6},{1,7},{2,4},{3,5},{4,2},{5,3},{6,0},{7,1},{8,14},{9,15},{10,... | collective-permute-start | bytes 589832 | tf_op jit(solution)/shard_map/ppermute | solution.py:109
  78.4 11.8 %collective-permute-start.43 = (bf16[768,128]{1,0:T(8,128)(2,1)S(1)}, bf16[768,128]{1,0:T(8,128)(2,1)S(1)}, u32[]{:S(2)}, u32[]{:S(2)}) collective-permute-start(bf16[768,128]{1,0:T(8,128)(2,1)S(1)} %constant_dynamic-update-slice_fusion.7.refs_4_), channel_id=1, source_target_pairs={{0,1},{1,0},{2,3},{3,2},{4,5},{5,4},{6,7},{7,6},{8,9},{9,8},{10,11... | collective-permute-start | bytes 589832 | tf_op jit(solution)/shard_map/ppermute | solution.py:109
  78.4 8.3 %collective-permute-start.52 = (f32[128,128]{1,0:T(8,128)S(1)}, f32[128,128]{1,0:T(8,128)S(1)}, u32[]{:S(2)}, u32[]{:S(2)}) collective-permute-start(f32[128,128]{1,0:T(8,128)S(1)} %add.39), channel_id=1, source_target_pairs={{0,2},{1,3},{2,0},{3,1},{4,6},{5,7},{6,4},{7,5},{8,10},{9,11},{10,... | collective-permute-start | bytes 196616 | tf_op jit(solution)/shard_map/ppermute | solution.py:160
  88.1 8.4 %collective-permute-start.53 = (f32[128,128]{1,0:T(8,128)S(1)}, f32[128,128]{1,0:T(8,128)S(1)}, u32[]{:S(2)}, u32[]{:S(2)}) collective-permute-start(f32[128,128]{1,0:T(8,128)S(1)} %add.40), channel_id=1, source_target_pairs={{0,4},{1,5},{2,6},{3,7},{4,0},{5,1},{6,2},{7,3},{8,12},{9,13},{10,... | collective-permute-start | bytes 196616 | tf_op jit(solution)/shard_map/ppermute | solution.py:160
  89.5 3.3 %collective-permute-start.32 = (bf16[768,128]{1,0:T(8,128)(2,1)S(1)}, bf16[768,128]{1,0:T(8,128)(2,1)S(1)}, u32[]{:S(2)}, u32[]{:S(2)}) collective-permute-start(bf16[768,128]{1,0:T(8,128)(2,1)S(1)} %collective-permute-done.30.refs_0_), channel_id=1, source_target_pairs={{0,1},{1,0},{2,3},{3,2},{4,5},{5,4},{6,7},{7,6},{8,9},{9,8},{10,11... | collective-permute-start | bytes 589832 | tf_op jit(solution)/shard_map/ppermute | solution.py:109
  90.0 2.8 %collective-permute-start.33 = (bf16[768,128]{1,0:T(8,128)(2,1)S(1)}, bf16[768,128]{1,0:T(8,128)(2,1)S(1)}, u32[]{:S(2)}, u32[]{:S(2)}) collective-permute-start(bf16[768,128]{1,0:T(8,128)(2,1)S(1)} %collective-permute-done.31.refs_1_), channel_id=1, source_target_pairs={{0,1},{1,0},{2,3},{3,2},{4,5},{5,4},{6,7},{7,6},{8,9},{9,8},{10,11... | collective-permute-start | bytes 589832 | tf_op jit(solution)/shard_map/ppermute | solution.py:109
  97.3 3.9 %collective-permute-start.45 = (f32[64,64]{1,0:T(8,128)S(1)}, f32[64,64]{1,0:T(8,128)S(1)}, u32[]{:S(2)}, u32[]{:S(2)}) collective-permute-start(f32[64,64]{1,0:T(8,128)S(1)} %add.33), channel_id=1, source_target_pairs={{0,2},{1,3},{2,0},{3,1},{4,6},{5,7},{6,4},{7,5},{8,10},{9,11},{10,... | collective-permute-start | bytes 49160 | tf_op jit(solution)/shard_map/ppermute | solution.py:160
  101.2 3.9 %collective-permute-start.46 = (f32[64,64]{1,0:T(8,128)S(1)}, f32[64,64]{1,0:T(8,128)S(1)}, u32[]{:S(2)}, u32[]{:S(2)}) collective-permute-start(f32[64,64]{1,0:T(8,128)S(1)} %add.34), channel_id=1, source_target_pairs={{0,8},{1,9},{2,10},{3,11},{4,12},{5,13},{6,14},{7,15},{8,0},{9,1},... | collective-permute-start | bytes 49160 | tf_op jit(solution)/shard_map/ppermute | solution.py:160
  105.1 5.2 %collective-permute-start.47 = (f32[64,64]{1,0:T(8,128)S(1)}, f32[64,64]{1,0:T(8,128)S(1)}, u32[]{:S(2)}, u32[]{:S(2)}) collective-permute-start(f32[64,64]{1,0:T(8,128)S(1)} %add.35), channel_id=1, source_target_pairs={{0,16},{1,17},{2,18},{3,19},{4,20},{5,21},{6,22},{7,23},{8,24},{9,... | collective-permute-start | bytes 49160 | tf_op jit(solution)/shard_map/ppermute | solution.py:160
  110.3 3.9 %collective-permute-start.48 = (f32[64,64]{1,0:T(8,128)S(1)}, f32[64,64]{1,0:T(8,128)S(1)}, u32[]{:S(2)}, u32[]{:S(2)}) collective-permute-start(f32[64,64]{1,0:T(8,128)S(1)} %add.36.gram), channel_id=1, source_target_pairs={{0,4},{1,5},{2,6},{3,7},{4,0},{5,1},{6,2},{7,3},{8,12},{9,13},{10,... | collective-permute-start | bytes 49160 | tf_op jit(solution)/shard_map/ppermute | solution.py:160
  (14 other events, 62.3 us)
